TPU v7x, 256 devices: a whole 4x4x8 slice. The times are simulated.
256 devices in a mesh: dp: 32 (over x, z), vocab: 8 (over y, core).
Axes of the slice: x: 4, y: 4, z: 8, core: 2. Of those that a mesh axis runs over, the one named last changes fastest.
Arguments:
- hidden: bfloat16 [256, 14, 4096], P('dp', None, 'vocab'), may hold values from -400 to 400
- weight: bfloat16 [4096, 128256], P(None, ('dp', 'vocab')), may hold values from -0.09375 to 0.09375
- targets: int32 [256, 14], P('dp'), may hold values from 0 to 128255
- lengths: int32 [32, 8], P('dp'), may hold values from 1 to 14, 56 in all within a row
- rewards: int32 [32, 8], P('dp'), may hold values from -256 to 256
- arrival: int32 [256], replicated, may hold values from 0 to 255, each once
Outputs:
- token_logprobs: float32 [256, 14], P('dp')
- advantages: float32 [256], P('dp')
- weighted: float32 [256], P('dp')
Inputs may be any that keep to these rules, and one draw needn't show every extreme that they name: The lengths of one device's 8 completions sum to exactly 56, and one of them is 14. `arrival`: every completion number appears once; completion p * 8 + j is sample j of prompt p.
All inputs are finite; a program needn't handle non-finite values.
Results may differ from a plain program's by a relative error of at most 0.0003.
Values may be sent and summed in bfloat16 or wider, within the bound.
No kernel may reach another device: no remote copies, remote signals or barrier semaphores. Data moves between devices by JAX's collectives and lax.ppermute only.
A program may use at most 192 MiB of HBM per device.

v0:
```python
import jax
import jax.numpy as jnp
from jax import lax
from jax.experimental import pallas as pl
from jax.experimental.pallas import tpu as pltpu
from jax.sharding import Mesh
from jax.sharding import PartitionSpec as P


SAMPLES = 8
DP = ("x", "z")
VOCAB = ("y", "c")
REWARD_UNIT = 1.0 / 64.0
NX, NZ, NY, NC = 4, 8, 4, 2
SLOTS, WINDOW, WIDTH = 8, 14, 512
HALF = 28
MSG = 32
ROWS = NZ * HALF
META = NZ
SHARD = 501
TALL = ROWS + META
OFFSETS = (0, -1, 1, 2)
F32 = jnp.float32
BF16 = jnp.bfloat16
VMEM = pl.BlockSpec(memory_space=pltpu.VMEM)
SMEM = pl.BlockSpec(memory_space=pltpu.SMEM)
HBM = pl.BlockSpec(memory_space=pltpu.HBM)


def params(mib=32):
    return pltpu.CompilerParams(vmem_limit_bytes=mib * 2**20)


def in_hbm(*arrays):
    return [pltpu.with_memory_space_constraint(a, pltpu.HBM) for a in arrays]


def shift(value, axis, by):
    size = lax.axis_size(axis)
    return lax.ppermute(value, axis, [(i, (i + by) % size) for i in range(size)])


def pack_kernel(hidden_hbm, targets_hbm, lengths_hbm, rewards_hbm, out, hidden, targets, lengths, rewards, sems):
    copies = [
        pltpu.make_async_copy(src, dst, sems.at[k])
        for k, (src, dst) in enumerate(
            (
                (lengths_hbm, lengths),
                (rewards_hbm, rewards),
                (targets_hbm, targets),
                (hidden_hbm, hidden),
            )
        )
    ]
    for copy in copies:
        copy.start()
    for copy in copies:
        copy.wait()
    lane = lax.broadcasted_iota(jnp.int32, (1, 128), 1)
    offsets, both = [], jnp.zeros((1, 128), jnp.int32)
    offset_of = jnp.zeros((MSG, SLOTS), jnp.int32)
    length_of = jnp.zeros((MSG, SLOTS), jnp.int32)
    slot = lax.broadcasted_iota(jnp.int32, (MSG, SLOTS), 1)
    at = jnp.int32(0)
    for g in range(SLOTS):
        offsets.append(at)
        offset_of = jnp.where(slot == g, at, offset_of)
        length_of = jnp.where(slot == g, lengths[0, g], length_of)
        both = jnp.where(lane == g, lengths[0, g], both)
        both = jnp.where(lane == SLOTS + g, rewards[0, g], both)
        at = at + lengths[0, g]
    row_of = lax.broadcasted_iota(jnp.int32, (MSG, SLOTS), 0)
    row = lax.broadcasted_iota(jnp.int32, (MSG, WINDOW), 0)
    step = lax.broadcasted_iota(jnp.int32, (MSG, WINDOW), 1)
    wanted = targets[...]
    digits = [(wanted & 255), (wanted >> 8) & 255, wanted >> 16]
    out_row = lax.broadcasted_iota(jnp.int32, (MSG, WIDTH), 0)
    for half in range(NC):
        rows = jnp.zeros((MSG, WIDTH), F32)
        for t in range(WINDOW):
            here = (row_of + half * HALF == offset_of + t) & (t < length_of) & (row_of < HALF)
            chooser = jnp.where(here, 1.0, 0.0).astype(BF16)
            rows += jnp.dot(chooser, hidden[t], preferred_element_type=F32)
        ids = jnp.zeros((8, MSG), F32)
        for g in range(SLOTS):
            here = (row + half * HALF == offsets[g] + step) & (step < lengths[0, g]) & (row < HALF)
            chooser = jnp.where(here, 1.0, 0.0).astype(BF16)
            three = jnp.concatenate(
                [d[g : g + 1, :] for d in digits] + [jnp.zeros((5, WINDOW), jnp.int32)], axis=0
            )
            ids += lax.dot_general(
                three.astype(F32).astype(BF16),
                chooser,
                (((1,), (1,)), ((), ())),
                preferred_element_type=F32,
            )
        pad = jnp.zeros((1, 128 - MSG), F32)
        meta = jnp.concatenate(
            [ids[0:1], pad, ids[1:2], pad, ids[2:3], pad, both.astype(F32)], axis=1
        )
        message = jnp.where(out_row == HALF, meta, rows).astype(BF16)
        for z in range(NZ):
            out[z * NC + half] = message


def unpack_kernel(got, first, second):
    for core, out in enumerate((first, second)):
        pieces = [got[z * NC + core].astype(F32)[:HALF] for z in range(NZ)]
        if core == 0:
            pieces += [got[z * NC].astype(F32)[HALF : HALF + 1] for z in range(NZ)]
        out[...] = jnp.concatenate(pieces, axis=0).astype(BF16)


def join_kernel(one, two, out):
    out[: one.shape[0]] = one[...]
    out[one.shape[0] :] = two[...]


def join(one, two):
    return pl.pallas_call(
        join_kernel,
        out_shape=jax.ShapeDtypeStruct((one.shape[0] + two.shape[0], one.shape[1]), BF16),
        in_specs=[VMEM, VMEM],
        out_specs=VMEM,
        compiler_params=params(),
    )(one, two)


def gathered_planes(own, firsts, lasts):
    both = range(2)
    up = [shift(own[k], firsts[k], 1) for k in both]
    down = [shift(own[k], firsts[k], -1) for k in both]
    far = [shift(up[k], firsts[k], 1) for k in both]
    one = [join(own[k], up[k]) for k in both]
    two = [join(down[k], far[k]) for k in both]
    planes = []
    for k in both:
        up1 = shift(one[k], lasts[k], 1)
        down1 = shift(one[k], lasts[k], -1)
        down2 = shift(two[k], lasts[k], -1)
        up2 = shift(two[k], lasts[k], 1)
        far2 = shift(down2, lasts[k], -1)
        far1 = shift(up1, lasts[k], 1)
        planes.append(((one[k], two[k]), (up1, up2), (down1, down2), (far1, far2)))
    return planes


def product(w, block):
    return lax.dot_general(w[...], block, (((1,), (1,)), ((), ())), preferred_element_type=F32)


def matmul_kernel(which, last):
    def kernel(at, *refs):
        y = at[0]
        n = 2 * len(which)
        a, b, weights, rest = refs[:n], refs[n : 2 * n], refs[2 * n : 2 * n + 2], refs[2 * n + 2 :]
        if last:
            before, ids, out, acc, held, held_w, sems = rest
        else:
            acc, held_w, sems = rest
        wanted = [(j, 0) for j in which] + [(j, 1) for j in range(NY)]
        copies = {}
        for k, (j, core) in enumerate(wanted):
            column = pl.multiple_of(((y + OFFSETS[j] + NY) % NY * NC + core) * WIDTH, WIDTH)
            copies[j, core] = [
                pltpu.make_async_copy(
                    weights[w].at[:, pl.ds(column, WIDTH)], held_w.at[k, w], sems.at[k, w]
                )
                for w in range(2)
            ]
            for copy in copies[j, core]:
                copy.start()
        ready = set()
        for i in [i for i in range(NX) if i not in which] + list(which):
            terms = []
            for p, j in enumerate(which):
                lo = i % 2 * TALL
                terms.append(((j, 0), a[2 * p + i // 2][lo : lo + ROWS, :]))
            if i in which:
                p = which.index(i)
                for j in range(NY):
                    lo = j % 2 * ROWS
                    terms.append(((j, 1), b[2 * p + j // 2][lo : lo + ROWS, :]))
            for key, _ in terms:
                if key not in ready:
                    ready.add(key)
                    for copy in copies[key]:
                        copy.wait()
            for w in range(2):
                total = before[i, w] if last else None
                for key, block in terms:
                    term = product(held_w.at[wanted.index(key), w], block)
                    total = term if total is None else total + term
                acc[i, w] = total
        if last:
            statistics(at, ids, acc, out, held)

    return kernel


def statistics(at, ids, acc, out, held):
    x = at[1]
    held[...] = jnp.zeros_like(held)
    column = lax.broadcasted_iota(jnp.int32, (SHARD, ROWS), 0)
    for i in range(NX):
        own, other = acc[i, 0], acc[i, 1]
        top = jnp.maximum(jnp.max(own, 0, keepdims=True), jnp.max(other, 0, keepdims=True))
        total = jnp.sum(jnp.exp(own - top), 0, keepdims=True) + jnp.sum(
            jnp.exp(other - top), 0, keepdims=True
        )
        wanted = ids[i : i + 1, :ROWS]
        hit = jnp.sum(jnp.where(column == wanted - at[2], own, 0.0), 0, keepdims=True)
        hit += jnp.sum(jnp.where(column == wanted - at[3], other, 0.0), 0, keepdims=True)
        x_at = (x + OFFSETS[i] + NX) % NX
        held[pl.ds(x_at, 1), :ROWS] = top + jnp.log(total)
        held[pl.ds(4 + x_at, 1), :ROWS] = hit
    for k in range(out.shape[0]):
        out[k] = held[...]


def head(at, plane0, plane1, weights, ids):
    acc_shape = (NX, 2, SHARD, ROWS)

    def call(which, *more):
        parts = [piece for j in which for piece in plane0[j]]
        parts += [piece for j in which for piece in plane1[j]]
        last = bool(more)
        slices = len(which) + NY
        scratch = [pltpu.VMEM(acc_shape, F32), pltpu.VMEM((8, 256), F32)] if last else []
        scratch += [
            pltpu.VMEM((slices, 2, SHARD, WIDTH), BF16),
            pltpu.SemaphoreType.DMA((slices, 2)),
        ]
        shape = (NX * NY, 8, 256) if last else acc_shape
        return pl.pallas_call(
            matmul_kernel(which, last),
            out_shape=jax.ShapeDtypeStruct(shape, F32),
            in_specs=[SMEM] + [VMEM] * len(parts) + [HBM] * 2 + [VMEM] * len(more),
            out_specs=VMEM,
            scratch_shapes=scratch,
            compiler_params=params(26),
        )(at, *parts, *weights, *more)

    acc = call((0, 1, 2))
    return call((3,), acc, ids)


def merged_parts(parts):
    top, hit = parts[0][:4], parts[0][4:]
    for part in parts[1:]:
        top = jnp.maximum(top, part[:4])
        hit = hit + part[4:]
    total = jnp.zeros_like(top)
    for part in parts:
        total = total + jnp.exp(part[:4] - top)
    return top + jnp.log(total), hit


def merge_kernel(parts, out):
    lse, hit = merged_parts([parts[k] for k in range(parts.shape[0])])
    for k in range(out.shape[0]):
        out[k, :4] = lse
        out[k, 4:] = hit


def final_kernel(parts, source, advantage, length, logprobs, weighted):
    tables = []
    for core in range(NC):
        lse, hit = merged_parts([parts[z * NC + core] for z in range(NZ)])
        tables.append(hit - lse)
    lane = lax.broadcasted_iota(jnp.int32, (SLOTS, 256), 1)
    wanted = source[...]
    total = jnp.zeros((SLOTS, 1), F32)
    columns = []
    for t in range(WINDOW):
        at = wanted[:, t : t + 1]
        found = jnp.zeros((SLOTS, 256), F32)
        for core in range(NC):
            for x in range(NX):
                here = at - (core * NX + x) * 256 == lane
                found = jnp.where(here, tables[core][x : x + 1, :], found)
        value = jnp.sum(found, axis=1, keepdims=True)
        columns.append(value)
        total = total + value
    logprobs[...] = jnp.concatenate(columns, axis=1)
    row = lax.broadcasted_iota(jnp.int32, (SLOTS, SLOTS), 0)
    across = lax.broadcasted_iota(jnp.int32, (SLOTS, SLOTS), 1)
    line = jnp.sum(jnp.where(row == across, total, 0.0), axis=0, keepdims=True)
    weighted[...] = advantage[...] * line / length[...]


def local(hidden, weight, targets, lengths, rewards, arrival):
    shard = weight.shape[1]
    x, z, y, c = (lax.axis_index(a) for a in ("x", "z", "y", "c"))
    swapped = shift(weight, "c", 1)
    sent = pl.pallas_call(
        pack_kernel,
        out_shape=jax.ShapeDtypeStruct((NZ * NC, MSG, WIDTH), BF16),
        in_specs=[HBM] * 4,
        out_specs=VMEM,
        scratch_shapes=[
            pltpu.VMEM((WINDOW, SLOTS, WIDTH), BF16),
            pltpu.VMEM((SLOTS, WINDOW), jnp.int32),
            pltpu.SMEM((1, SLOTS), jnp.int32),
            pltpu.SMEM((1, SLOTS), jnp.int32),
            pltpu.SemaphoreType.DMA((4,)),
        ],
        compiler_params=params(),
    )(*in_hbm(hidden.transpose(1, 0, 2), targets, lengths, rewards))
    got = lax.all_to_all(sent, ("z", "c"), 0, 0, tiled=True)
    own0, own1 = pl.pallas_call(
        unpack_kernel,
        out_shape=[
            jax.ShapeDtypeStruct((TALL, WIDTH), BF16),
            jax.ShapeDtypeStruct((ROWS, WIDTH), BF16),
        ],
        in_specs=[VMEM],
        out_specs=[VMEM, VMEM],
        compiler_params=params(),
    )(got)
    plane0, plane1 = gathered_planes((own0, own1), ("x", "y"), ("y", "x"))
    line0 = plane0[0]

    metas = jnp.stack([line0[i // 2][i % 2 * TALL + ROWS : i % 2 * TALL + TALL] for i in range(NX)])
    whole = metas.astype(F32).astype(jnp.int32)
    ids = whole[:, :, :HALF] + 256 * whole[:, :, 128 : 128 + HALF] + 65536 * whole[:, :, 256 : 256 + HALF]
    ids = jnp.pad(ids.reshape(NX, ROWS), ((0, 4), (0, 0)), constant_values=-1)

    dp = x * NZ + z
    base = (dp * NY + y) * NC
    at = jnp.stack([y, x, (base + c) * shard, (base + 1 - c) * shard]).astype(jnp.int32)
    partial = head(at, plane0, plane1, in_hbm(weight.T, swapped.T), ids)

    order = (lax.iota(jnp.int32, NX) - x + NX) % NX
    relative = jnp.where(order == 0, 0, jnp.where(order == 3, 1, order + 1))
    per_slot = jnp.sum(
        jnp.where(
            (relative[:, None] == lax.iota(jnp.int32, NX)[None, :])[:, :, None, None],
            whole[None, :, :, 384 : 384 + 2 * SLOTS],
            0,
        ),
        axis=1,
    ).reshape(NX * NZ, 2 * SLOTS)
    all_lengths, all_rewards = per_slot[:, :SLOTS], per_slot[:, SLOTS:]
    count = NX * NZ * SLOTS
    slot_ids = lax.iota(jnp.int32, count)
    mine = lax.iota(jnp.int32, SLOTS) + dp * SLOTS
    matching = arrival[None, :] == mine[:, None]

    def lookup(table):
        return jnp.sum(jnp.where(matching, table.reshape(count)[None, :], 0), axis=1)

    slot_of = lookup(slot_ids)
    length_of = lookup(all_lengths)
    reward_of = lookup(all_rewards).astype(F32) * REWARD_UNIT
    offset_of = lookup(jnp.cumsum(all_lengths, axis=1) - all_lengths)
    group = slot_of // SLOTS
    line = offset_of[:, None] + lax.iota(jnp.int32, WINDOW)[None, :]
    usable = lax.iota(jnp.int32, WINDOW)[None, :] < length_of[:, None]
    place = group // NZ * 256 + group % NZ * HALF
    source = jnp.where(usable, place[:, None] + line // HALF * 1024 + line % HALF, -1)
    groups = jnp.sum(reward_of.reshape(SLOTS // SAMPLES, SAMPLES), axis=1)
    advantages = reward_of - (jnp.repeat(groups, SAMPLES) - reward_of) / (SAMPLES - 1.0)

    stats = lax.all_to_all(partial, ("x", "y"), 0, 0, tiled=True)
    stats = pl.pallas_call(
        merge_kernel,
        out_shape=jax.ShapeDtypeStruct((NZ * NC, 8, 256), F32),
        in_specs=[VMEM],
        out_specs=VMEM,
        compiler_params=params(),
    )(stats)
    stats = lax.all_to_all(stats, ("z", "c"), 0, 0, tiled=True)
    token_logprobs, weighted = pl.pallas_call(
        final_kernel,
        out_shape=[
            jax.ShapeDtypeStruct((SLOTS, WINDOW), F32),
            jax.ShapeDtypeStruct((1, SLOTS), F32),
        ],
        in_specs=[VMEM] * 4,
        out_specs=[VMEM, VMEM],
        compiler_params=params(),
    )(stats, source, advantages[None, :], length_of.astype(F32)[None, :])
    return token_logprobs, advantages, weighted.reshape(SLOTS)


def solution(mesh):
    finer = Mesh(mesh.devices.reshape(NX, NZ, NY, NC), ("x", "z", "y", "c"))
    every = ("x", "z", "y", "c")
    placed = (P(DP, None, VOCAB), P(None, every), P(DP, None), P(DP, None), P(DP, None), P())

    return jax.shard_map(
        local, mesh=finer, in_specs=placed, out_specs=(P(DP, None), P(DP), P(DP)), check_vma=False
    )
```

profile of v0, /device:TPU:1, one launch (start us, length us, event | category | flops | bytes accessed | tf_op | source)
XLA Modules:
  0.0 127.0 jit_solution(14281071508655676969)
XLA Ops:
  0.6 3.3 %collective-permute-start.14 = (bf16[4096,501]{0,1:T(8,128)(2,1)}, bf16[4096,501]{0,1:T(8,128)(2,1)}, u32[]{:S(2)}, u32[]{:S(2)}) collective-permute-start(bf16[4096,501]{0,1:T(8,128)(2,1)} %param.7), channel_id=1, source_target_pairs={{0,1},{1,0},{2,3},{3,2},{4,5},{5,4},{6,7},{7,6},{8,9},{9,8},{10,11... | collective-permute-start | bytes 12312584 | tf_op jit(solution)/shard_map/ppermute | solution.py:40
  3.9 1.4 %shard_map.85 = bf16[16,32,512]{2,1,0:T(8,128)(2,1)S(1)} custom-call(bf16[14,8,512]{2,1,0:T(8,128)(2,1)} %bitcast.32, s32[8,14]{1,0:T(8,128)} %targets_hbm.1, s32[1,8]{1,0:T(1,128)} %lengths_hbm.1, s32[1,8]{1,0:T(1,128)} %rewards_hbm.1), custom_call_target="tpu_custom_call" | custom-call | tf_op jit(solution)/shard_map/pallas_call | solution.py:296
  5.4 23.9 %all_to_all.15.got = bf16[16,32,512]{2,1,0:T(8,128)(2,1)S(1)} all-to-all(bf16[16,32,512]{2,1,0:T(8,128)(2,1)S(1)} %shard_map.85), channel_id=1, replica_groups=mesh['x'=4,'z'=8,'y'=4,'c'=2] {'z','c'}, dimensions={0} | all-to-all | bytes 1048576 | tf_op jit(solution)/shard_map/all_to_all | solution.py:310
  29.3 1.3 %collective-permute-start = (bf16[232,512]{1,0:T(8,128)(2,1)S(1)}, bf16[232,512]{1,0:T(8,128)(2,1)S(1)}, u32[]{:S(2)}, u32[]{:S(2)}) collective-permute-start(bf16[232,512]{1,0:T(8,128)(2,1)S(1)} %get-tuple-element.7.one), channel_id=1, source_target_pairs={{0,64},{64,128},{128,192},{192,0},{1,65},{65,129},{129,193},{193,1... | collective-permute-start | bytes 712712 | tf_op jit(solution)/shard_map/ppermute | solution.py:40
  30.6 1.3 %collective-permute-start.7 = (bf16[224,512]{1,0:T(8,128)(2,1)S(1)}, bf16[224,512]{1,0:T(8,128)(2,1)S(1)}, u32[]{:S(2)}, u32[]{:S(2)}) collective-permute-start(bf16[224,512]{1,0:T(8,128)(2,1)S(1)} %get-tuple-element.8.one), channel_id=1, source_target_pairs={{0,2},{2,4},{4,6},{6,0},{1,3},{3,5},{5,7},{7,1},{8,10},{10,12},{12... | collective-permute-start | bytes 688136 | tf_op jit(solution)/shard_map/ppermute | solution.py:40
  31.9 1.5 %collective-permute-start.3 = (bf16[232,512]{1,0:T(8,128)(2,1)S(1)}, bf16[232,512]{1,0:T(8,128)(2,1)S(1)}, u32[]{:S(2)}, u32[]{:S(2)}) collective-permute-start(bf16[232,512]{1,0:T(8,128)(2,1)S(1)} %get-tuple-element.7.one), channel_id=1, source_target_pairs={{0,192},{64,0},{128,64},{192,128},{1,193},{65,1},{129,65},{193,129... | collective-permute-start | bytes 712712 | tf_op jit(solution)/shard_map/ppermute | solution.py:40
  33.5 1.4 %collective-permute-start.10 = (bf16[224,512]{1,0:T(8,128)(2,1)S(1)}, bf16[224,512]{1,0:T(8,128)(2,1)S(1)}, u32[]{:S(2)}, u32[]{:S(2)}) collective-permute-start(bf16[224,512]{1,0:T(8,128)(2,1)S(1)} %get-tuple-element.8.one), channel_id=1, source_target_pairs={{0,6},{2,0},{4,2},{6,4},{1,7},{3,1},{5,3},{7,5},{8,14},{10,8},{12,... | collective-permute-start | bytes 688136 | tf_op jit(solution)/shard_map/ppermute | solution.py:40
  34.9 3.8 %collective-permute-done.7.two = bf16[224,512]{1,0:T(8,128)(2,1)S(1)} collective-permute-done((bf16[224,512]{1,0:T(8,128)(2,1)S(1)}, bf16[224,512]{1,0:T(8,128)(2,1)S(1)}, u32[]{:S(2)}, u32[]{:S(2)}) %collective-permute-start.7) | collective-permute-done | bytes 229408 | tf_op jit(solution)/shard_map/ppermute | solution.py:40
  38.7 0.4 collective-permute-start.11
  39.1 1.2 collective-permute-start.4
  40.3 0.1 pad_add_fusion.at
  40.5 0.4 collective-permute-done.10.one
  41.0 0.6 collective-permute-start.8
  41.6 2.1 %collective-permute-start.18 = (bf16[448,512]{1,0:T(8,128)(2,1)S(1)}, bf16[448,512]{1,0:T(8,128)(2,1)}, u32[]{:S(2)}, u32[]{:S(2)}) collective-permute-start(bf16[448,512]{1,0:T(8,128)(2,1)S(1)} %shard_map.89.refs_6_), channel_id=1, source_target_pairs={{0,192},{64,0},{128,64},{192,128},{1,193},{65,1},{129,65},{193,129... | collective-permute-start | bytes 1376264 | tf_op jit(solution)/shard_map/ppermute | solution.py:40
  43.6 3.3 %collective-permute-done.11.two = bf16[224,512]{1,0:T(8,128)(2,1)S(1)} collective-permute-done((bf16[224,512]{1,0:T(8,128)(2,1)S(1)}, bf16[224,512]{1,0:T(8,128)(2,1)S(1)}, u32[]{:S(2)}, u32[]{:S(2)}) %collective-permute-start.11) | collective-permute-done | bytes 229408 | tf_op jit(solution)/shard_map/ppermute | solution.py:40
  46.9 0.5 collective-permute-done.4.two
  47.4 2.2 %collective-permute-start.16 = (bf16[464,512]{1,0:T(8,128)(2,1)S(1)}, bf16[464,512]{1,0:T(8,128)(2,1)S(1)}, u32[]{:S(2)}, u32[]{:S(2)}) collective-permute-start(bf16[464,512]{1,0:T(8,128)(2,1)S(1)} %shard_map.87.refs_0_), channel_id=1, source_target_pairs={{0,6},{2,0},{4,2},{6,4},{1,7},{3,1},{5,3},{7,5},{8,14},{10,8},{12,... | collective-permute-start | bytes 1425416 | tf_op jit(solution)/shard_map/ppermute | solution.py:40
  49.7 0.1 select_reduce_fusion
  49.8 0.1 broadcast_in_dim.82
  49.9 0.2 reduce_window_sum.11
  50.0 7.2 %collective-permute-done.8.refs_8_ = bf16[448,512]{1,0:T(8,128)(2,1)S(1)} collective-permute-done((bf16[448,512]{1,0:T(8,128)(2,1)S(1)}, bf16[448,512]{1,0:T(8,128)(2,1)S(1)}, u32[]{:S(2)}, u32[]{:S(2)}) %collective-permute-start.8) | collective-permute-done | bytes 458784 | tf_op jit(solution)/shard_map/ppermute | solution.py:40
  57.2 0.3 collective-permute-start.12
  57.5 1.2 collective-permute-start.17
  58.7 0.8 collective-permute-done.1.refs_2_
  59.5 1.3 %collective-permute-start.5 = (bf16[464,512]{1,0:T(8,128)(2,1)S(1)}, bf16[464,512]{1,0:T(8,128)(2,1)S(1)}, u32[]{:S(2)}, u32[]{:S(2)}) collective-permute-start(bf16[464,512]{1,0:T(8,128)(2,1)S(1)} %shard_map.88.refs_1_), channel_id=1, source_target_pairs={{0,6},{2,0},{4,2},{6,4},{1,7},{3,1},{5,3},{7,5},{8,14},{10,8},{12,... | collective-permute-start | bytes 1425416 | tf_op jit(solution)/shard_map/ppermute | solution.py:40
  60.8 0.2 collective-permute-start.15
  61.0 0.1 broadcast_in_dim.86
  61.1 0.1 broadcast_in_dim.88
  61.2 0.2 fusion.5
  61.4 6.9 %collective-permute-done.12.refs_11_ = bf16[448,512]{1,0:T(8,128)(2,1)} collective-permute-done((bf16[448,512]{1,0:T(8,128)(2,1)S(1)}, bf16[448,512]{1,0:T(8,128)(2,1)}, u32[]{:S(2)}, u32[]{:S(2)}) %collective-permute-start.12) | collective-permute-done | bytes 458784 | tf_op jit(solution)/shard_map/ppermute | solution.py:40
  68.3 1.2 collective-permute-done.17.refs_9_
  69.5 1.3 %collective-permute-start.2 = (bf16[464,512]{1,0:T(8,128)(2,1)S(1)}, bf16[464,512]{1,0:T(8,128)(2,1)}, u32[]{:S(2)}, u32[]{:S(2)}) collective-permute-start(bf16[464,512]{1,0:T(8,128)(2,1)S(1)} %collective-permute-done.1.refs_2_), channel_id=1, source_target_pairs={{0,2},{2,4},{4,6},{6,0},{1,3},{3,5},{5,7},{7,1},{8,10},{10,12},{12... | collective-permute-start | bytes 1425416 | tf_op jit(solution)/shard_map/ppermute | solution.py:40
  70.8 2.2 %collective-permute-start.13 = (bf16[448,512]{1,0:T(8,128)(2,1)}, bf16[448,512]{1,0:T(8,128)(2,1)}, u32[]{:S(2)}, u32[]{:S(2)}) collective-permute-start(bf16[448,512]{1,0:T(8,128)(2,1)} %collective-permute-done.12.refs_11_), channel_id=1, source_target_pairs={{0,192},{64,0},{128,64},{192,128},{1,193},{65,1},{129,65},{193,129... | collective-permute-start | bytes 1376264 | tf_op jit(solution)/shard_map/ppermute | solution.py:40
  73.0 1.9 %collective-permute-start.6 = (bf16[464,512]{1,0:T(8,128)(2,1)S(1)}, bf16[464,512]{1,0:T(8,128)(2,1)}, u32[]{:S(2)}, u32[]{:S(2)}) collective-permute-start(bf16[464,512]{1,0:T(8,128)(2,1)S(1)} %collective-permute-done.5.refs_5_), channel_id=1, source_target_pairs={{0,6},{2,0},{4,2},{6,4},{1,7},{3,1},{5,3},{7,5},{8,14},{10,8},{12,... | collective-permute-start | bytes 1425416 | tf_op jit(solution)/shard_map/ppermute | solution.py:40
  75.0 0.6 fusion.19
  75.6 0.1 reshape.153
  75.7 1.2 multiply_subtract_fusion
  76.8 0.7 bitcast_subtract_fusion.advantage
  77.5 1.0 copy-done.1
  78.5 10.5 %shard_map.91.refs_6_ = f32[4,2,501,224]{3,2,1,0:T(8,128)S(1)} custom-call(s32[4]{0:T(128)S(1)} %pad_add_fusion.at, bf16[464,512]{1,0:T(8,128)(2,1)S(1)} %shard_map.87.refs_0_, bf16[464,512]{1,0:T(8,128)(2,1)S(1)} %shard_map.88.refs_1_, bf16[464,512]{1,0:T(8,128)(2,1)S(1)} %collective-permute-done.1.refs_2_, ...), custom_call_target="tpu_custom_call" | custom-call | tf_op jit(solution)/shard_map/pallas_call | solution.py:235
  89.1 7.7 %shard_map.92 = f32[16,8,256]{2,1,0:T(8,128)} custom-call(s32[4]{0:T(128)S(1)} %pad_add_fusion.at, bf16[464,512]{1,0:T(8,128)(2,1)} %collective-permute-done.2.refs_0_, bf16[464,512]{1,0:T(8,128)(2,1)} %collective-permute-done.6.refs_1_, bf16[448,512]{1,0:T(8,128)(2,1)} %collective-permute-done.9.refs_2_, bf16[448,512]{1,0:T(8,128)(2,1)} %collective-permute-done.13.refs_3_, ...), custom_call_target="tpu_custom_call" | custom-call | tf_op jit(solution)/shard_map/pallas_call | solution.py:235
  96.8 3.5 %all-to-all-start.1 = ((f32[16,8,256]{2,1,0:T(8,128)}), f32[16,8,256]{2,1,0:T(8,128)S(1)}, u32[]{:S(2)}, u32[]{:S(2)}) async-start(f32[16,8,256]{2,1,0:T(8,128)} %shard_map.92), calls=%async_computation.1 | async-start | bytes 262144 | tf_op jit(solution)/shard_map/all_to_all | solution.py:365
  100.3 6.6 %all-to-all-done.1.parts = f32[16,8,256]{2,1,0:T(8,128)S(1)} async-done(((f32[16,8,256]{2,1,0:T(8,128)}), f32[16,8,256]{2,1,0:T(8,128)S(1)}, u32[]{:S(2)}, u32[]{:S(2)}) %all-to-all-start.1) | async-done | bytes 131104 | tf_op jit(solution)/shard_map/all_to_all | solution.py:365
  106.9 0.7 shard_map.93
  107.6 8.7 %all-to-all-start.2 = ((f32[16,8,256]{2,1,0:T(8,128)}), f32[16,8,256]{2,1,0:T(8,128)S(1)}, u32[]{:S(2)}, u32[]{:S(2)}) async-start(f32[16,8,256]{2,1,0:T(8,128)} %shard_map.93), calls=%async_computation.2 | async-start | bytes 262144 | tf_op jit(solution)/shard_map/all_to_all | solution.py:373
  116.4 0.1 fusion.9.source
  116.4 9.1 %all-to-all-done.2.parts = f32[16,8,256]{2,1,0:T(8,128)S(1)} async-done(((f32[16,8,256]{2,1,0:T(8,128)}), f32[16,8,256]{2,1,0:T(8,128)S(1)}, u32[]{:S(2)}, u32[]{:S(2)}) %all-to-all-start.2) | async-done | bytes 131104 | tf_op jit(solution)/shard_map/all_to_all | solution.py:373
  125.5 1.4 %shard_map.94 = (f32[8,14]{1,0:T(8,128)}, f32[1,8]{1,0:T(1,128)}) custom-call(f32[16,8,256]{2,1,0:T(8,128)S(1)} %all-to-all-done.2.parts, s32[8,14]{1,0:T(8,128)S(1)} %fusion.9.source, f32[1,8]{1,0:T(1,128)S(1)} %bitcast_subtract_fusion.advantage, f32[1,8]{1,0:T(1,128)S(1)} %convert_bitcast_fusion.length), custom_call_target="tpu_custom_call" | custom-call | tf_op jit(solution)/shard_map/pallas_call | solution.py:374
  (35 shorter events, 0.5 us)
Async XLA Ops:
  0.6 60.6 %copy-start.2 = (s32[256]{0:T(256)S(1)}, s32[256]{0:T(256)}, u32[]{:S(2)}) copy-start(s32[256]{0:T(256)} %param.11) | copy-start | bytes 3076
  0.6 76.9 %collective-permute-start.14 = (bf16[4096,501]{0,1:T(8,128)(2,1)}, bf16[4096,501]{0,1:T(8,128)(2,1)}, u32[]{:S(2)}, u32[]{:S(2)}) collective-permute-start(bf16[4096,501]{0,1:T(8,128)(2,1)} %param.7), channel_id=1, source_target_pairs={{0,1},{1,0},{2,3},{3,2},{4,5},{5,4},{6,7},{7,6},{8,9},{9,8},{10,11... | collective-permute-start | bytes 12312584 | tf_op jit(solution)/shard_map/ppermute | solution.py:40
  29.3 9.8 %collective-permute-start = (bf16[232,512]{1,0:T(8,128)(2,1)S(1)}, bf16[232,512]{1,0:T(8,128)(2,1)S(1)}, u32[]{:S(2)}, u32[]{:S(2)}) collective-permute-start(bf16[232,512]{1,0:T(8,128)(2,1)S(1)} %get-tuple-element.7.one), channel_id=1, source_target_pairs={{0,64},{64,128},{128,192},{192,0},{1,65},{65,129},{129,193},{193,1... | collective-permute-start | bytes 712712 | tf_op jit(solution)/shard_map/ppermute | solution.py:40
  30.6 8.1 %collective-permute-start.7 = (bf16[224,512]{1,0:T(8,128)(2,1)S(1)}, bf16[224,512]{1,0:T(8,128)(2,1)S(1)}, u32[]{:S(2)}, u32[]{:S(2)}) collective-permute-start(bf16[224,512]{1,0:T(8,128)(2,1)S(1)} %get-tuple-element.8.one), channel_id=1, source_target_pairs={{0,2},{2,4},{4,6},{6,0},{1,3},{3,5},{5,7},{7,1},{8,10},{10,12},{12... | collective-permute-start | bytes 688136 | tf_op jit(solution)/shard_map/ppermute | solution.py:40
  31.9 9.6 %collective-permute-start.3 = (bf16[232,512]{1,0:T(8,128)(2,1)S(1)}, bf16[232,512]{1,0:T(8,128)(2,1)S(1)}, u32[]{:S(2)}, u32[]{:S(2)}) collective-permute-start(bf16[232,512]{1,0:T(8,128)(2,1)S(1)} %get-tuple-element.7.one), channel_id=1, source_target_pairs={{0,192},{64,0},{128,64},{192,128},{1,193},{65,1},{129,65},{193,129... | collective-permute-start | bytes 712712 | tf_op jit(solution)/shard_map/ppermute | solution.py:40
  33.5 7.5 %collective-permute-start.10 = (bf16[224,512]{1,0:T(8,128)(2,1)S(1)}, bf16[224,512]{1,0:T(8,128)(2,1)S(1)}, u32[]{:S(2)}, u32[]{:S(2)}) collective-permute-start(bf16[224,512]{1,0:T(8,128)(2,1)S(1)} %get-tuple-element.8.one), channel_id=1, source_target_pairs={{0,6},{2,0},{4,2},{6,4},{1,7},{3,1},{5,3},{7,5},{8,14},{10,8},{12,... | collective-permute-start | bytes 688136 | tf_op jit(solution)/shard_map/ppermute | solution.py:40
  38.7 8.2 %collective-permute-start.11 = (bf16[224,512]{1,0:T(8,128)(2,1)S(1)}, bf16[224,512]{1,0:T(8,128)(2,1)S(1)}, u32[]{:S(2)}, u32[]{:S(2)}) collective-permute-start(bf16[224,512]{1,0:T(8,128)(2,1)S(1)} %collective-permute-done.7.two), channel_id=1, source_target_pairs={{0,2},{2,4},{4,6},{6,0},{1,3},{3,5},{5,7},{7,1},{8,10},{10,12},{12... | collective-permute-start | bytes 688136 | tf_op jit(solution)/shard_map/ppermute | solution.py:40
  39.1 8.3 %collective-permute-start.4 = (bf16[232,512]{1,0:T(8,128)(2,1)S(1)}, bf16[232,512]{1,0:T(8,128)(2,1)S(1)}, u32[]{:S(2)}, u32[]{:S(2)}) collective-permute-start(bf16[232,512]{1,0:T(8,128)(2,1)S(1)} %collective-permute-done.two), channel_id=1, source_target_pairs={{0,64},{64,128},{128,192},{192,0},{1,65},{65,129},{129,193},{193,1... | collective-permute-start | bytes 712712 | tf_op jit(solution)/shard_map/ppermute | solution.py:40
  41.0 16.3 %collective-permute-start.8 = (bf16[448,512]{1,0:T(8,128)(2,1)S(1)}, bf16[448,512]{1,0:T(8,128)(2,1)S(1)}, u32[]{:S(2)}, u32[]{:S(2)}) collective-permute-start(bf16[448,512]{1,0:T(8,128)(2,1)S(1)} %shard_map.89.refs_6_), channel_id=1, source_target_pairs={{0,64},{64,128},{128,192},{192,0},{1,65},{65,129},{129,193},{193,1... | collective-permute-start | bytes 1376264 | tf_op jit(solution)/shard_map/ppermute | solution.py:40
  41.6 15.9 %collective-permute-start.18 = (bf16[448,512]{1,0:T(8,128)(2,1)S(1)}, bf16[448,512]{1,0:T(8,128)(2,1)}, u32[]{:S(2)}, u32[]{:S(2)}) collective-permute-start(bf16[448,512]{1,0:T(8,128)(2,1)S(1)} %shard_map.89.refs_6_), channel_id=1, source_target_pairs={{0,192},{64,0},{128,64},{192,128},{1,193},{65,1},{129,65},{193,129... | collective-permute-start | bytes 1376264 | tf_op jit(solution)/shard_map/ppermute | solution.py:40
  46.9 12.6 %collective-permute-start.1 = (bf16[464,512]{1,0:T(8,128)(2,1)S(1)}, bf16[464,512]{1,0:T(8,128)(2,1)S(1)}, u32[]{:S(2)}, u32[]{:S(2)}) collective-permute-start(bf16[464,512]{1,0:T(8,128)(2,1)S(1)} %shard_map.87.refs_0_), channel_id=1, source_target_pairs={{0,2},{2,4},{4,6},{6,0},{1,3},{3,5},{5,7},{7,1},{8,10},{10,12},{12... | collective-permute-start | bytes 1425416 | tf_op jit(solution)/shard_map/ppermute | solution.py:40
  47.4 13.4 %collective-permute-start.16 = (bf16[464,512]{1,0:T(8,128)(2,1)S(1)}, bf16[464,512]{1,0:T(8,128)(2,1)S(1)}, u32[]{:S(2)}, u32[]{:S(2)}) collective-permute-start(bf16[464,512]{1,0:T(8,128)(2,1)S(1)} %shard_map.87.refs_0_), channel_id=1, source_target_pairs={{0,6},{2,0},{4,2},{6,4},{1,7},{3,1},{5,3},{7,5},{8,14},{10,8},{12,... | collective-permute-start | bytes 1425416 | tf_op jit(solution)/shard_map/ppermute | solution.py:40
  57.2 1.5 %copy-start = (bf16[448,512]{1,0:T(8,128)(2,1)}, bf16[448,512]{1,0:T(8,128)(2,1)S(1)}, u32[]{:S(2)}) copy-start(bf16[448,512]{1,0:T(8,128)(2,1)S(1)} %collective-permute-done.8.refs_8_) | copy-start | bytes 1376260
  57.2 11.1 %collective-permute-start.12 = (bf16[448,512]{1,0:T(8,128)(2,1)S(1)}, bf16[448,512]{1,0:T(8,128)(2,1)}, u32[]{:S(2)}, u32[]{:S(2)}) collective-permute-start(bf16[448,512]{1,0:T(8,128)(2,1)S(1)} %shard_map.90.refs_7_), channel_id=1, source_target_pairs={{0,192},{64,0},{128,64},{192,128},{1,193},{65,1},{129,65},{193,129... | collective-permute-start | bytes 1376264 | tf_op jit(solution)/shard_map/ppermute | solution.py:40
  57.5 12.0 %collective-permute-start.17 = (bf16[448,512]{1,0:T(8,128)(2,1)S(1)}, bf16[448,512]{1,0:T(8,128)(2,1)}, u32[]{:S(2)}, u32[]{:S(2)}) collective-permute-start(bf16[448,512]{1,0:T(8,128)(2,1)S(1)} %shard_map.90.refs_7_), channel_id=1, source_target_pairs={{0,64},{64,128},{128,192},{192,0},{1,65},{65,129},{129,193},{193,1... | collective-permute-start | bytes 1376264 | tf_op jit(solution)/shard_map/ppermute | solution.py:40
  59.5 11.3 %collective-permute-start.5 = (bf16[464,512]{1,0:T(8,128)(2,1)S(1)}, bf16[464,512]{1,0:T(8,128)(2,1)S(1)}, u32[]{:S(2)}, u32[]{:S(2)}) collective-permute-start(bf16[464,512]{1,0:T(8,128)(2,1)S(1)} %shard_map.88.refs_1_), channel_id=1, source_target_pairs={{0,6},{2,0},{4,2},{6,4},{1,7},{3,1},{5,3},{7,5},{8,14},{10,8},{12,... | collective-permute-start | bytes 1425416 | tf_op jit(solution)/shard_map/ppermute | solution.py:40
  60.8 12.3 %collective-permute-start.15 = (bf16[464,512]{1,0:T(8,128)(2,1)S(1)}, bf16[464,512]{1,0:T(8,128)(2,1)}, u32[]{:S(2)}, u32[]{:S(2)}) collective-permute-start(bf16[464,512]{1,0:T(8,128)(2,1)S(1)} %shard_map.88.refs_1_), channel_id=1, source_target_pairs={{0,2},{2,4},{4,6},{6,0},{1,3},{3,5},{5,7},{7,1},{8,10},{10,12},{12... | collective-permute-start | bytes 1425416 | tf_op jit(solution)/shard_map/ppermute | solution.py:40
  68.3 20.7 %collective-permute-start.9 = (bf16[448,512]{1,0:T(8,128)(2,1)}, bf16[448,512]{1,0:T(8,128)(2,1)}, u32[]{:S(2)}, u32[]{:S(2)}) collective-permute-start(bf16[448,512]{1,0:T(8,128)(2,1)} %copy-done), channel_id=1, source_target_pairs={{0,64},{64,128},{128,192},{192,0},{1,65},{65,129},{129,193},{193,1... | collective-permute-start | bytes 1376264 | tf_op jit(solution)/shard_map/ppermute | solution.py:40
  69.5 19.6 %collective-permute-start.2 = (bf16[464,512]{1,0:T(8,128)(2,1)S(1)}, bf16[464,512]{1,0:T(8,128)(2,1)}, u32[]{:S(2)}, u32[]{:S(2)}) collective-permute-start(bf16[464,512]{1,0:T(8,128)(2,1)S(1)} %collective-permute-done.1.refs_2_), channel_id=1, source_target_pairs={{0,2},{2,4},{4,6},{6,0},{1,3},{3,5},{5,7},{7,1},{8,10},{10,12},{12... | collective-permute-start | bytes 1425416 | tf_op jit(solution)/shard_map/ppermute | solution.py:40
  70.8 18.3 %collective-permute-start.13 = (bf16[448,512]{1,0:T(8,128)(2,1)}, bf16[448,512]{1,0:T(8,128)(2,1)}, u32[]{:S(2)}, u32[]{:S(2)}) collective-permute-start(bf16[448,512]{1,0:T(8,128)(2,1)} %collective-permute-done.12.refs_11_), channel_id=1, source_target_pairs={{0,192},{64,0},{128,64},{192,128},{1,193},{65,1},{129,65},{193,129... | collective-permute-start | bytes 1376264 | tf_op jit(solution)/shard_map/ppermute | solution.py:40
  73.0 16.1 %collective-permute-start.6 = (bf16[464,512]{1,0:T(8,128)(2,1)S(1)}, bf16[464,512]{1,0:T(8,128)(2,1)}, u32[]{:S(2)}, u32[]{:S(2)}) collective-permute-start(bf16[464,512]{1,0:T(8,128)(2,1)S(1)} %collective-permute-done.5.refs_5_), channel_id=1, source_target_pairs={{0,6},{2,0},{4,2},{6,4},{1,7},{3,1},{5,3},{7,5},{8,14},{10,8},{12,... | collective-permute-start | bytes 1425416 | tf_op jit(solution)/shard_map/ppermute | solution.py:40
  77.5 1.0 copy-start.1
  96.8 10.2 %all-to-all-start.1 = ((f32[16,8,256]{2,1,0:T(8,128)}), f32[16,8,256]{2,1,0:T(8,128)S(1)}, u32[]{:S(2)}, u32[]{:S(2)}) async-start(f32[16,8,256]{2,1,0:T(8,128)} %shard_map.92), calls=%async_computation.1 | async-start | bytes 262144 | tf_op jit(solution)/shard_map/all_to_all | solution.py:365
  107.6 17.9 %all-to-all-start.2 = ((f32[16,8,256]{2,1,0:T(8,128)}), f32[16,8,256]{2,1,0:T(8,128)S(1)}, u32[]{:S(2)}, u32[]{:S(2)}) async-start(f32[16,8,256]{2,1,0:T(8,128)} %shard_map.93), calls=%async_computation.2 | async-start | bytes 262144 | tf_op jit(solution)/shard_map/all_to_all | solution.py:373
where the time goes:
time: 127 us
  waiting for transfers between devices  39.7 us (31%)
  starting transfers between devices  35.9 us (28%)
  blocking collectives  23.9 us (19%)
  Pallas kernels  21.9 us (17%)
  other arithmetic  3.24 us (3%)
  local copies, waits for them, and re-layouts  1.38 us (1%)
    ppermute x19, waiting for transfers between devices, shift(): lax.ppermute(value, axis, [(i, (i + by) % size) for i in range(size)])  24 us
    all_to_all x1, blocking collectives, local(): got = lax.all_to_all(sent, ('z', 'c'), 0, 0, tiled=True)  23.9 us
    ppermute x19, starting transfers between devices, shift(): lax.ppermute(value, axis, [(i, (i + by) % size) for i in range(size)])  23.7 us
    pallas_call x2, Pallas kernels, call(): pl.pallas_call(matmul_kernel(which, last), out_shape=jax.ShapeDtypeStruct...  18.2 us
    all_to_all x1, waiting for transfers between devices, local(): stats = lax.all_to_all(stats, ('z', 'c'), 0, 0, tiled=True)  9.09 us
    all_to_all x1, starting transfers between devices, local(): stats = lax.all_to_all(stats, ('z', 'c'), 0, 0, tiled=True)  8.71 us
    all_to_all x1, waiting for transfers between devices, local(): stats = lax.all_to_all(partial, ('x', 'y'), 0, 0, tiled=True)  6.61 us
    all_to_all x1, starting transfers between devices, local(): stats = lax.all_to_all(partial, ('x', 'y'), 0, 0, tiled=True)  3.52 us
  transfers between devices with their start and end apart: 21, of which 10 were waited for; matrix products, arithmetic and copies ran while one was open for 3% of the time, Pallas kernels for 10%

commit v1 on v0

--- a/solution.py
+++ b/solution.py
@@ -149,51 +149,86 @@
     return lax.dot_general(w[...], block, (((1,), (1,)), ((), ())), preferred_element_type=F32)
 
 
-def matmul_kernel(which, last):
+def matmul_kernel(which, on_chip, first, last):
+    names = [(k, j, part) for k in range(2) for j in which for part in range(2)]
+
     def kernel(at, *refs):
         y = at[0]
-        n = 2 * len(which)
-        a, b, weights, rest = refs[:n], refs[n : 2 * n], refs[2 * n : 2 * n + 2], refs[2 * n + 2 :]
+        pieces = dict(zip(names, refs))
+        refs = refs[len(names) :]
+        weights, refs = refs[:2], refs[2:]
+        before = None
+        if not first:
+            before, refs = refs[0], refs[1:]
         if last:
-            before, ids, out, acc, held, held_w, sems = rest
+            ids, out, acc, held, held_p, held_w, sems, sems_w, sems_a = refs
         else:
-            acc, held_w, sems = rest
-        wanted = [(j, 0) for j in which] + [(j, 1) for j in range(NY)]
-        copies = {}
-        for k, (j, core) in enumerate(wanted):
-            column = pl.multiple_of(((y + OFFSETS[j] + NY) % NY * NC + core) * WIDTH, WIDTH)
-            copies[j, core] = [
-                pltpu.make_async_copy(
-                    weights[w].at[:, pl.ds(column, WIDTH)], held_w.at[k, w], sems.at[k, w]
-                )
-                for w in range(2)
-            ]
-            for copy in copies[j, core]:
-                copy.start()
-        ready = set()
+            out, acc, held_p, held_w, sems, sems_w, sems_a = refs
+
+        plan = []
         for i in [i for i in range(NX) if i not in which] + list(which):
             terms = []
-            for p, j in enumerate(which):
-                lo = i % 2 * TALL
-                terms.append(((j, 0), a[2 * p + i // 2][lo : lo + ROWS, :]))
+            for j in which:
+                terms.append(((j, 0), (0, j, i // 2), i % 2 * TALL))
             if i in which:
-                p = which.index(i)
-                for j in range(NY):
-                    lo = j % 2 * ROWS
-                    terms.append(((j, 1), b[2 * p + j // 2][lo : lo + ROWS, :]))
-            for key, _ in terms:
-                if key not in ready:
-                    ready.add(key)
-                    for copy in copies[key]:
-                        copy.wait()
+                terms += [((j, 1), (1, i, j // 2), j % 2 * ROWS) for j in range(NY)]
+            plan.append((i, terms))
+
+        slices, moved, waits, views = {}, {}, {}, {}
+        for i, terms in plan:
+            if not first:
+                waits[i] = [pltpu.make_async_copy(before.at[i], acc.at[i], sems_a.at[i])]
+                waits[i][0].start()
+            for key, name, _ in terms:
+                if key not in slices:
+                    n = slices[key] = len(slices)
+                    j, colour = key
+                    row = (y + OFFSETS[j] + NY) % NY * NC
+                    column = pl.multiple_of((row + colour) * WIDTH, WIDTH)
+                    waits[key] = [
+                        pltpu.make_async_copy(
+                            weights[w].at[:, pl.ds(column, WIDTH)], held_w.at[n, w], sems_w.at[n, w]
+                        )
+                        for w in range(2)
+                    ]
+                    for copy in waits[key]:
+                        copy.start()
+                if name not in views:
+                    ref = pieces[name]
+                    if on_chip(name):
+                        views[name] = ref
+                    else:
+                        n = moved[name] = len(moved)
+                        views[name] = held_p.at[n]
+                        copy = pltpu.make_async_copy(
+                            ref, held_p.at[n, pl.ds(0, ref.shape[0])], sems.at[n]
+                        )
+                        copy.start()
+                        waits[name] = [copy]
+
+        def ready(key):
+            for copy in waits.pop(key, ()):
+                copy.wait()
+
+        leaving = []
+        for i, terms in plan:
+            ready(i)
+            for key, name, _ in terms:
+                ready(key)
+                ready(name)
             for w in range(2):
-                total = before[i, w] if last else None
-                for key, block in terms:
-                    term = product(held_w.at[wanted.index(key), w], block)
+                total = None if first else acc[i, w]
+                for key, name, lo in terms:
+                    term = product(held_w.at[slices[key], w], views[name][lo : lo + ROWS, :])
                     total = term if total is None else total + term
                 acc[i, w] = total
+            if not last:
+                leaving.append(pltpu.make_async_copy(acc.at[i], out.at[i], sems_a.at[i]))
+                leaving[-1].start()
         if last:
             statistics(at, ids, acc, out, held)
+        for copy in leaving:
+            copy.wait()
 
     return kernel
 
@@ -218,31 +253,42 @@
         out[k] = held[...]
 
 
-def head(at, plane0, plane1, weights, ids):
+def head(at, planes, weights, ids):
     acc_shape = (NX, 2, SHARD, ROWS)
 
-    def call(which, *more):
-        parts = [piece for j in which for piece in plane0[j]]
-        parts += [piece for j in which for piece in plane1[j]]
-        last = bool(more)
+    def call(which, on_chip, first, last, *more):
+        names = [(k, j, part) for k in range(2) for j in which for part in range(2)]
+        parts, specs = [], []
+        for name in names:
+            piece = planes[name[0]][name[1]][name[2]]
+            parts += [piece] if on_chip(name) else in_hbm(piece)
+            specs.append(VMEM if on_chip(name) else HBM)
         slices = len(which) + NY
-        scratch = [pltpu.VMEM(acc_shape, F32), pltpu.VMEM((8, 256), F32)] if last else []
+        late = max(1, sum(not on_chip(name) for name in names))
+        scratch = [pltpu.VMEM(acc_shape, F32)] + ([pltpu.VMEM((8, 256), F32)] if last else [])
         scratch += [
+            pltpu.VMEM((late, 2 * TALL, WIDTH), BF16),
             pltpu.VMEM((slices, 2, SHARD, WIDTH), BF16),
+            pltpu.SemaphoreType.DMA((late,)),
             pltpu.SemaphoreType.DMA((slices, 2)),
+            pltpu.SemaphoreType.DMA((NX,)),
         ]
         shape = (NX * NY, 8, 256) if last else acc_shape
+        specs = [SMEM] + specs + [HBM] * 2
+        specs += [] if first else [HBM]
+        specs += [VMEM] if last else []
         return pl.pallas_call(
-            matmul_kernel(which, last),
-            out_shape=jax.ShapeDtypeStruct(shape, F32),
-            in_specs=[SMEM] + [VMEM] * len(parts) + [HBM] * 2 + [VMEM] * len(more),
-            out_specs=VMEM,
+            matmul_kernel(which, on_chip, first, last),
+            out_shape=pltpu.VMEM(shape, F32) if last else pltpu.HBM(shape, F32),
+            in_specs=specs,
+            out_specs=VMEM if last else HBM,
             scratch_shapes=scratch,
-            compiler_params=params(26),
+            compiler_params=params(24),
         )(at, *parts, *weights, *more)
 
-    acc = call((0, 1, 2))
-    return call((3,), acc, ids)
+    (acc,) = in_hbm(call((0,), lambda name: True, True, False))
+    (acc,) = in_hbm(call((1, 2), lambda name: name[1] - 1 == name[2], False, False, acc))
+    return call((3,), lambda name: False, False, True, acc, ids)
 
 
 def merged_parts(parts):
@@ -295,7 +341,7 @@
     swapped = shift(weight, "c", 1)
     sent = pl.pallas_call(
         pack_kernel,
-        out_shape=jax.ShapeDtypeStruct((NZ * NC, MSG, WIDTH), BF16),
+        out_shape=pltpu.VMEM((NZ * NC, MSG, WIDTH), BF16),
         in_specs=[HBM] * 4,
         out_specs=VMEM,
         scratch_shapes=[
@@ -318,8 +364,8 @@
         out_specs=[VMEM, VMEM],
         compiler_params=params(),
     )(got)
-    plane0, plane1 = gathered_planes((own0, own1), ("x", "y"), ("y", "x"))
-    line0 = plane0[0]
+    planes = gathered_planes((own0, own1), ("x", "y"), ("y", "x"))
+    line0 = planes[0][0]
 
     metas = jnp.stack([line0[i // 2][i % 2 * TALL + ROWS : i % 2 * TALL + TALL] for i in range(NX)])
     whole = metas.astype(F32).astype(jnp.int32)
@@ -329,7 +375,7 @@
     dp = x * NZ + z
     base = (dp * NY + y) * NC
     at = jnp.stack([y, x, (base + c) * shard, (base + 1 - c) * shard]).astype(jnp.int32)
-    partial = head(at, plane0, plane1, in_hbm(weight.T, swapped.T), ids)
+    partial = head(at, planes, in_hbm(weight.T, swapped.T), ids)
 
     order = (lax.iota(jnp.int32, NX) - x + NX) % NX
     relative = jnp.where(order == 0, 0, jnp.where(order == 3, 1, order + 1))
@@ -365,7 +411,7 @@
     stats = lax.all_to_all(partial, ("x", "y"), 0, 0, tiled=True)
     stats = pl.pallas_call(
         merge_kernel,
-        out_shape=jax.ShapeDtypeStruct((NZ * NC, 8, 256), F32),
+        out_shape=pltpu.VMEM((NZ * NC, 8, 256), F32),
         in_specs=[VMEM],
         out_specs=VMEM,
         compiler_params=params(),

time: 127 us -> 132 us (1.039)
  Pallas kernels: 21.9 us -> 27.9 us
  starting transfers between devices: 35.9 us -> 33.9 us
    pallas_call x4 -> x5, Pallas kernels: 20.3 us -> 26.3 us  [the longest x3 24.2 us: call(): pl.pallas_call(matmul_kernel(which, on_chip, first, last), out_shape=pltp...]
    all_to_all x1, starting transfers between devices: 8.71 us -> 6.54 us  [local(): stats = lax.all_to_all(stats, ('z', 'c'), 0, 0, tiled=True)]
  transfers between devices with their start and end apart: 21 -> 21, of which waited for: 10 -> 10; matrix products, arithmetic and copies ran while one was open for 3% -> 3% of each run, Pallas kernels for 10% -> 13%
where the time goes in v1:
time: 132 us; the launch traced here: 131 us
  waiting for transfers between devices  39.4 us (30%)
  starting transfers between devices  33.9 us (26%)
  Pallas kernels  27.9 us (21%)
  blocking collectives  23.9 us (18%)
  other arithmetic  3.24 us (2%)
  local copies, waits for them, and re-layouts  1.98 us (2%)
    pallas_call x3, Pallas kernels, call(): pl.pallas_call(matmul_kernel(which, on_chip, first, last), out_shape=pltp...  24.2 us
    all_to_all x1, blocking collectives, local(): got = lax.all_to_all(sent, ('z', 'c'), 0, 0, tiled=True)  23.9 us
    ppermute x19, starting transfers between devices, shift(): lax.ppermute(value, axis, [(i, (i + by) % size) for i in range(size)])  23.8 us
    ppermute x19, waiting for transfers between devices, shift(): lax.ppermute(value, axis, [(i, (i + by) % size) for i in range(size)])  23.6 us
    all_to_all x1, waiting for transfers between devices, local(): stats = lax.all_to_all(stats, ('z', 'c'), 0, 0, tiled=True)  9.09 us
    all_to_all x1, waiting for transfers between devices, local(): stats = lax.all_to_all(partial, ('x', 'y'), 0, 0, tiled=True)  6.67 us
    all_to_all x1, starting transfers between devices, local(): stats = lax.all_to_all(stats, ('z', 'c'), 0, 0, tiled=True)  6.54 us
    all_to_all x1, starting transfers between devices, local(): stats = lax.all_to_all(partial, ('x', 'y'), 0, 0, tiled=True)  3.52 us
  transfers between devices with their start and end apart: 21, of which 10 were waited for; matrix products, arithmetic and copies ran while one was open for 3% of the time, Pallas kernels for 13%

profile of v1, /device:TPU:1, one launch (start us, length us, event | category | flops | bytes accessed | tf_op | source)
XLA Modules:
  0.0 131.1 jit_solution(1011668765931464994)
XLA Ops:
  0.6 3.3 %collective-permute-start.14 = (bf16[4096,501]{0,1:T(8,128)(2,1)}, bf16[4096,501]{0,1:T(8,128)(2,1)}, u32[]{:S(2)}, u32[]{:S(2)}) collective-permute-start(bf16[4096,501]{0,1:T(8,128)(2,1)} %param.7), channel_id=1, source_target_pairs={{0,1},{1,0},{2,3},{3,2},{4,5},{5,4},{6,7},{7,6},{8,9},{9,8},{10,11... | collective-permute-start | bytes 12312584 | tf_op jit(solution)/shard_map/ppermute | solution.py:40
  3.9 1.4 %shard_map.85 = bf16[16,32,512]{2,1,0:T(8,128)(2,1)S(1)} custom-call(bf16[14,8,512]{2,1,0:T(8,128)(2,1)} %bitcast.33, s32[8,14]{1,0:T(8,128)} %targets_hbm.1, s32[1,8]{1,0:T(1,128)} %lengths_hbm.1, s32[1,8]{1,0:T(1,128)} %rewards_hbm.1), custom_call_target="tpu_custom_call" | custom-call | tf_op jit(solution)/shard_map/pallas_call | solution.py:342
  5.4 23.9 %all_to_all.15.got = bf16[16,32,512]{2,1,0:T(8,128)(2,1)S(1)} all-to-all(bf16[16,32,512]{2,1,0:T(8,128)(2,1)S(1)} %shard_map.85), channel_id=1, replica_groups=mesh['x'=4,'z'=8,'y'=4,'c'=2] {'z','c'}, dimensions={0} | all-to-all | bytes 1048576 | tf_op jit(solution)/shard_map/all_to_all | solution.py:356
  29.3 1.4 %collective-permute-start.7 = (bf16[224,512]{1,0:T(8,128)(2,1)S(1)}, bf16[224,512]{1,0:T(8,128)(2,1)S(1)}, u32[]{:S(2)}, u32[]{:S(2)}) collective-permute-start(bf16[224,512]{1,0:T(8,128)(2,1)S(1)} %get-tuple-element.8.one), channel_id=1, source_target_pairs={{0,2},{2,4},{4,6},{6,0},{1,3},{3,5},{5,7},{7,1},{8,10},{10,12},{12... | collective-permute-start | bytes 688136 | tf_op jit(solution)/shard_map/ppermute | solution.py:40
  30.7 1.3 collective-permute-start
  32.0 1.5 %collective-permute-start.3 = (bf16[232,512]{1,0:T(8,128)(2,1)S(1)}, bf16[232,512]{1,0:T(8,128)(2,1)S(1)}, u32[]{:S(2)}, u32[]{:S(2)}) collective-permute-start(bf16[232,512]{1,0:T(8,128)(2,1)S(1)} %get-tuple-element.7.one), channel_id=1, source_target_pairs={{0,192},{64,0},{128,64},{192,128},{1,193},{65,1},{129,65},{193,129... | collective-permute-start | bytes 712712 | tf_op jit(solution)/shard_map/ppermute | solution.py:40
  33.5 1.5 %collective-permute-start.10 = (bf16[224,512]{1,0:T(8,128)(2,1)S(1)}, bf16[224,512]{1,0:T(8,128)(2,1)S(1)}, u32[]{:S(2)}, u32[]{:S(2)}) collective-permute-start(bf16[224,512]{1,0:T(8,128)(2,1)S(1)} %get-tuple-element.8.one), channel_id=1, source_target_pairs={{0,6},{2,0},{4,2},{6,4},{1,7},{3,1},{5,3},{7,5},{8,14},{10,8},{12,... | collective-permute-start | bytes 688136 | tf_op jit(solution)/shard_map/ppermute | solution.py:40
  34.9 2.6 %collective-permute-done.7.two = bf16[224,512]{1,0:T(8,128)(2,1)S(1)} collective-permute-done((bf16[224,512]{1,0:T(8,128)(2,1)S(1)}, bf16[224,512]{1,0:T(8,128)(2,1)S(1)}, u32[]{:S(2)}, u32[]{:S(2)}) %collective-permute-start.7) | collective-permute-done | bytes 229408 | tf_op jit(solution)/shard_map/ppermute | solution.py:40
  37.5 0.1 collective-permute-start.11
  37.7 1.4 %collective-permute-done.two = bf16[232,512]{1,0:T(8,128)(2,1)S(1)} collective-permute-done((bf16[232,512]{1,0:T(8,128)(2,1)S(1)}, bf16[232,512]{1,0:T(8,128)(2,1)S(1)}, u32[]{:S(2)}, u32[]{:S(2)}) %collective-permute-start) | collective-permute-done | bytes 237600 | tf_op jit(solution)/shard_map/ppermute | solution.py:40
  39.1 0.3 collective-permute-start.4
  39.5 1.4 %collective-permute-done.10.one = bf16[224,512]{1,0:T(8,128)(2,1)S(1)} collective-permute-done((bf16[224,512]{1,0:T(8,128)(2,1)S(1)}, bf16[224,512]{1,0:T(8,128)(2,1)S(1)}, u32[]{:S(2)}, u32[]{:S(2)}) %collective-permute-start.10) | collective-permute-done | bytes 229408 | tf_op jit(solution)/shard_map/ppermute | solution.py:40
  41.0 2.7 %collective-permute-start.18 = (bf16[448,512]{1,0:T(8,128)(2,1)S(1)}, bf16[448,512]{1,0:T(8,128)(2,1)}, u32[]{:S(2)}, u32[]{:S(2)}) collective-permute-start(bf16[448,512]{1,0:T(8,128)(2,1)S(1)} %shard_map.89.refs_2_), channel_id=1, source_target_pairs={{0,192},{64,0},{128,64},{192,128},{1,193},{65,1},{129,65},{193,129... | collective-permute-start | bytes 1376264 | tf_op jit(solution)/shard_map/ppermute | solution.py:40
  43.6 2.6 %collective-permute-done.11.two = bf16[224,512]{1,0:T(8,128)(2,1)S(1)} collective-permute-done((bf16[224,512]{1,0:T(8,128)(2,1)S(1)}, bf16[224,512]{1,0:T(8,128)(2,1)S(1)}, u32[]{:S(2)}, u32[]{:S(2)}) %collective-permute-start.11) | collective-permute-done | bytes 229408 | tf_op jit(solution)/shard_map/ppermute | solution.py:40
  46.3 0.7 copy-done
  47.0 0.9 copy-done.1
  48.0 2.8 %collective-permute-start.16 = (bf16[464,512]{1,0:T(8,128)(2,1)S(1)}, bf16[464,512]{1,0:T(8,128)(2,1)}, u32[]{:S(2)}, u32[]{:S(2)}) collective-permute-start(bf16[464,512]{1,0:T(8,128)(2,1)S(1)} %shard_map.87.refs_0_), channel_id=1, source_target_pairs={{0,6},{2,0},{4,2},{6,4},{1,7},{3,1},{5,3},{7,5},{8,14},{10,8},{12,... | collective-permute-start | bytes 1425416 | tf_op jit(solution)/shard_map/ppermute | solution.py:40
  50.8 0.1 select_reduce_fusion
  50.9 0.1 broadcast_in_dim.82
  51.0 0.2 reduce_window_sum.11
  51.1 6.1 %collective-permute-done.8.refs_4_ = bf16[448,512]{1,0:T(8,128)(2,1)S(1)} collective-permute-done((bf16[448,512]{1,0:T(8,128)(2,1)S(1)}, bf16[448,512]{1,0:T(8,128)(2,1)S(1)}, u32[]{:S(2)}, u32[]{:S(2)}) %collective-permute-start.8) | collective-permute-done | bytes 458784 | tf_op jit(solution)/shard_map/ppermute | solution.py:40
  57.2 0.8 collective-permute-start.12
  57.9 0.7 collective-permute-start.17
  58.7 1.5 %collective-permute-done.1.refs_0_ = bf16[464,512]{1,0:T(8,128)(2,1)S(1)} collective-permute-done((bf16[464,512]{1,0:T(8,128)(2,1)S(1)}, bf16[464,512]{1,0:T(8,128)(2,1)S(1)}, u32[]{:S(2)}, u32[]{:S(2)}) %collective-permute-start.1) | collective-permute-done | bytes 475168 | tf_op jit(solution)/shard_map/ppermute | solution.py:40
  60.1 0.7 collective-permute-start.5
  60.9 0.1 broadcast_in_dim.86
  61.0 0.1 broadcast_in_dim.88
  61.1 0.2 fusion.5
  61.3 1.0 collective-permute-start.15
  62.3 5.9 %collective-permute-done.12.refs_7_ = bf16[448,512]{1,0:T(8,128)(2,1)} collective-permute-done((bf16[448,512]{1,0:T(8,128)(2,1)S(1)}, bf16[448,512]{1,0:T(8,128)(2,1)}, u32[]{:S(2)}, u32[]{:S(2)}) %collective-permute-start.12) | collective-permute-done | bytes 458784 | tf_op jit(solution)/shard_map/ppermute | solution.py:40
  68.3 2.1 %collective-permute-done.17.refs_5_ = bf16[448,512]{1,0:T(8,128)(2,1)} collective-permute-done((bf16[448,512]{1,0:T(8,128)(2,1)S(1)}, bf16[448,512]{1,0:T(8,128)(2,1)}, u32[]{:S(2)}, u32[]{:S(2)}) %collective-permute-start.17) | collective-permute-done | bytes 458784 | tf_op jit(solution)/shard_map/ppermute | solution.py:40
  70.3 1.3 collective-permute-start.2
  71.6 2.2 %collective-permute-start.13 = (bf16[448,512]{1,0:T(8,128)(2,1)}, bf16[448,512]{1,0:T(8,128)(2,1)}, u32[]{:S(2)}, u32[]{:S(2)}) collective-permute-start(bf16[448,512]{1,0:T(8,128)(2,1)} %collective-permute-done.12.refs_7_), channel_id=1, source_target_pairs={{0,192},{64,0},{128,64},{192,128},{1,193},{65,1},{129,65},{193,129... | collective-permute-start | bytes 1376264 | tf_op jit(solution)/shard_map/ppermute | solution.py:40
  73.8 2.5 %collective-permute-start.6 = (bf16[464,512]{1,0:T(8,128)(2,1)S(1)}, bf16[464,512]{1,0:T(8,128)(2,1)}, u32[]{:S(2)}, u32[]{:S(2)}) collective-permute-start(bf16[464,512]{1,0:T(8,128)(2,1)S(1)} %collective-permute-done.5.refs_3_), channel_id=1, source_target_pairs={{0,6},{2,0},{4,2},{6,4},{1,7},{3,1},{5,3},{7,5},{8,14},{10,8},{12,... | collective-permute-start | bytes 1425416 | tf_op jit(solution)/shard_map/ppermute | solution.py:40
  76.3 0.6 fusion.19
  76.9 0.1 reshape.153
  77.0 1.2 multiply_subtract_fusion
  78.1 0.7 bitcast_subtract_fusion.advantage
  78.8 5.7 %shard_map.91.refs_10_ = f32[4,2,501,224]{3,2,1,0:T(8,128)} custom-call(s32[4]{0:T(128)S(1)} %pad_add_fusion.at, bf16[464,512]{1,0:T(8,128)(2,1)S(1)} %shard_map.87.refs_0_, bf16[464,512]{1,0:T(8,128)(2,1)S(1)} %shard_map.88.refs_1_, bf16[448,512]{1,0:T(8,128)(2,1)S(1)} %shard_map.89.refs_2_, bf16[448,512]{1,0:T(8,128)(2,1)S(1)} %shard_map.90.refs_3_, ...), custom_call_target="tpu_custom_call" | custom-call | tf_op jit(solution)/shard_map/pallas_call | solution.py:280
  84.5 9.9 %shard_map.92.refs_6_ = f32[4,2,501,224]{3,2,1,0:T(8,128)} custom-call(s32[4]{0:T(128)S(1)} %pad_add_fusion.at, bf16[464,512]{1,0:T(8,128)(2,1)S(1)} %collective-permute-done.1.refs_0_, bf16[464,512]{1,0:T(8,128)(2,1)} %collective-permute-done.15.refs_1_, bf16[464,512]{1,0:T(8,128)(2,1)} %collective-permute-done.16.refs_2_, ...), custom_call_target="tpu_custom_call" | custom-call | tf_op jit(solution)/shard_map/pallas_call | solution.py:280
  94.5 8.5 %shard_map.93 = f32[16,8,256]{2,1,0:T(8,128)} custom-call(s32[4]{0:T(128)S(1)} %pad_add_fusion.at, bf16[464,512]{1,0:T(8,128)(2,1)} %collective-permute-done.2.refs_0_, bf16[464,512]{1,0:T(8,128)(2,1)} %collective-permute-done.6.refs_1_, bf16[448,512]{1,0:T(8,128)(2,1)} %collective-permute-done.9.refs_2_, bf16[448,512]{1,0:T(8,128)(2,1)} %collective-permute-done.13.refs_3_, ...), custom_call_target="tpu_custom_call" | custom-call | tf_op jit(solution)/shard_map/pallas_call | solution.py:280
  103.1 3.5 %all-to-all-start.1 = ((f32[16,8,256]{2,1,0:T(8,128)}), f32[16,8,256]{2,1,0:T(8,128)S(1)}, u32[]{:S(2)}, u32[]{:S(2)}) async-start(f32[16,8,256]{2,1,0:T(8,128)} %shard_map.93), calls=%async_computation.1 | async-start | bytes 262144 | tf_op jit(solution)/shard_map/all_to_all | solution.py:411
  106.6 6.7 %all-to-all-done.1.parts = f32[16,8,256]{2,1,0:T(8,128)S(1)} async-done(((f32[16,8,256]{2,1,0:T(8,128)}), f32[16,8,256]{2,1,0:T(8,128)S(1)}, u32[]{:S(2)}, u32[]{:S(2)}) %all-to-all-start.1) | async-done | bytes 131104 | tf_op jit(solution)/shard_map/all_to_all | solution.py:411
  113.3 0.7 shard_map.94
  114.0 6.5 %all-to-all-start.2 = ((f32[16,8,256]{2,1,0:T(8,128)}), f32[16,8,256]{2,1,0:T(8,128)S(1)}, u32[]{:S(2)}, u32[]{:S(2)}) async-start(f32[16,8,256]{2,1,0:T(8,128)} %shard_map.94), calls=%async_computation.2 | async-start | bytes 262144 | tf_op jit(solution)/shard_map/all_to_all | solution.py:419
  120.5 0.1 fusion.9.source
  120.6 9.1 %all-to-all-done.2.parts = f32[16,8,256]{2,1,0:T(8,128)S(1)} async-done(((f32[16,8,256]{2,1,0:T(8,128)}), f32[16,8,256]{2,1,0:T(8,128)S(1)}, u32[]{:S(2)}, u32[]{:S(2)}) %all-to-all-start.2) | async-done | bytes 131104 | tf_op jit(solution)/shard_map/all_to_all | solution.py:419
  129.7 1.4 %shard_map.95 = (f32[8,14]{1,0:T(8,128)}, f32[1,8]{1,0:T(1,128)}) custom-call(f32[16,8,256]{2,1,0:T(8,128)S(1)} %all-to-all-done.2.parts, s32[8,14]{1,0:T(8,128)S(1)} %fusion.9.source, f32[1,8]{1,0:T(1,128)S(1)} %bitcast_subtract_fusion.advantage, f32[1,8]{1,0:T(1,128)S(1)} %convert_bitcast_fusion.length), custom_call_target="tpu_custom_call" | custom-call | tf_op jit(solution)/shard_map/pallas_call | solution.py:420
  (36 shorter events, 0.5 us)
Async XLA Ops:
  0.6 60.4 %copy-start.2 = (s32[256]{0:T(256)S(1)}, s32[256]{0:T(256)}, u32[]{:S(2)}) copy-start(s32[256]{0:T(256)} %param.11) | copy-start | bytes 3076
  0.6 73.2 %collective-permute-start.14 = (bf16[4096,501]{0,1:T(8,128)(2,1)}, bf16[4096,501]{0,1:T(8,128)(2,1)}, u32[]{:S(2)}, u32[]{:S(2)}) collective-permute-start(bf16[4096,501]{0,1:T(8,128)(2,1)} %param.7), channel_id=1, source_target_pairs={{0,1},{1,0},{2,3},{3,2},{4,5},{5,4},{6,7},{7,6},{8,9},{9,8},{10,11... | collective-permute-start | bytes 12312584 | tf_op jit(solution)/shard_map/ppermute | solution.py:40
  29.3 8.2 %collective-permute-start.7 = (bf16[224,512]{1,0:T(8,128)(2,1)S(1)}, bf16[224,512]{1,0:T(8,128)(2,1)S(1)}, u32[]{:S(2)}, u32[]{:S(2)}) collective-permute-start(bf16[224,512]{1,0:T(8,128)(2,1)S(1)} %get-tuple-element.8.one), channel_id=1, source_target_pairs={{0,2},{2,4},{4,6},{6,0},{1,3},{3,5},{5,7},{7,1},{8,10},{10,12},{12... | collective-permute-start | bytes 688136 | tf_op jit(solution)/shard_map/ppermute | solution.py:40
  30.7 8.4 %collective-permute-start = (bf16[232,512]{1,0:T(8,128)(2,1)S(1)}, bf16[232,512]{1,0:T(8,128)(2,1)S(1)}, u32[]{:S(2)}, u32[]{:S(2)}) collective-permute-start(bf16[232,512]{1,0:T(8,128)(2,1)S(1)} %get-tuple-element.7.one), channel_id=1, source_target_pairs={{0,64},{64,128},{128,192},{192,0},{1,65},{65,129},{129,193},{193,1... | collective-permute-start | bytes 712712 | tf_op jit(solution)/shard_map/ppermute | solution.py:40
  32.0 9.0 %collective-permute-start.3 = (bf16[232,512]{1,0:T(8,128)(2,1)S(1)}, bf16[232,512]{1,0:T(8,128)(2,1)S(1)}, u32[]{:S(2)}, u32[]{:S(2)}) collective-permute-start(bf16[232,512]{1,0:T(8,128)(2,1)S(1)} %get-tuple-element.7.one), channel_id=1, source_target_pairs={{0,192},{64,0},{128,64},{192,128},{1,193},{65,1},{129,65},{193,129... | collective-permute-start | bytes 712712 | tf_op jit(solution)/shard_map/ppermute | solution.py:40
  33.5 7.5 %collective-permute-start.10 = (bf16[224,512]{1,0:T(8,128)(2,1)S(1)}, bf16[224,512]{1,0:T(8,128)(2,1)S(1)}, u32[]{:S(2)}, u32[]{:S(2)}) collective-permute-start(bf16[224,512]{1,0:T(8,128)(2,1)S(1)} %get-tuple-element.8.one), channel_id=1, source_target_pairs={{0,6},{2,0},{4,2},{6,4},{1,7},{3,1},{5,3},{7,5},{8,14},{10,8},{12,... | collective-permute-start | bytes 688136 | tf_op jit(solution)/shard_map/ppermute | solution.py:40
  37.5 8.7 %collective-permute-start.11 = (bf16[224,512]{1,0:T(8,128)(2,1)S(1)}, bf16[224,512]{1,0:T(8,128)(2,1)S(1)}, u32[]{:S(2)}, u32[]{:S(2)}) collective-permute-start(bf16[224,512]{1,0:T(8,128)(2,1)S(1)} %collective-permute-done.7.two), channel_id=1, source_target_pairs={{0,2},{2,4},{4,6},{6,0},{1,3},{3,5},{5,7},{7,1},{8,10},{10,12},{12... | collective-permute-start | bytes 688136 | tf_op jit(solution)/shard_map/ppermute | solution.py:40
  39.1 8.9 %collective-permute-start.4 = (bf16[232,512]{1,0:T(8,128)(2,1)S(1)}, bf16[232,512]{1,0:T(8,128)(2,1)S(1)}, u32[]{:S(2)}, u32[]{:S(2)}) collective-permute-start(bf16[232,512]{1,0:T(8,128)(2,1)S(1)} %collective-permute-done.two), channel_id=1, source_target_pairs={{0,64},{64,128},{128,192},{192,0},{1,65},{65,129},{129,193},{193,1... | collective-permute-start | bytes 712712 | tf_op jit(solution)/shard_map/ppermute | solution.py:40
  40.9 16.2 %collective-permute-start.8 = (bf16[448,512]{1,0:T(8,128)(2,1)S(1)}, bf16[448,512]{1,0:T(8,128)(2,1)S(1)}, u32[]{:S(2)}, u32[]{:S(2)}) collective-permute-start(bf16[448,512]{1,0:T(8,128)(2,1)S(1)} %shard_map.89.refs_2_), channel_id=1, source_target_pairs={{0,64},{64,128},{128,192},{192,0},{1,65},{65,129},{129,193},{193,1... | collective-permute-start | bytes 1376264 | tf_op jit(solution)/shard_map/ppermute | solution.py:40
  41.0 17.0 %collective-permute-start.18 = (bf16[448,512]{1,0:T(8,128)(2,1)S(1)}, bf16[448,512]{1,0:T(8,128)(2,1)}, u32[]{:S(2)}, u32[]{:S(2)}) collective-permute-start(bf16[448,512]{1,0:T(8,128)(2,1)S(1)} %shard_map.89.refs_2_), channel_id=1, source_target_pairs={{0,192},{64,0},{128,64},{192,128},{1,193},{65,1},{129,65},{193,129... | collective-permute-start | bytes 1376264 | tf_op jit(solution)/shard_map/ppermute | solution.py:40
  46.3 0.7 copy-start
  47.0 13.2 %collective-permute-start.1 = (bf16[464,512]{1,0:T(8,128)(2,1)S(1)}, bf16[464,512]{1,0:T(8,128)(2,1)S(1)}, u32[]{:S(2)}, u32[]{:S(2)}) collective-permute-start(bf16[464,512]{1,0:T(8,128)(2,1)S(1)} %shard_map.87.refs_0_), channel_id=1, source_target_pairs={{0,2},{2,4},{4,6},{6,0},{1,3},{3,5},{5,7},{7,1},{8,10},{10,12},{12... | collective-permute-start | bytes 1425416 | tf_op jit(solution)/shard_map/ppermute | solution.py:40
  47.0 0.9 copy-start.1
  48.0 13.4 %collective-permute-start.16 = (bf16[464,512]{1,0:T(8,128)(2,1)S(1)}, bf16[464,512]{1,0:T(8,128)(2,1)}, u32[]{:S(2)}, u32[]{:S(2)}) collective-permute-start(bf16[464,512]{1,0:T(8,128)(2,1)S(1)} %shard_map.87.refs_0_), channel_id=1, source_target_pairs={{0,6},{2,0},{4,2},{6,4},{1,7},{3,1},{5,3},{7,5},{8,14},{10,8},{12,... | collective-permute-start | bytes 1425416 | tf_op jit(solution)/shard_map/ppermute | solution.py:40
  57.2 11.1 %collective-permute-start.12 = (bf16[448,512]{1,0:T(8,128)(2,1)S(1)}, bf16[448,512]{1,0:T(8,128)(2,1)}, u32[]{:S(2)}, u32[]{:S(2)}) collective-permute-start(bf16[448,512]{1,0:T(8,128)(2,1)S(1)} %shard_map.90.refs_3_), channel_id=1, source_target_pairs={{0,192},{64,0},{128,64},{192,128},{1,193},{65,1},{129,65},{193,129... | collective-permute-start | bytes 1376264 | tf_op jit(solution)/shard_map/ppermute | solution.py:40
  57.9 12.4 %collective-permute-start.17 = (bf16[448,512]{1,0:T(8,128)(2,1)S(1)}, bf16[448,512]{1,0:T(8,128)(2,1)}, u32[]{:S(2)}, u32[]{:S(2)}) collective-permute-start(bf16[448,512]{1,0:T(8,128)(2,1)S(1)} %shard_map.90.refs_3_), channel_id=1, source_target_pairs={{0,64},{64,128},{128,192},{192,0},{1,65},{65,129},{129,193},{193,1... | collective-permute-start | bytes 1376264 | tf_op jit(solution)/shard_map/ppermute | solution.py:40
  60.1 11.5 %collective-permute-start.5 = (bf16[464,512]{1,0:T(8,128)(2,1)S(1)}, bf16[464,512]{1,0:T(8,128)(2,1)S(1)}, u32[]{:S(2)}, u32[]{:S(2)}) collective-permute-start(bf16[464,512]{1,0:T(8,128)(2,1)S(1)} %shard_map.88.refs_1_), channel_id=1, source_target_pairs={{0,6},{2,0},{4,2},{6,4},{1,7},{3,1},{5,3},{7,5},{8,14},{10,8},{12,... | collective-permute-start | bytes 1425416 | tf_op jit(solution)/shard_map/ppermute | solution.py:40
  61.3 23.2 %collective-permute-start.15 = (bf16[464,512]{1,0:T(8,128)(2,1)S(1)}, bf16[464,512]{1,0:T(8,128)(2,1)}, u32[]{:S(2)}, u32[]{:S(2)}) collective-permute-start(bf16[464,512]{1,0:T(8,128)(2,1)S(1)} %shard_map.88.refs_1_), channel_id=1, source_target_pairs={{0,2},{2,4},{4,6},{6,0},{1,3},{3,5},{5,7},{7,1},{8,10},{10,12},{12... | collective-permute-start | bytes 1425416 | tf_op jit(solution)/shard_map/ppermute | solution.py:40
  68.3 26.2 %collective-permute-start.9 = (bf16[448,512]{1,0:T(8,128)(2,1)S(1)}, bf16[448,512]{1,0:T(8,128)(2,1)}, u32[]{:S(2)}, u32[]{:S(2)}) collective-permute-start(bf16[448,512]{1,0:T(8,128)(2,1)S(1)} %collective-permute-done.8.refs_4_), channel_id=1, source_target_pairs={{0,64},{64,128},{128,192},{192,0},{1,65},{65,129},{129,193},{193,1... | collective-permute-start | bytes 1376264 | tf_op jit(solution)/shard_map/ppermute | solution.py:40
  70.3 24.1 %collective-permute-start.2 = (bf16[464,512]{1,0:T(8,128)(2,1)S(1)}, bf16[464,512]{1,0:T(8,128)(2,1)}, u32[]{:S(2)}, u32[]{:S(2)}) collective-permute-start(bf16[464,512]{1,0:T(8,128)(2,1)S(1)} %collective-permute-done.1.refs_0_), channel_id=1, source_target_pairs={{0,2},{2,4},{4,6},{6,0},{1,3},{3,5},{5,7},{7,1},{8,10},{10,12},{12... | collective-permute-start | bytes 1425416 | tf_op jit(solution)/shard_map/ppermute | solution.py:40
  71.6 22.9 %collective-permute-start.13 = (bf16[448,512]{1,0:T(8,128)(2,1)}, bf16[448,512]{1,0:T(8,128)(2,1)}, u32[]{:S(2)}, u32[]{:S(2)}) collective-permute-start(bf16[448,512]{1,0:T(8,128)(2,1)} %collective-permute-done.12.refs_7_), channel_id=1, source_target_pairs={{0,192},{64,0},{128,64},{192,128},{1,193},{65,1},{129,65},{193,129... | collective-permute-start | bytes 1376264 | tf_op jit(solution)/shard_map/ppermute | solution.py:40
  73.8 20.7 %collective-permute-start.6 = (bf16[464,512]{1,0:T(8,128)(2,1)S(1)}, bf16[464,512]{1,0:T(8,128)(2,1)}, u32[]{:S(2)}, u32[]{:S(2)}) collective-permute-start(bf16[464,512]{1,0:T(8,128)(2,1)S(1)} %collective-permute-done.5.refs_3_), channel_id=1, source_target_pairs={{0,6},{2,0},{4,2},{6,4},{1,7},{3,1},{5,3},{7,5},{8,14},{10,8},{12,... | collective-permute-start | bytes 1425416 | tf_op jit(solution)/shard_map/ppermute | solution.py:40
  103.1 10.2 %all-to-all-start.1 = ((f32[16,8,256]{2,1,0:T(8,128)}), f32[16,8,256]{2,1,0:T(8,128)S(1)}, u32[]{:S(2)}, u32[]{:S(2)}) async-start(f32[16,8,256]{2,1,0:T(8,128)} %shard_map.93), calls=%async_computation.1 | async-start | bytes 262144 | tf_op jit(solution)/shard_map/all_to_all | solution.py:411
  114.0 15.7 %all-to-all-start.2 = ((f32[16,8,256]{2,1,0:T(8,128)}), f32[16,8,256]{2,1,0:T(8,128)S(1)}, u32[]{:S(2)}, u32[]{:S(2)}) async-start(f32[16,8,256]{2,1,0:T(8,128)} %shard_map.94), calls=%async_computation.2 | async-start | bytes 262144 | tf_op jit(solution)/shard_map/all_to_all | solution.py:419

commit v2 on v0

--- a/solution.py
+++ b/solution.py
@@ -149,53 +149,126 @@
     return lax.dot_general(w[...], block, (((1,), (1,)), ((), ())), preferred_element_type=F32)
 
 
-def matmul_kernel(which, last):
-    def kernel(at, *refs):
-        y = at[0]
-        n = 2 * len(which)
-        a, b, weights, rest = refs[:n], refs[n : 2 * n], refs[2 * n : 2 * n + 2], refs[2 * n + 2 :]
-        if last:
-            before, ids, out, acc, held, held_w, sems = rest
+LOOK = 4
+
+
+class Arrivals:
+    def __init__(self):
+        self.order, self.copies, self.begun = [], {}, 0
+
+    def add(self, key, *copies):
+        if key not in self.copies:
+            self.order.append(key)
+            self.copies[key] = copies
+
+    def begin(self, upto):
+        while self.begun < min(upto, len(self.order)):
+            for copy in self.copies[self.order[self.begun]]:
+                copy.start()
+            self.begun += 1
+
+    def wait(self, key):
+        if self.copies.get(key):
+            self.begin(self.order.index(key) + 1 + LOOK)
+            for copy in self.copies[key]:
+                copy.wait()
+            self.copies[key] = ()
+
+
+def names_of(which):
+    return [(k, j, part) for k in range(2) for j in which for part in range(2)]
+
+
+def plan_of(which):
+    plan = []
+    for i in [i for i in range(NX) if i not in which] + list(which):
+        terms = [((j, 0), (0, j, i // 2), i % 2 * TALL) for j in which]
+        if i in which:
+            terms += [((j, 1), (1, i, j // 2), j % 2 * ROWS) for j in range(NY)]
+        plan.append((i, terms))
+    return plan
+
+
+NEAR, FAR = (0, 1, 2), (3,)
+KEPT = tuple((j, 1) for j in range(NY)) + ((3, 0),)
+NEAR_LATE = [n for n in names_of(NEAR) if n[1] and n[1] - 1 != n[2]]
+FAR_LATE = names_of(FAR)
+
+
+def piece_copies(arrivals, name, pieces, late, held_p, sems):
+    ref = pieces[name]
+    if name not in late:
+        return ref
+    n = late.index(name)
+    arrivals.add(name, pltpu.make_async_copy(ref, held_p.at[n, pl.ds(0, ref.shape[0])], sems.at[n]))
+    return held_p.at[n]
+
+
+def near_kernel(at, *refs):
+    pieces = dict(zip(names_of(NEAR), refs))
+    weights, rest = refs[len(pieces) : len(pieces) + 2], refs[len(pieces) + 2 :]
+    acc, kept, held_p, held_w, sems, sems_w = rest
+    arrivals, views, slices = Arrivals(), {}, {}
+
+    def slice_copies(key):
+        j, colour = key
+        if key in KEPT:
+            slices[key] = kept.at[KEPT.index(key)]
         else:
-            acc, held_w, sems = rest
-        wanted = [(j, 0) for j in which] + [(j, 1) for j in range(NY)]
-        copies = {}
-        for k, (j, core) in enumerate(wanted):
-            column = pl.multiple_of(((y + OFFSETS[j] + NY) % NY * NC + core) * WIDTH, WIDTH)
-            copies[j, core] = [
+            slices[key] = held_w.at[j]
+        column = ((at[0] + OFFSETS[j] + NY) % NY * NC + colour) * WIDTH
+        column = pl.multiple_of(column, WIDTH)
+        arrivals.add(
+            key,
+            *(
                 pltpu.make_async_copy(
-                    weights[w].at[:, pl.ds(column, WIDTH)], held_w.at[k, w], sems.at[k, w]
+                    weights[w].at[:, pl.ds(column, WIDTH)], slices[key].at[w], sems_w.at[j, colour, w]
                 )
                 for w in range(2)
-            ]
-            for copy in copies[j, core]:
-                copy.start()
-        ready = set()
-        for i in [i for i in range(NX) if i not in which] + list(which):
-            terms = []
-            for p, j in enumerate(which):
-                lo = i % 2 * TALL
-                terms.append(((j, 0), a[2 * p + i // 2][lo : lo + ROWS, :]))
-            if i in which:
-                p = which.index(i)
-                for j in range(NY):
-                    lo = j % 2 * ROWS
-                    terms.append(((j, 1), b[2 * p + j // 2][lo : lo + ROWS, :]))
-            for key, _ in terms:
-                if key not in ready:
-                    ready.add(key)
-                    for copy in copies[key]:
-                        copy.wait()
+            ),
+        )
+
+    plan = plan_of(NEAR)
+    for _, terms in plan:
+        for key, name, _ in terms:
+            if key not in slices:
+                slice_copies(key)
+            if name not in views:
+                views[name] = piece_copies(arrivals, name, pieces, NEAR_LATE, held_p, sems)
+    slice_copies((3, 0))
+    arrivals.begin(LOOK)
+    for i, terms in plan:
+        total = [None, None]
+        for key, name, lo in terms:
+            arrivals.wait(key)
+            arrivals.wait(name)
             for w in range(2):
-                total = before[i, w] if last else None
-                for key, block in terms:
-                    term = product(held_w.at[wanted.index(key), w], block)
-                    total = term if total is None else total + term
-                acc[i, w] = total
-        if last:
-            statistics(at, ids, acc, out, held)
-
-    return kernel
+                term = product(slices[key].at[w], views[name][lo : lo + ROWS, :])
+                total[w] = term if total[w] is None else total[w] + term
+        for w in range(2):
+            acc[i, w] = total[w]
+    arrivals.wait((3, 0))
+
+
+def far_kernel(at, *refs):
+    pieces = dict(zip(names_of(FAR), refs))
+    before, kept, ids, out, acc, held, held_p, sems = refs[len(pieces) :]
+    arrivals, views = Arrivals(), {}
+    plan = plan_of(FAR)
+    for _, terms in plan:
+        for _, name, _ in terms:
+            if name not in views:
+                views[name] = piece_copies(arrivals, name, pieces, FAR_LATE, held_p, sems)
+    arrivals.begin(LOOK)
+    for i, terms in plan:
+        total = [before[i, w] for w in range(2)]
+        for key, name, lo in terms:
+            arrivals.wait(name)
+            for w in range(2):
+                total[w] = total[w] + product(kept.at[KEPT.index(key), w], views[name][lo : lo + ROWS, :])
+        for w in range(2):
+            acc[i, w] = total[w]
+    statistics(at, ids, acc, out, held)
 
 
 def statistics(at, ids, acc, out, held):
@@ -218,31 +291,46 @@
         out[k] = held[...]
 
 
-def head(at, plane0, plane1, weights, ids):
-    acc_shape = (NX, 2, SHARD, ROWS)
-
-    def call(which, *more):
-        parts = [piece for j in which for piece in plane0[j]]
-        parts += [piece for j in which for piece in plane1[j]]
-        last = bool(more)
-        slices = len(which) + NY
-        scratch = [pltpu.VMEM(acc_shape, F32), pltpu.VMEM((8, 256), F32)] if last else []
-        scratch += [
-            pltpu.VMEM((slices, 2, SHARD, WIDTH), BF16),
-            pltpu.SemaphoreType.DMA((slices, 2)),
-        ]
-        shape = (NX * NY, 8, 256) if last else acc_shape
-        return pl.pallas_call(
-            matmul_kernel(which, last),
-            out_shape=jax.ShapeDtypeStruct(shape, F32),
-            in_specs=[SMEM] + [VMEM] * len(parts) + [HBM] * 2 + [VMEM] * len(more),
-            out_specs=VMEM,
-            scratch_shapes=scratch,
-            compiler_params=params(26),
-        )(at, *parts, *weights, *more)
-
-    acc = call((0, 1, 2))
-    return call((3,), acc, ids)
+def head(at, planes, weights, ids):
+    acc = pltpu.VMEM((NX, 2, SHARD, ROWS), F32)
+    kept = pltpu.VMEM((len(KEPT), 2, SHARD, WIDTH), BF16)
+
+    def operands(which, late):
+        parts, specs = [], []
+        for name in names_of(which):
+            piece = planes[name[0]][name[1]][name[2]]
+            parts += in_hbm(piece) if name in late else [piece]
+            specs.append(HBM if name in late else VMEM)
+        return parts, specs
+
+    parts, specs = operands(NEAR, NEAR_LATE)
+    sums, slices = pl.pallas_call(
+        near_kernel,
+        out_shape=[acc, kept],
+        in_specs=[SMEM] + specs + [HBM] * 2,
+        out_specs=[VMEM, VMEM],
+        scratch_shapes=[
+            pltpu.VMEM((len(NEAR_LATE), 2 * TALL, WIDTH), BF16),
+            pltpu.VMEM((len(NEAR), 2, SHARD, WIDTH), BF16),
+            pltpu.SemaphoreType.DMA((len(NEAR_LATE),)),
+            pltpu.SemaphoreType.DMA((NY, NC, 2)),
+        ],
+        compiler_params=params(24),
+    )(at, *parts, *weights)
+    parts, specs = operands(FAR, FAR_LATE)
+    return pl.pallas_call(
+        far_kernel,
+        out_shape=jax.ShapeDtypeStruct((NX * NY, 8, 256), F32),
+        in_specs=[SMEM] + specs + [VMEM] * 3,
+        out_specs=VMEM,
+        scratch_shapes=[
+            acc,
+            pltpu.VMEM((8, 256), F32),
+            pltpu.VMEM((len(FAR_LATE), 2 * TALL, WIDTH), BF16),
+            pltpu.SemaphoreType.DMA((len(FAR_LATE),)),
+        ],
+        compiler_params=params(24),
+    )(at, *parts, sums, slices, ids)
 
 
 def merged_parts(parts):
@@ -263,7 +351,7 @@
         out[k, 4:] = hit
 
 
-def final_kernel(parts, source, advantage, length, logprobs, weighted):
+def final_kernel(parts, source, reward, length, logprobs, advantage, weighted):
     tables = []
     for core in range(NC):
         lse, hit = merged_parts([parts[z * NC + core] for z in range(NZ)])
@@ -286,7 +374,10 @@
     row = lax.broadcasted_iota(jnp.int32, (SLOTS, SLOTS), 0)
     across = lax.broadcasted_iota(jnp.int32, (SLOTS, SLOTS), 1)
     line = jnp.sum(jnp.where(row == across, total, 0.0), axis=0, keepdims=True)
-    weighted[...] = advantage[...] * line / length[...]
+    own = reward[...].astype(F32) * REWARD_UNIT
+    spare = own - (jnp.sum(own, axis=1, keepdims=True) - own) / (SAMPLES - 1.0)
+    advantage[...] = spare
+    weighted[...] = spare * line / length[...].astype(F32)
 
 
 def local(hidden, weight, targets, lengths, rewards, arrival):
@@ -295,7 +386,7 @@
     swapped = shift(weight, "c", 1)
     sent = pl.pallas_call(
         pack_kernel,
-        out_shape=jax.ShapeDtypeStruct((NZ * NC, MSG, WIDTH), BF16),
+        out_shape=pltpu.VMEM((NZ * NC, MSG, WIDTH), BF16),
         in_specs=[HBM] * 4,
         out_specs=VMEM,
         scratch_shapes=[
@@ -318,8 +409,8 @@
         out_specs=[VMEM, VMEM],
         compiler_params=params(),
     )(got)
-    plane0, plane1 = gathered_planes((own0, own1), ("x", "y"), ("y", "x"))
-    line0 = plane0[0]
+    planes = gathered_planes((own0, own1), ("x", "y"), ("y", "x"))
+    line0 = planes[0][0]
 
     metas = jnp.stack([line0[i // 2][i % 2 * TALL + ROWS : i % 2 * TALL + TALL] for i in range(NX)])
     whole = metas.astype(F32).astype(jnp.int32)
@@ -329,7 +420,7 @@
     dp = x * NZ + z
     base = (dp * NY + y) * NC
     at = jnp.stack([y, x, (base + c) * shard, (base + 1 - c) * shard]).astype(jnp.int32)
-    partial = head(at, plane0, plane1, in_hbm(weight.T, swapped.T), ids)
+    partial = head(at, planes, in_hbm(weight.T, swapped.T), ids)
 
     order = (lax.iota(jnp.int32, NX) - x + NX) % NX
     relative = jnp.where(order == 0, 0, jnp.where(order == 3, 1, order + 1))
@@ -352,36 +443,35 @@
 
     slot_of = lookup(slot_ids)
     length_of = lookup(all_lengths)
-    reward_of = lookup(all_rewards).astype(F32) * REWARD_UNIT
+    reward_of = lookup(all_rewards)
     offset_of = lookup(jnp.cumsum(all_lengths, axis=1) - all_lengths)
     group = slot_of // SLOTS
     line = offset_of[:, None] + lax.iota(jnp.int32, WINDOW)[None, :]
     usable = lax.iota(jnp.int32, WINDOW)[None, :] < length_of[:, None]
     place = group // NZ * 256 + group % NZ * HALF
     source = jnp.where(usable, place[:, None] + line // HALF * 1024 + line % HALF, -1)
-    groups = jnp.sum(reward_of.reshape(SLOTS // SAMPLES, SAMPLES), axis=1)
-    advantages = reward_of - (jnp.repeat(groups, SAMPLES) - reward_of) / (SAMPLES - 1.0)
 
     stats = lax.all_to_all(partial, ("x", "y"), 0, 0, tiled=True)
     stats = pl.pallas_call(
         merge_kernel,
-        out_shape=jax.ShapeDtypeStruct((NZ * NC, 8, 256), F32),
+        out_shape=pltpu.VMEM((NZ * NC, 8, 256), F32),
         in_specs=[VMEM],
         out_specs=VMEM,
         compiler_params=params(),
     )(stats)
     stats = lax.all_to_all(stats, ("z", "c"), 0, 0, tiled=True)
-    token_logprobs, weighted = pl.pallas_call(
+    token_logprobs, advantages, weighted = pl.pallas_call(
         final_kernel,
         out_shape=[
             jax.ShapeDtypeStruct((SLOTS, WINDOW), F32),
             jax.ShapeDtypeStruct((1, SLOTS), F32),
+            jax.ShapeDtypeStruct((1, SLOTS), F32),
         ],
         in_specs=[VMEM] * 4,
-        out_specs=[VMEM, VMEM],
+        out_specs=[VMEM] * 3,
         compiler_params=params(),
-    )(stats, source, advantages[None, :], length_of.astype(F32)[None, :])
-    return token_logprobs, advantages, weighted.reshape(SLOTS)
+    )(stats, source, reward_of[None, :], length_of[None, :])
+    return token_logprobs, advantages.reshape(SLOTS), weighted.reshape(SLOTS)
 
 
 def solution(mesh):

time: 127 us -> 126 us (level)
  other arithmetic: 3.24 us -> 0.83 us
  waiting for transfers between devices: 39.7 us -> 41.2 us
  Pallas kernels: 21.9 us -> 20.6 us
    ppermute x19, waiting for transfers between devices: 24 us -> 26.3 us  [shift(): lax.ppermute(value, axis, [(i, (i + by) % size) for i in range(size)])]
    all_to_all x1, starting transfers between devices: 8.71 us -> 11 us  [local(): stats = lax.all_to_all(stats, ('z', 'c'), 0, 0, tiled=True)]
    sub x2 -> x0, other arithmetic: 1.82 us -> none  [local(): reward_of - (jnp.repeat(groups, SAMPLES) - reward_of) / (SAMPLES - 1.0)]
    pallas_call x4, Pallas kernels: 20.3 us -> 18.9 us  [the longest x1 10.2 us: head(): pl.pallas_call(near_kernel, out_shape=[acc, kept], in_specs=[SMEM] + spec...]
  transfers between devices with their start and end apart: 21 -> 21, of which waited for: 10 -> 9; matrix products, arithmetic and copies ran while one was open for 3% -> 1% of each run, Pallas kernels for 10% -> 9%
where the time goes in v2:
time: 126 us
  waiting for transfers between devices  41.2 us (33%)
  starting transfers between devices  37.1 us (29%)
  blocking collectives  23.9 us (19%)
  Pallas kernels  20.6 us (16%)
    ppermute x19, waiting for transfers between devices, shift(): lax.ppermute(value, axis, [(i, (i + by) % size) for i in range(size)])  26.3 us
    all_to_all x1, blocking collectives, local(): got = lax.all_to_all(sent, ('z', 'c'), 0, 0, tiled=True)  23.9 us
    ppermute x19, starting transfers between devices, shift(): lax.ppermute(value, axis, [(i, (i + by) % size) for i in range(size)])  22.6 us
    all_to_all x1, starting transfers between devices, local(): stats = lax.all_to_all(stats, ('z', 'c'), 0, 0, tiled=True)  11 us
    pallas_call x1, Pallas kernels, head(): pl.pallas_call(near_kernel, out_shape=[acc, kept], in_specs=[SMEM] + spec...  10.2 us
    all_to_all x1, waiting for transfers between devices, local(): stats = lax.all_to_all(stats, ('z', 'c'), 0, 0, tiled=True)  8.78 us
    pallas_call x1, Pallas kernels, head(): pl.pallas_call(far_kernel, out_shape=jax.ShapeDtypeStruct((NX * NY, 8, 25...  6.6 us
    all_to_all x1, waiting for transfers between devices, local(): stats = lax.all_to_all(partial, ('x', 'y'), 0, 0, tiled=True)  6.06 us
  transfers between devices with their start and end apart: 21, of which 9 were waited for; matrix products, arithmetic and copies ran while one was open for 1% of the time, Pallas kernels for 9%

profile of v2, /device:TPU:1, one launch (start us, length us, event | category | flops | bytes accessed | tf_op | source)
XLA Modules:
  0.0 125.6 jit_solution(8188371976007608514)
XLA Ops:
  0.6 3.3 %collective-permute-start.18 = (bf16[4096,501]{0,1:T(8,128)(2,1)}, bf16[4096,501]{0,1:T(8,128)(2,1)}, u32[]{:S(2)}, u32[]{:S(2)}) collective-permute-start(bf16[4096,501]{0,1:T(8,128)(2,1)} %param.7), channel_id=1, source_target_pairs={{0,1},{1,0},{2,3},{3,2},{4,5},{5,4},{6,7},{7,6},{8,9},{9,8},{10,11... | collective-permute-start | bytes 12312584 | tf_op jit(solution)/shard_map/ppermute | solution.py:40
  3.9 1.4 %shard_map.85 = bf16[16,32,512]{2,1,0:T(8,128)(2,1)S(1)} custom-call(bf16[14,8,512]{2,1,0:T(8,128)(2,1)} %bitcast.27, s32[8,14]{1,0:T(8,128)} %targets_hbm.1, s32[1,8]{1,0:T(1,128)} %lengths_hbm.1, s32[1,8]{1,0:T(1,128)} %rewards_hbm.1), custom_call_target="tpu_custom_call" | custom-call | tf_op jit(solution)/shard_map/pallas_call | solution.py:387
  5.4 23.9 %all_to_all.15.got = bf16[16,32,512]{2,1,0:T(8,128)(2,1)S(1)} all-to-all(bf16[16,32,512]{2,1,0:T(8,128)(2,1)S(1)} %shard_map.85), channel_id=1, replica_groups=mesh['x'=4,'z'=8,'y'=4,'c'=2] {'z','c'}, dimensions={0} | all-to-all | bytes 1048576 | tf_op jit(solution)/shard_map/all_to_all | solution.py:401
  29.2 0.1 shard_map.86
  29.3 1.3 %collective-permute-start = (bf16[232,512]{1,0:T(8,128)(2,1)S(1)}, bf16[232,512]{1,0:T(8,128)(2,1)S(1)}, u32[]{:S(2)}, u32[]{:S(2)}) collective-permute-start(bf16[232,512]{1,0:T(8,128)(2,1)S(1)} %get-tuple-element.10.one), channel_id=1, source_target_pairs={{0,64},{64,128},{128,192},{192,0},{1,65},{65,129},{129,193},{193,1... | collective-permute-start | bytes 712712 | tf_op jit(solution)/shard_map/ppermute | solution.py:40
  30.6 1.3 %collective-permute-start.7 = (bf16[224,512]{1,0:T(8,128)(2,1)S(1)}, bf16[224,512]{1,0:T(8,128)(2,1)S(1)}, u32[]{:S(2)}, u32[]{:S(2)}) collective-permute-start(bf16[224,512]{1,0:T(8,128)(2,1)S(1)} %get-tuple-element.11.one), channel_id=1, source_target_pairs={{0,2},{2,4},{4,6},{6,0},{1,3},{3,5},{5,7},{7,1},{8,10},{10,12},{12... | collective-permute-start | bytes 688136 | tf_op jit(solution)/shard_map/ppermute | solution.py:40
  31.9 1.5 %collective-permute-start.3 = (bf16[232,512]{1,0:T(8,128)(2,1)S(1)}, bf16[232,512]{1,0:T(8,128)(2,1)S(1)}, u32[]{:S(2)}, u32[]{:S(2)}) collective-permute-start(bf16[232,512]{1,0:T(8,128)(2,1)S(1)} %get-tuple-element.10.one), channel_id=1, source_target_pairs={{0,192},{64,0},{128,64},{192,128},{1,193},{65,1},{129,65},{193,129... | collective-permute-start | bytes 712712 | tf_op jit(solution)/shard_map/ppermute | solution.py:40
  33.4 1.4 %collective-permute-start.10 = (bf16[224,512]{1,0:T(8,128)(2,1)S(1)}, bf16[224,512]{1,0:T(8,128)(2,1)S(1)}, u32[]{:S(2)}, u32[]{:S(2)}) collective-permute-start(bf16[224,512]{1,0:T(8,128)(2,1)S(1)} %get-tuple-element.11.one), channel_id=1, source_target_pairs={{0,6},{2,0},{4,2},{6,4},{1,7},{3,1},{5,3},{7,5},{8,14},{10,8},{12,... | collective-permute-start | bytes 688136 | tf_op jit(solution)/shard_map/ppermute | solution.py:40
  34.8 2.9 %collective-permute-done.two = bf16[232,512]{1,0:T(8,128)(2,1)S(1)} collective-permute-done((bf16[232,512]{1,0:T(8,128)(2,1)S(1)}, bf16[232,512]{1,0:T(8,128)(2,1)S(1)}, u32[]{:S(2)}, u32[]{:S(2)}) %collective-permute-start) | collective-permute-done | bytes 237600 | tf_op jit(solution)/shard_map/ppermute | solution.py:40
  37.7 0.0 collective-permute-start.4
  37.7 1.0 collective-permute-done.7.two
  38.7 0.4 collective-permute-start.11
  39.1 1.7 %collective-permute-done.10.one = bf16[224,512]{1,0:T(8,128)(2,1)S(1)} collective-permute-done((bf16[224,512]{1,0:T(8,128)(2,1)S(1)}, bf16[224,512]{1,0:T(8,128)(2,1)S(1)}, u32[]{:S(2)}, u32[]{:S(2)}) %collective-permute-start.10) | collective-permute-done | bytes 229408 | tf_op jit(solution)/shard_map/ppermute | solution.py:40
  40.8 1.3 %collective-permute-start.1 = (bf16[464,512]{1,0:T(8,128)(2,1)S(1)}, bf16[464,512]{1,0:T(8,128)(2,1)S(1)}, u32[]{:S(2)}, u32[]{:S(2)}) collective-permute-start(bf16[464,512]{1,0:T(8,128)(2,1)S(1)} %shard_map.87.refs_0_), channel_id=1, source_target_pairs={{0,2},{2,4},{4,6},{6,0},{1,3},{3,5},{5,7},{7,1},{8,10},{10,12},{12... | collective-permute-start | bytes 1425416 | tf_op jit(solution)/shard_map/ppermute | solution.py:40
  42.1 1.4 %collective-permute-start.15 = (bf16[464,512]{1,0:T(8,128)(2,1)S(1)}, bf16[464,512]{1,0:T(8,128)(2,1)}, u32[]{:S(2)}, u32[]{:S(2)}) collective-permute-start(bf16[464,512]{1,0:T(8,128)(2,1)S(1)} %shard_map.87.refs_0_), channel_id=1, source_target_pairs={{0,6},{2,0},{4,2},{6,4},{1,7},{3,1},{5,3},{7,5},{8,14},{10,8},{12,... | collective-permute-start | bytes 1425416 | tf_op jit(solution)/shard_map/ppermute | solution.py:40
  43.6 3.3 %collective-permute-done.11.two = bf16[224,512]{1,0:T(8,128)(2,1)S(1)} collective-permute-done((bf16[224,512]{1,0:T(8,128)(2,1)S(1)}, bf16[224,512]{1,0:T(8,128)(2,1)S(1)}, u32[]{:S(2)}, u32[]{:S(2)}) %collective-permute-start.11) | collective-permute-done | bytes 229408 | tf_op jit(solution)/shard_map/ppermute | solution.py:40
  46.9 1.2 collective-permute-start.8
  48.1 1.5 %collective-permute-start.17 = (bf16[448,512]{1,0:T(8,128)(2,1)S(1)}, bf16[448,512]{1,0:T(8,128)(2,1)}, u32[]{:S(2)}, u32[]{:S(2)}) collective-permute-start(bf16[448,512]{1,0:T(8,128)(2,1)S(1)} %shard_map.89.refs_6_), channel_id=1, source_target_pairs={{0,192},{64,0},{128,64},{192,128},{1,193},{65,1},{129,65},{193,129... | collective-permute-start | bytes 1376264 | tf_op jit(solution)/shard_map/ppermute | solution.py:40
  49.7 8.8 %collective-permute-done.8.refs_8_ = bf16[448,512]{1,0:T(8,128)(2,1)S(1)} collective-permute-done((bf16[448,512]{1,0:T(8,128)(2,1)S(1)}, bf16[448,512]{1,0:T(8,128)(2,1)S(1)}, u32[]{:S(2)}, u32[]{:S(2)}) %collective-permute-start.8) | collective-permute-done | bytes 458784 | tf_op jit(solution)/shard_map/ppermute | solution.py:40
  58.4 1.6 %collective-permute-start.12 = (bf16[448,512]{1,0:T(8,128)(2,1)S(1)}, bf16[448,512]{1,0:T(8,128)(2,1)}, u32[]{:S(2)}, u32[]{:S(2)}) collective-permute-start(bf16[448,512]{1,0:T(8,128)(2,1)S(1)} %shard_map.90.refs_7_), channel_id=1, source_target_pairs={{0,192},{64,0},{128,64},{192,128},{1,193},{65,1},{129,65},{193,129... | collective-permute-start | bytes 1376264 | tf_op jit(solution)/shard_map/ppermute | solution.py:40
  60.0 1.5 %collective-permute-start.5 = (bf16[464,512]{1,0:T(8,128)(2,1)S(1)}, bf16[464,512]{1,0:T(8,128)(2,1)S(1)}, u32[]{:S(2)}, u32[]{:S(2)}) collective-permute-start(bf16[464,512]{1,0:T(8,128)(2,1)S(1)} %shard_map.88.refs_1_), channel_id=1, source_target_pairs={{0,6},{2,0},{4,2},{6,4},{1,7},{3,1},{5,3},{7,5},{8,14},{10,8},{12,... | collective-permute-start | bytes 1425416 | tf_op jit(solution)/shard_map/ppermute | solution.py:40
  61.5 0.0 collective-permute-start.14
  61.6 0.1 pad_add_fusion.at
  61.6 0.1 iota_compare_fusion.1
  61.7 6.3 %collective-permute-done.12.refs_11_ = bf16[448,512]{1,0:T(8,128)(2,1)} collective-permute-done((bf16[448,512]{1,0:T(8,128)(2,1)S(1)}, bf16[448,512]{1,0:T(8,128)(2,1)}, u32[]{:S(2)}, u32[]{:S(2)}) %collective-permute-start.12) | collective-permute-done | bytes 458784 | tf_op jit(solution)/shard_map/ppermute | solution.py:40
  68.0 0.8 collective-permute-start.9
  68.8 2.3 %collective-permute-done.16.refs_9_ = bf16[448,512]{1,0:T(8,128)(2,1)S(1)} collective-permute-done((bf16[448,512]{1,0:T(8,128)(2,1)S(1)}, bf16[448,512]{1,0:T(8,128)(2,1)S(1)}, u32[]{:S(2)}, u32[]{:S(2)}) %collective-permute-start.16) | collective-permute-done | bytes 458784 | tf_op jit(solution)/shard_map/ppermute | solution.py:40
  71.1 1.6 %collective-permute-start.13 = (bf16[448,512]{1,0:T(8,128)(2,1)}, bf16[448,512]{1,0:T(8,128)(2,1)}, u32[]{:S(2)}, u32[]{:S(2)}) collective-permute-start(bf16[448,512]{1,0:T(8,128)(2,1)} %collective-permute-done.12.refs_11_), channel_id=1, source_target_pairs={{0,192},{64,0},{128,64},{192,128},{1,193},{65,1},{129,65},{193,129... | collective-permute-start | bytes 1376264 | tf_op jit(solution)/shard_map/ppermute | solution.py:40
  72.8 0.8 copy-done
  73.6 2.5 %collective-permute-start.6 = (bf16[464,512]{1,0:T(8,128)(2,1)S(1)}, bf16[464,512]{1,0:T(8,128)(2,1)}, u32[]{:S(2)}, u32[]{:S(2)}) collective-permute-start(bf16[464,512]{1,0:T(8,128)(2,1)S(1)} %collective-permute-done.5.refs_5_), channel_id=1, source_target_pairs={{0,6},{2,0},{4,2},{6,4},{1,7},{3,1},{5,3},{7,5},{8,14},{10,8},{12,... | collective-permute-start | bytes 1425416 | tf_op jit(solution)/shard_map/ppermute | solution.py:40
  76.2 0.1 reshape.116
  76.3 0.1 select_reduce_fusion
  76.4 0.2 reduce_window_sum.11
  76.5 10.2 %shard_map.91 = (f32[4,2,501,224]{3,2,1,0:T(8,128)S(1)}, bf16[5,2,501,512]{3,2,1,0:T(8,128)(2,1)S(1)}) custom-call(s32[4]{0:T(128)S(1)} %pad_add_fusion.at, bf16[464,512]{1,0:T(8,128)(2,1)S(1)} %shard_map.87.refs_0_, bf16[464,512]{1,0:T(8,128)(2,1)S(1)} %shard_map.88.refs_1_, bf16[464,512]{1,0:T(8,128)(2,1)S(1)} %collective-permute-done.1.refs_2_, ...), custom_call_target="tpu_custom_call" | custom-call | tf_op jit(solution)/shard_map/pallas_call | solution.py:307
  86.8 0.0 copy-start.2
  86.8 6.6 %shard_map.92 = f32[16,8,256]{2,1,0:T(8,128)} custom-call(s32[4]{0:T(128)S(1)} %pad_add_fusion.at, bf16[464,512]{1,0:T(8,128)(2,1)} %collective-permute-done.2.refs_0_, bf16[464,512]{1,0:T(8,128)(2,1)} %collective-permute-done.6.refs_1_, bf16[448,512]{1,0:T(8,128)(2,1)} %collective-permute-done.9.refs_2_, bf16[448,512]{1,0:T(8,128)(2,1)} %collective-permute-done.13.refs_3_, ...), custom_call_target="tpu_custom_call" | custom-call | tf_op jit(solution)/shard_map/pallas_call | solution.py:321
  93.4 3.5 %all-to-all-start.1 = ((f32[16,8,256]{2,1,0:T(8,128)}), f32[16,8,256]{2,1,0:T(8,128)S(1)}, u32[]{:S(2)}, u32[]{:S(2)}) async-start(f32[16,8,256]{2,1,0:T(8,128)} %shard_map.92), calls=%async_computation.1 | async-start | bytes 262144 | tf_op jit(solution)/shard_map/all_to_all | solution.py:454
  96.9 0.1 slice_subtract_fusion
  97.0 0.1 broadcast_in_dim.85
  97.1 0.1 broadcast_in_dim.89
  97.2 0.1 broadcast_in_dim.91
  97.3 0.2 fusion.5
  97.5 6.1 %all-to-all-done.1.parts = f32[16,8,256]{2,1,0:T(8,128)S(1)} async-done(((f32[16,8,256]{2,1,0:T(8,128)}), f32[16,8,256]{2,1,0:T(8,128)S(1)}, u32[]{:S(2)}, u32[]{:S(2)}) %all-to-all-start.1) | async-done | bytes 131104 | tf_op jit(solution)/shard_map/all_to_all | solution.py:454
  103.6 0.7 shard_map.93
  104.3 11.0 %all-to-all-start.2 = ((f32[16,8,256]{2,1,0:T(8,128)}), f32[16,8,256]{2,1,0:T(8,128)S(1)}, u32[]{:S(2)}, u32[]{:S(2)}) async-start(f32[16,8,256]{2,1,0:T(8,128)} %shard_map.93), calls=%async_computation.2 | async-start | bytes 262144 | tf_op jit(solution)/shard_map/all_to_all | solution.py:462
  115.3 0.1 fusion.9.source
  115.4 8.8 %all-to-all-done.2.parts = f32[16,8,256]{2,1,0:T(8,128)S(1)} async-done(((f32[16,8,256]{2,1,0:T(8,128)}), f32[16,8,256]{2,1,0:T(8,128)S(1)}, u32[]{:S(2)}, u32[]{:S(2)}) %all-to-all-start.2) | async-done | bytes 131104 | tf_op jit(solution)/shard_map/all_to_all | solution.py:462
  124.1 1.4 %shard_map.94 = (f32[8,14]{1,0:T(8,128)}, f32[1,8]{1,0:T(1,128)}, f32[1,8]{1,0:T(1,128)}) custom-call(f32[16,8,256]{2,1,0:T(8,128)S(1)} %all-to-all-done.2.parts, s32[8,14]{1,0:T(8,128)S(1)} %fusion.9.source, s32[1,8]{1,0:T(1,128)S(1)} %bitcast.22, s32[1,8]{1,0:T(1,128)S(1)} %bitcast.21), custom_call_target="tpu_custom_call" | custom-call | tf_op jit(solution)/shard_map/pallas_call | solution.py:463
  (31 shorter events, 0.2 us)
Async XLA Ops:
  0.6 75.9 %collective-permute-start.18 = (bf16[4096,501]{0,1:T(8,128)(2,1)}, bf16[4096,501]{0,1:T(8,128)(2,1)}, u32[]{:S(2)}, u32[]{:S(2)}) collective-permute-start(bf16[4096,501]{0,1:T(8,128)(2,1)} %param.7), channel_id=1, source_target_pairs={{0,1},{1,0},{2,3},{3,2},{4,5},{5,4},{6,7},{7,6},{8,9},{9,8},{10,11... | collective-permute-start | bytes 12312584 | tf_op jit(solution)/shard_map/ppermute | solution.py:40
  29.3 8.4 %collective-permute-start = (bf16[232,512]{1,0:T(8,128)(2,1)S(1)}, bf16[232,512]{1,0:T(8,128)(2,1)S(1)}, u32[]{:S(2)}, u32[]{:S(2)}) collective-permute-start(bf16[232,512]{1,0:T(8,128)(2,1)S(1)} %get-tuple-element.10.one), channel_id=1, source_target_pairs={{0,64},{64,128},{128,192},{192,0},{1,65},{65,129},{129,193},{193,1... | collective-permute-start | bytes 712712 | tf_op jit(solution)/shard_map/ppermute | solution.py:40
  30.6 8.1 %collective-permute-start.7 = (bf16[224,512]{1,0:T(8,128)(2,1)S(1)}, bf16[224,512]{1,0:T(8,128)(2,1)S(1)}, u32[]{:S(2)}, u32[]{:S(2)}) collective-permute-start(bf16[224,512]{1,0:T(8,128)(2,1)S(1)} %get-tuple-element.11.one), channel_id=1, source_target_pairs={{0,2},{2,4},{4,6},{6,0},{1,3},{3,5},{5,7},{7,1},{8,10},{10,12},{12... | collective-permute-start | bytes 688136 | tf_op jit(solution)/shard_map/ppermute | solution.py:40
  31.9 10.3 %collective-permute-start.3 = (bf16[232,512]{1,0:T(8,128)(2,1)S(1)}, bf16[232,512]{1,0:T(8,128)(2,1)S(1)}, u32[]{:S(2)}, u32[]{:S(2)}) collective-permute-start(bf16[232,512]{1,0:T(8,128)(2,1)S(1)} %get-tuple-element.10.one), channel_id=1, source_target_pairs={{0,192},{64,0},{128,64},{192,128},{1,193},{65,1},{129,65},{193,129... | collective-permute-start | bytes 712712 | tf_op jit(solution)/shard_map/ppermute | solution.py:40
  33.4 7.5 %collective-permute-start.10 = (bf16[224,512]{1,0:T(8,128)(2,1)S(1)}, bf16[224,512]{1,0:T(8,128)(2,1)S(1)}, u32[]{:S(2)}, u32[]{:S(2)}) collective-permute-start(bf16[224,512]{1,0:T(8,128)(2,1)S(1)} %get-tuple-element.11.one), channel_id=1, source_target_pairs={{0,6},{2,0},{4,2},{6,4},{1,7},{3,1},{5,3},{7,5},{8,14},{10,8},{12,... | collective-permute-start | bytes 688136 | tf_op jit(solution)/shard_map/ppermute | solution.py:40
  37.7 10.4 %collective-permute-start.4 = (bf16[232,512]{1,0:T(8,128)(2,1)S(1)}, bf16[232,512]{1,0:T(8,128)(2,1)S(1)}, u32[]{:S(2)}, u32[]{:S(2)}) collective-permute-start(bf16[232,512]{1,0:T(8,128)(2,1)S(1)} %collective-permute-done.two), channel_id=1, source_target_pairs={{0,64},{64,128},{128,192},{192,0},{1,65},{65,129},{129,193},{193,1... | collective-permute-start | bytes 712712 | tf_op jit(solution)/shard_map/ppermute | solution.py:40
  38.7 8.2 %collective-permute-start.11 = (bf16[224,512]{1,0:T(8,128)(2,1)S(1)}, bf16[224,512]{1,0:T(8,128)(2,1)S(1)}, u32[]{:S(2)}, u32[]{:S(2)}) collective-permute-start(bf16[224,512]{1,0:T(8,128)(2,1)S(1)} %collective-permute-done.7.two), channel_id=1, source_target_pairs={{0,2},{2,4},{4,6},{6,0},{1,3},{3,5},{5,7},{7,1},{8,10},{10,12},{12... | collective-permute-start | bytes 688136 | tf_op jit(solution)/shard_map/ppermute | solution.py:40
  40.8 19.2 %collective-permute-start.1 = (bf16[464,512]{1,0:T(8,128)(2,1)S(1)}, bf16[464,512]{1,0:T(8,128)(2,1)S(1)}, u32[]{:S(2)}, u32[]{:S(2)}) collective-permute-start(bf16[464,512]{1,0:T(8,128)(2,1)S(1)} %shard_map.87.refs_0_), channel_id=1, source_target_pairs={{0,2},{2,4},{4,6},{6,0},{1,3},{3,5},{5,7},{7,1},{8,10},{10,12},{12... | collective-permute-start | bytes 1425416 | tf_op jit(solution)/shard_map/ppermute | solution.py:40
  42.1 19.4 %collective-permute-start.15 = (bf16[464,512]{1,0:T(8,128)(2,1)S(1)}, bf16[464,512]{1,0:T(8,128)(2,1)}, u32[]{:S(2)}, u32[]{:S(2)}) collective-permute-start(bf16[464,512]{1,0:T(8,128)(2,1)S(1)} %shard_map.87.refs_0_), channel_id=1, source_target_pairs={{0,6},{2,0},{4,2},{6,4},{1,7},{3,1},{5,3},{7,5},{8,14},{10,8},{12,... | collective-permute-start | bytes 1425416 | tf_op jit(solution)/shard_map/ppermute | solution.py:40
  46.9 11.6 %collective-permute-start.8 = (bf16[448,512]{1,0:T(8,128)(2,1)S(1)}, bf16[448,512]{1,0:T(8,128)(2,1)S(1)}, u32[]{:S(2)}, u32[]{:S(2)}) collective-permute-start(bf16[448,512]{1,0:T(8,128)(2,1)S(1)} %shard_map.89.refs_6_), channel_id=1, source_target_pairs={{0,64},{64,128},{128,192},{192,0},{1,65},{65,129},{129,193},{193,1... | collective-permute-start | bytes 1376264 | tf_op jit(solution)/shard_map/ppermute | solution.py:40
  48.1 11.9 %collective-permute-start.17 = (bf16[448,512]{1,0:T(8,128)(2,1)S(1)}, bf16[448,512]{1,0:T(8,128)(2,1)}, u32[]{:S(2)}, u32[]{:S(2)}) collective-permute-start(bf16[448,512]{1,0:T(8,128)(2,1)S(1)} %shard_map.89.refs_6_), channel_id=1, source_target_pairs={{0,192},{64,0},{128,64},{192,128},{1,193},{65,1},{129,65},{193,129... | collective-permute-start | bytes 1376264 | tf_op jit(solution)/shard_map/ppermute | solution.py:40
  58.4 9.6 %collective-permute-start.12 = (bf16[448,512]{1,0:T(8,128)(2,1)S(1)}, bf16[448,512]{1,0:T(8,128)(2,1)}, u32[]{:S(2)}, u32[]{:S(2)}) collective-permute-start(bf16[448,512]{1,0:T(8,128)(2,1)S(1)} %shard_map.90.refs_7_), channel_id=1, source_target_pairs={{0,192},{64,0},{128,64},{192,128},{1,193},{65,1},{129,65},{193,129... | collective-permute-start | bytes 1376264 | tf_op jit(solution)/shard_map/ppermute | solution.py:40
  60.0 11.1 %collective-permute-start.16 = (bf16[448,512]{1,0:T(8,128)(2,1)S(1)}, bf16[448,512]{1,0:T(8,128)(2,1)S(1)}, u32[]{:S(2)}, u32[]{:S(2)}) collective-permute-start(bf16[448,512]{1,0:T(8,128)(2,1)S(1)} %shard_map.90.refs_7_), channel_id=1, source_target_pairs={{0,64},{64,128},{128,192},{192,0},{1,65},{65,129},{129,193},{193,1... | collective-permute-start | bytes 1376264 | tf_op jit(solution)/shard_map/ppermute | solution.py:40
  60.0 11.1 %collective-permute-start.5 = (bf16[464,512]{1,0:T(8,128)(2,1)S(1)}, bf16[464,512]{1,0:T(8,128)(2,1)S(1)}, u32[]{:S(2)}, u32[]{:S(2)}) collective-permute-start(bf16[464,512]{1,0:T(8,128)(2,1)S(1)} %shard_map.88.refs_1_), channel_id=1, source_target_pairs={{0,6},{2,0},{4,2},{6,4},{1,7},{3,1},{5,3},{7,5},{8,14},{10,8},{12,... | collective-permute-start | bytes 1425416 | tf_op jit(solution)/shard_map/ppermute | solution.py:40
  61.5 11.2 %collective-permute-start.14 = (bf16[464,512]{1,0:T(8,128)(2,1)S(1)}, bf16[464,512]{1,0:T(8,128)(2,1)S(1)}, u32[]{:S(2)}, u32[]{:S(2)}) collective-permute-start(bf16[464,512]{1,0:T(8,128)(2,1)S(1)} %shard_map.88.refs_1_), channel_id=1, source_target_pairs={{0,2},{2,4},{4,6},{6,0},{1,3},{3,5},{5,7},{7,1},{8,10},{10,12},{12... | collective-permute-start | bytes 1425416 | tf_op jit(solution)/shard_map/ppermute | solution.py:40
  68.0 18.7 %collective-permute-start.9 = (bf16[448,512]{1,0:T(8,128)(2,1)S(1)}, bf16[448,512]{1,0:T(8,128)(2,1)}, u32[]{:S(2)}, u32[]{:S(2)}) collective-permute-start(bf16[448,512]{1,0:T(8,128)(2,1)S(1)} %collective-permute-done.8.refs_8_), channel_id=1, source_target_pairs={{0,64},{64,128},{128,192},{192,0},{1,65},{65,129},{129,193},{193,1... | collective-permute-start | bytes 1376264 | tf_op jit(solution)/shard_map/ppermute | solution.py:40
  71.1 5.0 %copy-start.1 = (bf16[448,512]{1,0:T(8,128)(2,1)}, bf16[448,512]{1,0:T(8,128)(2,1)S(1)}, u32[]{:S(2)}) copy-start(bf16[448,512]{1,0:T(8,128)(2,1)S(1)} %collective-permute-done.16.refs_9_) | copy-start | bytes 1376260
  71.1 15.6 %collective-permute-start.2 = (bf16[464,512]{1,0:T(8,128)(2,1)S(1)}, bf16[464,512]{1,0:T(8,128)(2,1)}, u32[]{:S(2)}, u32[]{:S(2)}) collective-permute-start(bf16[464,512]{1,0:T(8,128)(2,1)S(1)} %collective-permute-done.1.refs_2_), channel_id=1, source_target_pairs={{0,2},{2,4},{4,6},{6,0},{1,3},{3,5},{5,7},{7,1},{8,10},{10,12},{12... | collective-permute-start | bytes 1425416 | tf_op jit(solution)/shard_map/ppermute | solution.py:40
  71.1 15.6 %collective-permute-start.13 = (bf16[448,512]{1,0:T(8,128)(2,1)}, bf16[448,512]{1,0:T(8,128)(2,1)}, u32[]{:S(2)}, u32[]{:S(2)}) collective-permute-start(bf16[448,512]{1,0:T(8,128)(2,1)} %collective-permute-done.12.refs_11_), channel_id=1, source_target_pairs={{0,192},{64,0},{128,64},{192,128},{1,193},{65,1},{129,65},{193,129... | collective-permute-start | bytes 1376264 | tf_op jit(solution)/shard_map/ppermute | solution.py:40
  72.8 0.8 copy-start
  73.6 13.2 %collective-permute-start.6 = (bf16[464,512]{1,0:T(8,128)(2,1)S(1)}, bf16[464,512]{1,0:T(8,128)(2,1)}, u32[]{:S(2)}, u32[]{:S(2)}) collective-permute-start(bf16[464,512]{1,0:T(8,128)(2,1)S(1)} %collective-permute-done.5.refs_5_), channel_id=1, source_target_pairs={{0,6},{2,0},{4,2},{6,4},{1,7},{3,1},{5,3},{7,5},{8,14},{10,8},{12,... | collective-permute-start | bytes 1425416 | tf_op jit(solution)/shard_map/ppermute | solution.py:40
  86.8 10.5 %copy-start.2 = (s32[256]{0:T(256)S(1)}, s32[256]{0:T(256)}, u32[]{:S(2)}) copy-start(s32[256]{0:T(256)} %param.11) | copy-start | bytes 3076
  93.4 10.2 %all-to-all-start.1 = ((f32[16,8,256]{2,1,0:T(8,128)}), f32[16,8,256]{2,1,0:T(8,128)S(1)}, u32[]{:S(2)}, u32[]{:S(2)}) async-start(f32[16,8,256]{2,1,0:T(8,128)} %shard_map.92), calls=%async_computation.1 | async-start | bytes 262144 | tf_op jit(solution)/shard_map/all_to_all | solution.py:454
  104.3 19.9 %all-to-all-start.2 = ((f32[16,8,256]{2,1,0:T(8,128)}), f32[16,8,256]{2,1,0:T(8,128)S(1)}, u32[]{:S(2)}, u32[]{:S(2)}) async-start(f32[16,8,256]{2,1,0:T(8,128)} %shard_map.93), calls=%async_computation.2 | async-start | bytes 262144 | tf_op jit(solution)/shard_map/all_to_all | solution.py:462

commit v3 on v2

--- a/solution.py
+++ b/solution.py
@@ -131,8 +131,10 @@
     up = [shift(own[k], firsts[k], 1) for k in both]
     down = [shift(own[k], firsts[k], -1) for k in both]
     far = [shift(up[k], firsts[k], 1) for k in both]
-    one = [join(own[k], up[k]) for k in both]
-    two = [join(down[k], far[k]) for k in both]
+    one, two = [], []
+    for k in both:
+        one.append(join(own[k], up[k]))
+        two.append(join(down[k], far[k]))
     planes = []
     for k in both:
         up1 = shift(one[k], lasts[k], 1)
@@ -192,7 +194,6 @@
 NEAR, FAR = (0, 1, 2), (3,)
 KEPT = tuple((j, 1) for j in range(NY)) + ((3, 0),)
 NEAR_LATE = [n for n in names_of(NEAR) if n[1] and n[1] - 1 != n[2]]
-FAR_LATE = names_of(FAR)
 
 
 def piece_copies(arrivals, name, pieces, late, held_p, sems):
@@ -252,20 +253,12 @@
 
 def far_kernel(at, *refs):
     pieces = dict(zip(names_of(FAR), refs))
-    before, kept, ids, out, acc, held, held_p, sems = refs[len(pieces) :]
-    arrivals, views = Arrivals(), {}
-    plan = plan_of(FAR)
-    for _, terms in plan:
-        for _, name, _ in terms:
-            if name not in views:
-                views[name] = piece_copies(arrivals, name, pieces, FAR_LATE, held_p, sems)
-    arrivals.begin(LOOK)
-    for i, terms in plan:
+    before, kept, ids, out, acc, held = refs[len(pieces) :]
+    for i, terms in plan_of(FAR):
         total = [before[i, w] for w in range(2)]
         for key, name, lo in terms:
-            arrivals.wait(name)
             for w in range(2):
-                total[w] = total[w] + product(kept.at[KEPT.index(key), w], views[name][lo : lo + ROWS, :])
+                total[w] = total[w] + product(kept.at[KEPT.index(key), w], pieces[name][lo : lo + ROWS, :])
         for w in range(2):
             acc[i, w] = total[w]
     statistics(at, ids, acc, out, held)
@@ -295,7 +288,7 @@
     acc = pltpu.VMEM((NX, 2, SHARD, ROWS), F32)
     kept = pltpu.VMEM((len(KEPT), 2, SHARD, WIDTH), BF16)
 
-    def operands(which, late):
+    def operands(which, late=()):
         parts, specs = [], []
         for name in names_of(which):
             piece = planes[name[0]][name[1]][name[2]]
@@ -317,18 +310,13 @@
         ],
         compiler_params=params(24),
     )(at, *parts, *weights)
-    parts, specs = operands(FAR, FAR_LATE)
+    parts, specs = operands(FAR)
     return pl.pallas_call(
         far_kernel,
         out_shape=jax.ShapeDtypeStruct((NX * NY, 8, 256), F32),
         in_specs=[SMEM] + specs + [VMEM] * 3,
         out_specs=VMEM,
-        scratch_shapes=[
-            acc,
-            pltpu.VMEM((8, 256), F32),
-            pltpu.VMEM((len(FAR_LATE), 2 * TALL, WIDTH), BF16),
-            pltpu.SemaphoreType.DMA((len(FAR_LATE),)),
-        ],
+        scratch_shapes=[acc, pltpu.VMEM((8, 256), F32)],
         compiler_params=params(24),
     )(at, *parts, sums, slices, ids)
 
@@ -420,7 +408,6 @@
     dp = x * NZ + z
     base = (dp * NY + y) * NC
     at = jnp.stack([y, x, (base + c) * shard, (base + 1 - c) * shard]).astype(jnp.int32)
-    partial = head(at, planes, in_hbm(weight.T, swapped.T), ids)
 
     order = (lax.iota(jnp.int32, NX) - x + NX) % NX
     relative = jnp.where(order == 0, 0, jnp.where(order == 3, 1, order + 1))
@@ -450,6 +437,8 @@
     usable = lax.iota(jnp.int32, WINDOW)[None, :] < length_of[:, None]
     place = group // NZ * 256 + group % NZ * HALF
     source = jnp.where(usable, place[:, None] + line // HALF * 1024 + line % HALF, -1)
+
+    partial = head(at, planes, in_hbm(weight.T, swapped.T), ids)
 
     stats = lax.all_to_all(partial, ("x", "y"), 0, 0, tiled=True)
     stats = pl.pallas_call(

time: 126 us -> 125 us (level)
  transfers between devices with their start and end apart: 21 -> 21, of which waited for: 9 -> 9; matrix products, arithmetic and copies ran while one was open for 1% -> 1% of each run, Pallas kernels for 9% -> 10%
where the time goes in v3:
time: 125 us
  waiting for transfers between devices  41.4 us (33%)
  starting transfers between devices  37 us (30%)
  blocking collectives  23.9 us (19%)
  Pallas kernels  19.7 us (16%)
    ppermute x19, waiting for transfers between devices, shift(): lax.ppermute(value, axis, [(i, (i + by) % size) for i in range(size)])  26.5 us
    all_to_all x1, blocking collectives, local(): got = lax.all_to_all(sent, ('z', 'c'), 0, 0, tiled=True)  23.9 us
    ppermute x19, starting transfers between devices, shift(): lax.ppermute(value, axis, [(i, (i + by) % size) for i in range(size)])  22.1 us
    all_to_all x1, starting transfers between devices, local(): stats = lax.all_to_all(stats, ('z', 'c'), 0, 0, tiled=True)  11.4 us
    pallas_call x1, Pallas kernels, head(): pl.pallas_call(near_kernel, out_shape=[acc, kept], in_specs=[SMEM] + spec...  10.4 us
    all_to_all x1, waiting for transfers between devices, local(): stats = lax.all_to_all(stats, ('z', 'c'), 0, 0, tiled=True)  8.78 us
    all_to_all x1, waiting for transfers between devices, local(): stats = lax.all_to_all(partial, ('x', 'y'), 0, 0, tiled=True)  6.06 us
    pallas_call x1, Pallas kernels, head(): pl.pallas_call(far_kernel, out_shape=jax.ShapeDtypeStruct((NX * NY, 8, 25...  5.56 us
  transfers between devices with their start and end apart: 21, of which 9 were waited for; matrix products, arithmetic and copies ran while one was open for 1% of the time, Pallas kernels for 10%

profile of v3, /device:TPU:1, one launch (start us, length us, event | category | flops | bytes accessed | tf_op | source)
XLA Modules:
  0.0 124.8 jit_solution(11636103014133962740)
XLA Ops:
  0.6 3.3 %collective-permute-start.18 = (bf16[4096,501]{0,1:T(8,128)(2,1)}, bf16[4096,501]{0,1:T(8,128)(2,1)}, u32[]{:S(2)}, u32[]{:S(2)}) collective-permute-start(bf16[4096,501]{0,1:T(8,128)(2,1)} %param.7), channel_id=1, source_target_pairs={{0,1},{1,0},{2,3},{3,2},{4,5},{5,4},{6,7},{7,6},{8,9},{9,8},{10,11... | collective-permute-start | bytes 12312584 | tf_op jit(solution)/shard_map/ppermute | solution.py:40
  3.9 1.4 %shard_map.85 = bf16[16,32,512]{2,1,0:T(8,128)(2,1)S(1)} custom-call(bf16[14,8,512]{2,1,0:T(8,128)(2,1)} %bitcast.27, s32[8,14]{1,0:T(8,128)} %targets_hbm.1, s32[1,8]{1,0:T(1,128)} %lengths_hbm.1, s32[1,8]{1,0:T(1,128)} %rewards_hbm.1), custom_call_target="tpu_custom_call" | custom-call | tf_op jit(solution)/shard_map/pallas_call | solution.py:375
  5.4 23.9 %all_to_all.15.got = bf16[16,32,512]{2,1,0:T(8,128)(2,1)S(1)} all-to-all(bf16[16,32,512]{2,1,0:T(8,128)(2,1)S(1)} %shard_map.85), channel_id=1, replica_groups=mesh['x'=4,'z'=8,'y'=4,'c'=2] {'z','c'}, dimensions={0} | all-to-all | bytes 1048576 | tf_op jit(solution)/shard_map/all_to_all | solution.py:389
  29.2 0.1 shard_map.86
  29.3 1.3 %collective-permute-start = (bf16[232,512]{1,0:T(8,128)(2,1)S(1)}, bf16[232,512]{1,0:T(8,128)(2,1)S(1)}, u32[]{:S(2)}, u32[]{:S(2)}) collective-permute-start(bf16[232,512]{1,0:T(8,128)(2,1)S(1)} %get-tuple-element.10.one), channel_id=1, source_target_pairs={{0,64},{64,128},{128,192},{192,0},{1,65},{65,129},{129,193},{193,1... | collective-permute-start | bytes 712712 | tf_op jit(solution)/shard_map/ppermute | solution.py:40
  30.6 1.3 %collective-permute-start.7 = (bf16[224,512]{1,0:T(8,128)(2,1)S(1)}, bf16[224,512]{1,0:T(8,128)(2,1)S(1)}, u32[]{:S(2)}, u32[]{:S(2)}) collective-permute-start(bf16[224,512]{1,0:T(8,128)(2,1)S(1)} %get-tuple-element.11.one), channel_id=1, source_target_pairs={{0,2},{2,4},{4,6},{6,0},{1,3},{3,5},{5,7},{7,1},{8,10},{10,12},{12... | collective-permute-start | bytes 688136 | tf_op jit(solution)/shard_map/ppermute | solution.py:40
  31.9 1.5 %collective-permute-start.3 = (bf16[232,512]{1,0:T(8,128)(2,1)S(1)}, bf16[232,512]{1,0:T(8,128)(2,1)S(1)}, u32[]{:S(2)}, u32[]{:S(2)}) collective-permute-start(bf16[232,512]{1,0:T(8,128)(2,1)S(1)} %get-tuple-element.10.one), channel_id=1, source_target_pairs={{0,192},{64,0},{128,64},{192,128},{1,193},{65,1},{129,65},{193,129... | collective-permute-start | bytes 712712 | tf_op jit(solution)/shard_map/ppermute | solution.py:40
  33.4 1.4 %collective-permute-start.10 = (bf16[224,512]{1,0:T(8,128)(2,1)S(1)}, bf16[224,512]{1,0:T(8,128)(2,1)S(1)}, u32[]{:S(2)}, u32[]{:S(2)}) collective-permute-start(bf16[224,512]{1,0:T(8,128)(2,1)S(1)} %get-tuple-element.11.one), channel_id=1, source_target_pairs={{0,6},{2,0},{4,2},{6,4},{1,7},{3,1},{5,3},{7,5},{8,14},{10,8},{12,... | collective-permute-start | bytes 688136 | tf_op jit(solution)/shard_map/ppermute | solution.py:40
  34.8 2.9 %collective-permute-done.two = bf16[232,512]{1,0:T(8,128)(2,1)S(1)} collective-permute-done((bf16[232,512]{1,0:T(8,128)(2,1)S(1)}, bf16[232,512]{1,0:T(8,128)(2,1)S(1)}, u32[]{:S(2)}, u32[]{:S(2)}) %collective-permute-start) | collective-permute-done | bytes 237600 | tf_op jit(solution)/shard_map/ppermute | solution.py:40
  37.7 0.0 collective-permute-start.4
  37.7 1.0 collective-permute-done.7.two
  38.7 0.4 collective-permute-start.11
  39.1 1.7 %collective-permute-done.10.one = bf16[224,512]{1,0:T(8,128)(2,1)S(1)} collective-permute-done((bf16[224,512]{1,0:T(8,128)(2,1)S(1)}, bf16[224,512]{1,0:T(8,128)(2,1)S(1)}, u32[]{:S(2)}, u32[]{:S(2)}) %collective-permute-start.10) | collective-permute-done | bytes 229408 | tf_op jit(solution)/shard_map/ppermute | solution.py:40
  40.8 1.3 %collective-permute-start.1 = (bf16[464,512]{1,0:T(8,128)(2,1)S(1)}, bf16[464,512]{1,0:T(8,128)(2,1)S(1)}, u32[]{:S(2)}, u32[]{:S(2)}) collective-permute-start(bf16[464,512]{1,0:T(8,128)(2,1)S(1)} %shard_map.87.refs_0_), channel_id=1, source_target_pairs={{0,2},{2,4},{4,6},{6,0},{1,3},{3,5},{5,7},{7,1},{8,10},{10,12},{12... | collective-permute-start | bytes 1425416 | tf_op jit(solution)/shard_map/ppermute | solution.py:40
  42.1 1.4 %collective-permute-start.15 = (bf16[464,512]{1,0:T(8,128)(2,1)S(1)}, bf16[464,512]{1,0:T(8,128)(2,1)S(1)}, u32[]{:S(2)}, u32[]{:S(2)}) collective-permute-start(bf16[464,512]{1,0:T(8,128)(2,1)S(1)} %shard_map.87.refs_0_), channel_id=1, source_target_pairs={{0,6},{2,0},{4,2},{6,4},{1,7},{3,1},{5,3},{7,5},{8,14},{10,8},{12,... | collective-permute-start | bytes 1425416 | tf_op jit(solution)/shard_map/ppermute | solution.py:40
  43.6 3.3 %collective-permute-done.11.two = bf16[224,512]{1,0:T(8,128)(2,1)S(1)} collective-permute-done((bf16[224,512]{1,0:T(8,128)(2,1)S(1)}, bf16[224,512]{1,0:T(8,128)(2,1)S(1)}, u32[]{:S(2)}, u32[]{:S(2)}) %collective-permute-start.11) | collective-permute-done | bytes 229408 | tf_op jit(solution)/shard_map/ppermute | solution.py:40
  46.9 1.2 collective-permute-start.8
  48.1 1.5 %collective-permute-start.17 = (bf16[448,512]{1,0:T(8,128)(2,1)S(1)}, bf16[448,512]{1,0:T(8,128)(2,1)}, u32[]{:S(2)}, u32[]{:S(2)}) collective-permute-start(bf16[448,512]{1,0:T(8,128)(2,1)S(1)} %shard_map.89.refs_6_), channel_id=1, source_target_pairs={{0,192},{64,0},{128,64},{192,128},{1,193},{65,1},{129,65},{193,129... | collective-permute-start | bytes 1376264 | tf_op jit(solution)/shard_map/ppermute | solution.py:40
  49.7 8.9 %collective-permute-done.8.refs_8_ = bf16[448,512]{1,0:T(8,128)(2,1)} collective-permute-done((bf16[448,512]{1,0:T(8,128)(2,1)S(1)}, bf16[448,512]{1,0:T(8,128)(2,1)}, u32[]{:S(2)}, u32[]{:S(2)}) %collective-permute-start.8) | collective-permute-done | bytes 458784 | tf_op jit(solution)/shard_map/ppermute | solution.py:40
  58.5 1.5 %collective-permute-start.12 = (bf16[448,512]{1,0:T(8,128)(2,1)S(1)}, bf16[448,512]{1,0:T(8,128)(2,1)}, u32[]{:S(2)}, u32[]{:S(2)}) collective-permute-start(bf16[448,512]{1,0:T(8,128)(2,1)S(1)} %shard_map.90.refs_7_), channel_id=1, source_target_pairs={{0,192},{64,0},{128,64},{192,128},{1,193},{65,1},{129,65},{193,129... | collective-permute-start | bytes 1376264 | tf_op jit(solution)/shard_map/ppermute | solution.py:40
  60.0 0.0 collective-permute-start.16
  60.0 1.3 %collective-permute-start.5 = (bf16[464,512]{1,0:T(8,128)(2,1)S(1)}, bf16[464,512]{1,0:T(8,128)(2,1)S(1)}, u32[]{:S(2)}, u32[]{:S(2)}) collective-permute-start(bf16[464,512]{1,0:T(8,128)(2,1)S(1)} %shard_map.88.refs_1_), channel_id=1, source_target_pairs={{0,6},{2,0},{4,2},{6,4},{1,7},{3,1},{5,3},{7,5},{8,14},{10,8},{12,... | collective-permute-start | bytes 1425416 | tf_op jit(solution)/shard_map/ppermute | solution.py:40
  61.4 0.2 collective-permute-start.14
  61.6 0.1 pad_add_fusion.at
  61.6 0.1 iota_compare_fusion.1
  61.7 6.4 %collective-permute-done.12.refs_11_ = bf16[448,512]{1,0:T(8,128)(2,1)} collective-permute-done((bf16[448,512]{1,0:T(8,128)(2,1)S(1)}, bf16[448,512]{1,0:T(8,128)(2,1)}, u32[]{:S(2)}, u32[]{:S(2)}) %collective-permute-start.12) | collective-permute-done | bytes 458784 | tf_op jit(solution)/shard_map/ppermute | solution.py:40
  68.1 0.6 collective-permute-start.9
  68.7 2.3 %collective-permute-done.16.refs_9_ = bf16[448,512]{1,0:T(8,128)(2,1)S(1)} collective-permute-done((bf16[448,512]{1,0:T(8,128)(2,1)S(1)}, bf16[448,512]{1,0:T(8,128)(2,1)S(1)}, u32[]{:S(2)}, u32[]{:S(2)}) %collective-permute-start.16) | collective-permute-done | bytes 458784 | tf_op jit(solution)/shard_map/ppermute | solution.py:40
  71.0 1.6 %collective-permute-start.13 = (bf16[448,512]{1,0:T(8,128)(2,1)}, bf16[448,512]{1,0:T(8,128)(2,1)}, u32[]{:S(2)}, u32[]{:S(2)}) collective-permute-start(bf16[448,512]{1,0:T(8,128)(2,1)} %collective-permute-done.12.refs_11_), channel_id=1, source_target_pairs={{0,192},{64,0},{128,64},{192,128},{1,193},{65,1},{129,65},{193,129... | collective-permute-start | bytes 1376264 | tf_op jit(solution)/shard_map/ppermute | solution.py:40
  72.7 0.8 copy-done.1
  73.5 2.3 %collective-permute-start.6 = (bf16[464,512]{1,0:T(8,128)(2,1)S(1)}, bf16[464,512]{1,0:T(8,128)(2,1)}, u32[]{:S(2)}, u32[]{:S(2)}) collective-permute-start(bf16[464,512]{1,0:T(8,128)(2,1)S(1)} %collective-permute-done.5.refs_5_), channel_id=1, source_target_pairs={{0,6},{2,0},{4,2},{6,4},{1,7},{3,1},{5,3},{7,5},{8,14},{10,8},{12,... | collective-permute-start | bytes 1425416 | tf_op jit(solution)/shard_map/ppermute | solution.py:40
  75.9 0.1 reshape.116
  75.9 0.1 select_reduce_fusion
  76.0 0.2 reduce_window_sum.11
  76.2 10.4 %shard_map.91 = (f32[4,2,501,224]{3,2,1,0:T(8,128)S(1)}, bf16[5,2,501,512]{3,2,1,0:T(8,128)(2,1)S(1)}) custom-call(s32[4]{0:T(128)S(1)} %pad_add_fusion.at, bf16[464,512]{1,0:T(8,128)(2,1)S(1)} %shard_map.87.refs_0_, bf16[464,512]{1,0:T(8,128)(2,1)S(1)} %shard_map.88.refs_1_, bf16[464,512]{1,0:T(8,128)(2,1)S(1)} %collective-permute-done.1.refs_2_, ...), custom_call_target="tpu_custom_call" | custom-call | tf_op jit(solution)/shard_map/pallas_call | solution.py:300
  86.6 5.6 %shard_map.92 = f32[16,8,256]{2,1,0:T(8,128)} custom-call(s32[4]{0:T(128)S(1)} %pad_add_fusion.at, bf16[464,512]{1,0:T(8,128)(2,1)S(1)} %collective-permute-done.2.refs_0_, bf16[464,512]{1,0:T(8,128)(2,1)} %collective-permute-done.6.refs_1_, bf16[448,512]{1,0:T(8,128)(2,1)} %collective-permute-done.9.refs_2_, ...), custom_call_target="tpu_custom_call" | custom-call | tf_op jit(solution)/shard_map/pallas_call | solution.py:314
  92.2 3.5 %all-to-all-start.1 = ((f32[16,8,256]{2,1,0:T(8,128)}), f32[16,8,256]{2,1,0:T(8,128)S(1)}, u32[]{:S(2)}, u32[]{:S(2)}) async-start(f32[16,8,256]{2,1,0:T(8,128)} %shard_map.92), calls=%async_computation.1 | async-start | bytes 262144 | tf_op jit(solution)/shard_map/all_to_all | solution.py:443
  95.7 0.1 slice_subtract_fusion
  95.8 0.1 broadcast_in_dim.85
  95.9 0.1 broadcast_in_dim.89
  96.0 0.1 broadcast_in_dim.91
  96.1 0.2 fusion.5
  96.3 6.1 %all-to-all-done.1.parts = f32[16,8,256]{2,1,0:T(8,128)S(1)} async-done(((f32[16,8,256]{2,1,0:T(8,128)}), f32[16,8,256]{2,1,0:T(8,128)S(1)}, u32[]{:S(2)}, u32[]{:S(2)}) %all-to-all-start.1) | async-done | bytes 131104 | tf_op jit(solution)/shard_map/all_to_all | solution.py:443
  102.3 0.7 shard_map.93
  103.1 11.4 %all-to-all-start.2 = ((f32[16,8,256]{2,1,0:T(8,128)}), f32[16,8,256]{2,1,0:T(8,128)S(1)}, u32[]{:S(2)}, u32[]{:S(2)}) async-start(f32[16,8,256]{2,1,0:T(8,128)} %shard_map.93), calls=%async_computation.2 | async-start | bytes 262144 | tf_op jit(solution)/shard_map/all_to_all | solution.py:451
  114.5 0.1 fusion.9.source
  114.6 8.8 %all-to-all-done.2.parts = f32[16,8,256]{2,1,0:T(8,128)S(1)} async-done(((f32[16,8,256]{2,1,0:T(8,128)}), f32[16,8,256]{2,1,0:T(8,128)S(1)}, u32[]{:S(2)}, u32[]{:S(2)}) %all-to-all-start.2) | async-done | bytes 131104 | tf_op jit(solution)/shard_map/all_to_all | solution.py:451
  123.3 1.4 %shard_map.94 = (f32[8,14]{1,0:T(8,128)}, f32[1,8]{1,0:T(1,128)}, f32[1,8]{1,0:T(1,128)}) custom-call(f32[16,8,256]{2,1,0:T(8,128)S(1)} %all-to-all-done.2.parts, s32[8,14]{1,0:T(8,128)S(1)} %fusion.9.source, s32[1,8]{1,0:T(1,128)S(1)} %bitcast.22, s32[1,8]{1,0:T(1,128)S(1)} %bitcast.21), custom_call_target="tpu_custom_call" | custom-call | tf_op jit(solution)/shard_map/pallas_call | solution.py:452
  (33 shorter events, 0.3 us)
Async XLA Ops:
  0.6 75.6 %collective-permute-start.18 = (bf16[4096,501]{0,1:T(8,128)(2,1)}, bf16[4096,501]{0,1:T(8,128)(2,1)}, u32[]{:S(2)}, u32[]{:S(2)}) collective-permute-start(bf16[4096,501]{0,1:T(8,128)(2,1)} %param.7), channel_id=1, source_target_pairs={{0,1},{1,0},{2,3},{3,2},{4,5},{5,4},{6,7},{7,6},{8,9},{9,8},{10,11... | collective-permute-start | bytes 12312584 | tf_op jit(solution)/shard_map/ppermute | solution.py:40
  29.3 8.4 %collective-permute-start = (bf16[232,512]{1,0:T(8,128)(2,1)S(1)}, bf16[232,512]{1,0:T(8,128)(2,1)S(1)}, u32[]{:S(2)}, u32[]{:S(2)}) collective-permute-start(bf16[232,512]{1,0:T(8,128)(2,1)S(1)} %get-tuple-element.10.one), channel_id=1, source_target_pairs={{0,64},{64,128},{128,192},{192,0},{1,65},{65,129},{129,193},{193,1... | collective-permute-start | bytes 712712 | tf_op jit(solution)/shard_map/ppermute | solution.py:40
  30.6 8.1 %collective-permute-start.7 = (bf16[224,512]{1,0:T(8,128)(2,1)S(1)}, bf16[224,512]{1,0:T(8,128)(2,1)S(1)}, u32[]{:S(2)}, u32[]{:S(2)}) collective-permute-start(bf16[224,512]{1,0:T(8,128)(2,1)S(1)} %get-tuple-element.11.one), channel_id=1, source_target_pairs={{0,2},{2,4},{4,6},{6,0},{1,3},{3,5},{5,7},{7,1},{8,10},{10,12},{12... | collective-permute-start | bytes 688136 | tf_op jit(solution)/shard_map/ppermute | solution.py:40
  31.9 10.3 %collective-permute-start.3 = (bf16[232,512]{1,0:T(8,128)(2,1)S(1)}, bf16[232,512]{1,0:T(8,128)(2,1)S(1)}, u32[]{:S(2)}, u32[]{:S(2)}) collective-permute-start(bf16[232,512]{1,0:T(8,128)(2,1)S(1)} %get-tuple-element.10.one), channel_id=1, source_target_pairs={{0,192},{64,0},{128,64},{192,128},{1,193},{65,1},{129,65},{193,129... | collective-permute-start | bytes 712712 | tf_op jit(solution)/shard_map/ppermute | solution.py:40
  33.4 7.5 %collective-permute-start.10 = (bf16[224,512]{1,0:T(8,128)(2,1)S(1)}, bf16[224,512]{1,0:T(8,128)(2,1)S(1)}, u32[]{:S(2)}, u32[]{:S(2)}) collective-permute-start(bf16[224,512]{1,0:T(8,128)(2,1)S(1)} %get-tuple-element.11.one), channel_id=1, source_target_pairs={{0,6},{2,0},{4,2},{6,4},{1,7},{3,1},{5,3},{7,5},{8,14},{10,8},{12,... | collective-permute-start | bytes 688136 | tf_op jit(solution)/shard_map/ppermute | solution.py:40
  37.7 10.4 %collective-permute-start.4 = (bf16[232,512]{1,0:T(8,128)(2,1)S(1)}, bf16[232,512]{1,0:T(8,128)(2,1)S(1)}, u32[]{:S(2)}, u32[]{:S(2)}) collective-permute-start(bf16[232,512]{1,0:T(8,128)(2,1)S(1)} %collective-permute-done.two), channel_id=1, source_target_pairs={{0,64},{64,128},{128,192},{192,0},{1,65},{65,129},{129,193},{193,1... | collective-permute-start | bytes 712712 | tf_op jit(solution)/shard_map/ppermute | solution.py:40
  38.7 8.2 %collective-permute-start.11 = (bf16[224,512]{1,0:T(8,128)(2,1)S(1)}, bf16[224,512]{1,0:T(8,128)(2,1)S(1)}, u32[]{:S(2)}, u32[]{:S(2)}) collective-permute-start(bf16[224,512]{1,0:T(8,128)(2,1)S(1)} %collective-permute-done.7.two), channel_id=1, source_target_pairs={{0,2},{2,4},{4,6},{6,0},{1,3},{3,5},{5,7},{7,1},{8,10},{10,12},{12... | collective-permute-start | bytes 688136 | tf_op jit(solution)/shard_map/ppermute | solution.py:40
  40.8 19.2 %collective-permute-start.1 = (bf16[464,512]{1,0:T(8,128)(2,1)S(1)}, bf16[464,512]{1,0:T(8,128)(2,1)S(1)}, u32[]{:S(2)}, u32[]{:S(2)}) collective-permute-start(bf16[464,512]{1,0:T(8,128)(2,1)S(1)} %shard_map.87.refs_0_), channel_id=1, source_target_pairs={{0,2},{2,4},{4,6},{6,0},{1,3},{3,5},{5,7},{7,1},{8,10},{10,12},{12... | collective-permute-start | bytes 1425416 | tf_op jit(solution)/shard_map/ppermute | solution.py:40
  42.1 19.2 %collective-permute-start.15 = (bf16[464,512]{1,0:T(8,128)(2,1)S(1)}, bf16[464,512]{1,0:T(8,128)(2,1)S(1)}, u32[]{:S(2)}, u32[]{:S(2)}) collective-permute-start(bf16[464,512]{1,0:T(8,128)(2,1)S(1)} %shard_map.87.refs_0_), channel_id=1, source_target_pairs={{0,6},{2,0},{4,2},{6,4},{1,7},{3,1},{5,3},{7,5},{8,14},{10,8},{12,... | collective-permute-start | bytes 1425416 | tf_op jit(solution)/shard_map/ppermute | solution.py:40
  46.9 11.7 %collective-permute-start.8 = (bf16[448,512]{1,0:T(8,128)(2,1)S(1)}, bf16[448,512]{1,0:T(8,128)(2,1)}, u32[]{:S(2)}, u32[]{:S(2)}) collective-permute-start(bf16[448,512]{1,0:T(8,128)(2,1)S(1)} %shard_map.89.refs_6_), channel_id=1, source_target_pairs={{0,64},{64,128},{128,192},{192,0},{1,65},{65,129},{129,193},{193,1... | collective-permute-start | bytes 1376264 | tf_op jit(solution)/shard_map/ppermute | solution.py:40
  48.1 11.9 %collective-permute-start.17 = (bf16[448,512]{1,0:T(8,128)(2,1)S(1)}, bf16[448,512]{1,0:T(8,128)(2,1)}, u32[]{:S(2)}, u32[]{:S(2)}) collective-permute-start(bf16[448,512]{1,0:T(8,128)(2,1)S(1)} %shard_map.89.refs_6_), channel_id=1, source_target_pairs={{0,192},{64,0},{128,64},{192,128},{1,193},{65,1},{129,65},{193,129... | collective-permute-start | bytes 1376264 | tf_op jit(solution)/shard_map/ppermute | solution.py:40
  58.5 9.6 %collective-permute-start.12 = (bf16[448,512]{1,0:T(8,128)(2,1)S(1)}, bf16[448,512]{1,0:T(8,128)(2,1)}, u32[]{:S(2)}, u32[]{:S(2)}) collective-permute-start(bf16[448,512]{1,0:T(8,128)(2,1)S(1)} %shard_map.90.refs_7_), channel_id=1, source_target_pairs={{0,192},{64,0},{128,64},{192,128},{1,193},{65,1},{129,65},{193,129... | collective-permute-start | bytes 1376264 | tf_op jit(solution)/shard_map/ppermute | solution.py:40
  60.0 11.0 %collective-permute-start.16 = (bf16[448,512]{1,0:T(8,128)(2,1)S(1)}, bf16[448,512]{1,0:T(8,128)(2,1)S(1)}, u32[]{:S(2)}, u32[]{:S(2)}) collective-permute-start(bf16[448,512]{1,0:T(8,128)(2,1)S(1)} %shard_map.90.refs_7_), channel_id=1, source_target_pairs={{0,64},{64,128},{128,192},{192,0},{1,65},{65,129},{129,193},{193,1... | collective-permute-start | bytes 1376264 | tf_op jit(solution)/shard_map/ppermute | solution.py:40
  60.0 11.0 %collective-permute-start.5 = (bf16[464,512]{1,0:T(8,128)(2,1)S(1)}, bf16[464,512]{1,0:T(8,128)(2,1)S(1)}, u32[]{:S(2)}, u32[]{:S(2)}) collective-permute-start(bf16[464,512]{1,0:T(8,128)(2,1)S(1)} %shard_map.88.refs_1_), channel_id=1, source_target_pairs={{0,6},{2,0},{4,2},{6,4},{1,7},{3,1},{5,3},{7,5},{8,14},{10,8},{12,... | collective-permute-start | bytes 1425416 | tf_op jit(solution)/shard_map/ppermute | solution.py:40
  61.4 7.4 %copy-start = (bf16[464,512]{1,0:T(8,128)(2,1)}, bf16[464,512]{1,0:T(8,128)(2,1)S(1)}, u32[]{:S(2)}) copy-start(bf16[464,512]{1,0:T(8,128)(2,1)S(1)} %collective-permute-done.15.refs_4_) | copy-start | bytes 1425412
  61.4 11.3 %collective-permute-start.14 = (bf16[464,512]{1,0:T(8,128)(2,1)S(1)}, bf16[464,512]{1,0:T(8,128)(2,1)S(1)}, u32[]{:S(2)}, u32[]{:S(2)}) collective-permute-start(bf16[464,512]{1,0:T(8,128)(2,1)S(1)} %shard_map.88.refs_1_), channel_id=1, source_target_pairs={{0,2},{2,4},{4,6},{6,0},{1,3},{3,5},{5,7},{7,1},{8,10},{10,12},{12... | collective-permute-start | bytes 1425416 | tf_op jit(solution)/shard_map/ppermute | solution.py:40
  68.1 18.4 %collective-permute-start.9 = (bf16[448,512]{1,0:T(8,128)(2,1)}, bf16[448,512]{1,0:T(8,128)(2,1)}, u32[]{:S(2)}, u32[]{:S(2)}) collective-permute-start(bf16[448,512]{1,0:T(8,128)(2,1)} %collective-permute-done.8.refs_8_), channel_id=1, source_target_pairs={{0,64},{64,128},{128,192},{192,0},{1,65},{65,129},{129,193},{193,1... | collective-permute-start | bytes 1376264 | tf_op jit(solution)/shard_map/ppermute | solution.py:40
  71.0 4.8 %copy-start.2 = (bf16[448,512]{1,0:T(8,128)(2,1)}, bf16[448,512]{1,0:T(8,128)(2,1)S(1)}, u32[]{:S(2)}) copy-start(bf16[448,512]{1,0:T(8,128)(2,1)S(1)} %collective-permute-done.16.refs_9_) | copy-start | bytes 1376260
  71.0 15.6 %collective-permute-start.2 = (bf16[464,512]{1,0:T(8,128)(2,1)S(1)}, bf16[464,512]{1,0:T(8,128)(2,1)S(1)}, u32[]{:S(2)}, u32[]{:S(2)}) collective-permute-start(bf16[464,512]{1,0:T(8,128)(2,1)S(1)} %collective-permute-done.1.refs_2_), channel_id=1, source_target_pairs={{0,2},{2,4},{4,6},{6,0},{1,3},{3,5},{5,7},{7,1},{8,10},{10,12},{12... | collective-permute-start | bytes 1425416 | tf_op jit(solution)/shard_map/ppermute | solution.py:40
  71.0 15.6 %collective-permute-start.13 = (bf16[448,512]{1,0:T(8,128)(2,1)}, bf16[448,512]{1,0:T(8,128)(2,1)}, u32[]{:S(2)}, u32[]{:S(2)}) collective-permute-start(bf16[448,512]{1,0:T(8,128)(2,1)} %collective-permute-done.12.refs_11_), channel_id=1, source_target_pairs={{0,192},{64,0},{128,64},{192,128},{1,193},{65,1},{129,65},{193,129... | collective-permute-start | bytes 1376264 | tf_op jit(solution)/shard_map/ppermute | solution.py:40
  72.7 0.8 copy-start.1
  73.5 13.1 %collective-permute-start.6 = (bf16[464,512]{1,0:T(8,128)(2,1)S(1)}, bf16[464,512]{1,0:T(8,128)(2,1)}, u32[]{:S(2)}, u32[]{:S(2)}) collective-permute-start(bf16[464,512]{1,0:T(8,128)(2,1)S(1)} %collective-permute-done.5.refs_5_), channel_id=1, source_target_pairs={{0,6},{2,0},{4,2},{6,4},{1,7},{3,1},{5,3},{7,5},{8,14},{10,8},{12,... | collective-permute-start | bytes 1425416 | tf_op jit(solution)/shard_map/ppermute | solution.py:40
  86.6 9.4 %copy-start.3 = (s32[256]{0:T(256)S(1)}, s32[256]{0:T(256)}, u32[]{:S(2)}) copy-start(s32[256]{0:T(256)} %param.11) | copy-start | bytes 3076
  92.2 10.1 %all-to-all-start.1 = ((f32[16,8,256]{2,1,0:T(8,128)}), f32[16,8,256]{2,1,0:T(8,128)S(1)}, u32[]{:S(2)}, u32[]{:S(2)}) async-start(f32[16,8,256]{2,1,0:T(8,128)} %shard_map.92), calls=%async_computation.1 | async-start | bytes 262144 | tf_op jit(solution)/shard_map/all_to_all | solution.py:443
  103.1 20.3 %all-to-all-start.2 = ((f32[16,8,256]{2,1,0:T(8,128)}), f32[16,8,256]{2,1,0:T(8,128)S(1)}, u32[]{:S(2)}, u32[]{:S(2)}) async-start(f32[16,8,256]{2,1,0:T(8,128)} %shard_map.93), calls=%async_computation.2 | async-start | bytes 262144 | tf_op jit(solution)/shard_map/all_to_all | solution.py:451

commit v4 on v3

--- a/solution.py
+++ b/solution.py
@@ -112,14 +112,14 @@
 
 
 def join_kernel(one, two, out):
-    out[: one.shape[0]] = one[...]
-    out[one.shape[0] :] = two[...]
+    out[:ROWS] = one[:ROWS]
+    out[ROWS:] = two[:ROWS]
 
 
 def join(one, two):
     return pl.pallas_call(
         join_kernel,
-        out_shape=jax.ShapeDtypeStruct((one.shape[0] + two.shape[0], one.shape[1]), BF16),
+        out_shape=jax.ShapeDtypeStruct((2 * ROWS, WIDTH), BF16),
         in_specs=[VMEM, VMEM],
         out_specs=VMEM,
         compiler_params=params(),
@@ -144,7 +144,7 @@
         far2 = shift(down2, lasts[k], -1)
         far1 = shift(up1, lasts[k], 1)
         planes.append(((one[k], two[k]), (up1, up2), (down1, down2), (far1, far2)))
-    return planes
+    return planes, (own[0], up[0], down[0], far[0])
 
 
 def product(w, block):
@@ -184,16 +184,16 @@
 def plan_of(which):
     plan = []
     for i in [i for i in range(NX) if i not in which] + list(which):
-        terms = [((j, 0), (0, j, i // 2), i % 2 * TALL) for j in which]
+        terms = [((j, 0), (0, j, i // 2), i % 2 * ROWS) for j in which]
         if i in which:
             terms += [((j, 1), (1, i, j // 2), j % 2 * ROWS) for j in range(NY)]
         plan.append((i, terms))
     return plan
 
 
-NEAR, FAR = (0, 1, 2), (3,)
-KEPT = tuple((j, 1) for j in range(NY)) + ((3, 0),)
-NEAR_LATE = [n for n in names_of(NEAR) if n[1] and n[1] - 1 != n[2]]
+LOCAL, NEAR, FAR = (0,), (1, 2), (3,)
+KEPT = tuple((j, 1) for j in range(NY)) + tuple((j, 0) for j in NEAR + FAR)
+NEAR_LATE = [n for n in names_of(NEAR) if n[1] - 1 != n[2] or n == (1, 2, 1)]
 
 
 def piece_copies(arrivals, name, pieces, late, held_p, sems):
@@ -205,18 +205,15 @@
     return held_p.at[n]
 
 
-def near_kernel(at, *refs):
-    pieces = dict(zip(names_of(NEAR), refs))
+def local_kernel(at, *refs):
+    pieces = dict(zip(names_of(LOCAL), refs))
     weights, rest = refs[len(pieces) : len(pieces) + 2], refs[len(pieces) + 2 :]
-    acc, kept, held_p, held_w, sems, sems_w = rest
-    arrivals, views, slices = Arrivals(), {}, {}
+    acc, kept, held_w, sems_w = rest
+    arrivals, slices = Arrivals(), {}
 
     def slice_copies(key):
         j, colour = key
-        if key in KEPT:
-            slices[key] = kept.at[KEPT.index(key)]
-        else:
-            slices[key] = held_w.at[j]
+        slices[key] = kept.at[KEPT.index(key)] if key in KEPT else held_w
         column = ((at[0] + OFFSETS[j] + NY) % NY * NC + colour) * WIDTH
         column = pl.multiple_of(column, WIDTH)
         arrivals.add(
@@ -229,38 +226,55 @@
             ),
         )
 
-    plan = plan_of(NEAR)
+    plan = plan_of(LOCAL)
     for _, terms in plan:
-        for key, name, _ in terms:
+        for key, _, _ in terms:
             if key not in slices:
                 slice_copies(key)
-            if name not in views:
-                views[name] = piece_copies(arrivals, name, pieces, NEAR_LATE, held_p, sems)
-    slice_copies((3, 0))
+    for key in KEPT:
+        if key not in slices:
+            slice_copies(key)
     arrivals.begin(LOOK)
     for i, terms in plan:
         total = [None, None]
         for key, name, lo in terms:
             arrivals.wait(key)
-            arrivals.wait(name)
             for w in range(2):
-                term = product(slices[key].at[w], views[name][lo : lo + ROWS, :])
+                term = product(slices[key].at[w], pieces[name][lo : lo + ROWS, :])
                 total[w] = term if total[w] is None else total[w] + term
         for w in range(2):
             acc[i, w] = total[w]
-    arrivals.wait((3, 0))
+    for key in KEPT:
+        arrivals.wait(key)
+
+
+def add_terms(which, before, kept, views, acc, ready):
+    for i, terms in plan_of(which):
+        total = [before[i, w] for w in range(2)]
+        for key, name, lo in terms:
+            ready(name)
+            for w in range(2):
+                total[w] = total[w] + product(kept.at[KEPT.index(key), w], views[name][lo : lo + ROWS, :])
+        for w in range(2):
+            acc[i, w] = total[w]
+
+
+def near_kernel(*refs):
+    pieces = dict(zip(names_of(NEAR), refs))
+    before, kept, acc, held_p, sems = refs[len(pieces) :]
+    arrivals, views = Arrivals(), {}
+    for _, terms in plan_of(NEAR):
+        for _, name, _ in terms:
+            if name not in views:
+                views[name] = piece_copies(arrivals, name, pieces, NEAR_LATE, held_p, sems)
+    arrivals.begin(LOOK)
+    add_terms(NEAR, before, kept, views, acc, arrivals.wait)
 
 
 def far_kernel(at, *refs):
     pieces = dict(zip(names_of(FAR), refs))
     before, kept, ids, out, acc, held = refs[len(pieces) :]
-    for i, terms in plan_of(FAR):
-        total = [before[i, w] for w in range(2)]
-        for key, name, lo in terms:
-            for w in range(2):
-                total[w] = total[w] + product(kept.at[KEPT.index(key), w], pieces[name][lo : lo + ROWS, :])
-        for w in range(2):
-            acc[i, w] = total[w]
+    add_terms(FAR, before, kept, pieces, acc, lambda name: None)
     statistics(at, ids, acc, out, held)
 
 
@@ -296,20 +310,28 @@
             specs.append(HBM if name in late else VMEM)
         return parts, specs
 
-    parts, specs = operands(NEAR, NEAR_LATE)
+    parts, specs = operands(LOCAL)
     sums, slices = pl.pallas_call(
-        near_kernel,
+        local_kernel,
         out_shape=[acc, kept],
         in_specs=[SMEM] + specs + [HBM] * 2,
         out_specs=[VMEM, VMEM],
+        scratch_shapes=[pltpu.VMEM((2, SHARD, WIDTH), BF16), pltpu.SemaphoreType.DMA((NY, NC, 2))],
+        compiler_params=params(20),
+    )(at, *parts, *weights)
+    parts, specs = operands(NEAR, NEAR_LATE)
+    sums = pl.pallas_call(
+        near_kernel,
+        out_shape=acc,
+        in_specs=specs + [VMEM] * 2,
+        out_specs=VMEM,
         scratch_shapes=[
-            pltpu.VMEM((len(NEAR_LATE), 2 * TALL, WIDTH), BF16),
-            pltpu.VMEM((len(NEAR), 2, SHARD, WIDTH), BF16),
+            pltpu.VMEM((len(NEAR_LATE), 2 * ROWS, WIDTH), BF16),
             pltpu.SemaphoreType.DMA((len(NEAR_LATE),)),
-            pltpu.SemaphoreType.DMA((NY, NC, 2)),
         ],
-        compiler_params=params(24),
-    )(at, *parts, *weights)
+        input_output_aliases={len(parts): 0},
+        compiler_params=params(20),
+    )(*parts, sums, slices)
     parts, specs = operands(FAR)
     return pl.pallas_call(
         far_kernel,
@@ -397,10 +419,8 @@
         out_specs=[VMEM, VMEM],
         compiler_params=params(),
     )(got)
-    planes = gathered_planes((own0, own1), ("x", "y"), ("y", "x"))
-    line0 = planes[0][0]
-
-    metas = jnp.stack([line0[i // 2][i % 2 * TALL + ROWS : i % 2 * TALL + TALL] for i in range(NX)])
+    planes, line0 = gathered_planes((own0, own1), ("x", "y"), ("y", "x"))
+    metas = jnp.stack([block[ROWS:] for block in line0])
     whole = metas.astype(F32).astype(jnp.int32)
     ids = whole[:, :, :HALF] + 256 * whole[:, :, 128 : 128 + HALF] + 65536 * whole[:, :, 256 : 256 + HALF]
     ids = jnp.pad(ids.reshape(NX, ROWS), ((0, 4), (0, 0)), constant_values=-1)

time: 125 us -> 129 us (1.032)
  waiting for transfers between devices: 41.4 us -> 46.2 us
  starting transfers between devices: 37 us -> 33.1 us
  local copies, waits for them, and re-layouts: 1.17 us -> 3.41 us
    ppermute x19, waiting for transfers between devices: 26.5 us -> 31.1 us  [shift(): lax.ppermute(value, axis, [(i, (i + by) % size) for i in range(size)])]
    all_to_all x1, starting transfers between devices: 11.4 us -> 7.35 us  [local(): stats = lax.all_to_all(stats, ('z', 'c'), 0, 0, tiled=True)]
    another operation x2 -> x4, local copies, waits for them, and re-layouts: 0.01 us -> 1.4 us  [local(): metas = jnp.stack([block[ROWS:] for block in line0])]
    pallas_call x5 -> x6, Pallas kernels: 10.5 us -> 11.2 us  [the longest x1 5.92 us: head(): pl.pallas_call(near_kernel, out_shape=acc, in_specs=specs + [VMEM] * 2, o...]
  transfers between devices with their start and end apart: 21 -> 21, of which waited for: 9 -> 9; matrix products, arithmetic and copies ran while one was open for 1% -> 2% of each run, Pallas kernels for 10% -> 10%
where the time goes in v4:
time: 129 us
  waiting for transfers between devices  46.2 us (36%)
  starting transfers between devices  33.1 us (26%)
  blocking collectives  23.9 us (19%)
  Pallas kernels  20.4 us (16%)
  local copies, waits for them, and re-layouts  3.41 us (3%)
    ppermute x19, waiting for transfers between devices, shift(): lax.ppermute(value, axis, [(i, (i + by) % size) for i in range(size)])  31.1 us
    all_to_all x1, blocking collectives, local(): got = lax.all_to_all(sent, ('z', 'c'), 0, 0, tiled=True)  23.9 us
    ppermute x19, starting transfers between devices, shift(): lax.ppermute(value, axis, [(i, (i + by) % size) for i in range(size)])  22.2 us
    all_to_all x1, waiting for transfers between devices, local(): stats = lax.all_to_all(stats, ('z', 'c'), 0, 0, tiled=True)  9.08 us
    all_to_all x1, starting transfers between devices, local(): stats = lax.all_to_all(stats, ('z', 'c'), 0, 0, tiled=True)  7.35 us
    all_to_all x1, waiting for transfers between devices, local(): stats = lax.all_to_all(partial, ('x', 'y'), 0, 0, tiled=True)  6.06 us
    pallas_call x1, Pallas kernels, head(): pl.pallas_call(near_kernel, out_shape=acc, in_specs=specs + [VMEM] * 2, o...  5.92 us
    pallas_call x1, Pallas kernels, head(): pl.pallas_call(far_kernel, out_shape=jax.ShapeDtypeStruct((NX * NY, 8, 25...  5.57 us
  transfers between devices with their start and end apart: 21, of which 9 were waited for; matrix products, arithmetic and copies ran while one was open for 2% of the time, Pallas kernels for 10%

profile of v4, /device:TPU:1, one launch (start us, length us, event | category | flops | bytes accessed | tf_op | source)
XLA Modules:
  0.0 128.7 jit_solution(4704033792605164013)
XLA Ops:
  0.6 3.3 %collective-permute-start.18 = (bf16[4096,501]{0,1:T(8,128)(2,1)}, bf16[4096,501]{0,1:T(8,128)(2,1)}, u32[]{:S(2)}, u32[]{:S(2)}) collective-permute-start(bf16[4096,501]{0,1:T(8,128)(2,1)} %param.7), channel_id=1, source_target_pairs={{0,1},{1,0},{2,3},{3,2},{4,5},{5,4},{6,7},{7,6},{8,9},{9,8},{10,11... | collective-permute-start | bytes 12312584 | tf_op jit(solution)/shard_map/ppermute | solution.py:40
  3.9 1.4 %shard_map.85 = bf16[16,32,512]{2,1,0:T(8,128)(2,1)S(1)} custom-call(bf16[14,8,512]{2,1,0:T(8,128)(2,1)} %bitcast.27, s32[8,14]{1,0:T(8,128)} %targets_hbm.1, s32[1,8]{1,0:T(1,128)} %lengths_hbm.1, s32[1,8]{1,0:T(1,128)} %rewards_hbm.1), custom_call_target="tpu_custom_call" | custom-call | tf_op jit(solution)/shard_map/pallas_call | solution.py:397
  5.4 23.9 %all_to_all.15.got = bf16[16,32,512]{2,1,0:T(8,128)(2,1)S(1)} all-to-all(bf16[16,32,512]{2,1,0:T(8,128)(2,1)S(1)} %shard_map.85), channel_id=1, replica_groups=mesh['x'=4,'z'=8,'y'=4,'c'=2] {'z','c'}, dimensions={0} | all-to-all | bytes 1048576 | tf_op jit(solution)/shard_map/all_to_all | solution.py:411
  29.2 0.1 shard_map.86
  29.3 1.3 %collective-permute-start = (bf16[232,512]{1,0:T(8,128)(2,1)S(1)}, bf16[232,512]{1,0:T(8,128)(2,1)S(1)}, u32[]{:S(2)}, u32[]{:S(2)}) collective-permute-start(bf16[232,512]{1,0:T(8,128)(2,1)S(1)} %get-tuple-element.10.one), channel_id=1, source_target_pairs={{0,64},{64,128},{128,192},{192,0},{1,65},{65,129},{129,193},{193,1... | collective-permute-start | bytes 712712 | tf_op jit(solution)/shard_map/ppermute | solution.py:40
  30.6 1.5 %collective-permute-start.3 = (bf16[232,512]{1,0:T(8,128)(2,1)S(1)}, bf16[232,512]{1,0:T(8,128)(2,1)S(1)}, u32[]{:S(2)}, u32[]{:S(2)}) collective-permute-start(bf16[232,512]{1,0:T(8,128)(2,1)S(1)} %get-tuple-element.10.one), channel_id=1, source_target_pairs={{0,192},{64,0},{128,64},{192,128},{1,193},{65,1},{129,65},{193,129... | collective-permute-start | bytes 712712 | tf_op jit(solution)/shard_map/ppermute | solution.py:40
  32.1 1.3 %collective-permute-start.7 = (bf16[224,512]{1,0:T(8,128)(2,1)S(1)}, bf16[224,512]{1,0:T(8,128)(2,1)S(1)}, u32[]{:S(2)}, u32[]{:S(2)}) collective-permute-start(bf16[224,512]{1,0:T(8,128)(2,1)S(1)} %get-tuple-element.11.one), channel_id=1, source_target_pairs={{0,2},{2,4},{4,6},{6,0},{1,3},{3,5},{5,7},{7,1},{8,10},{10,12},{12... | collective-permute-start | bytes 688136 | tf_op jit(solution)/shard_map/ppermute | solution.py:40
  33.4 1.4 %collective-permute-start.10 = (bf16[224,512]{1,0:T(8,128)(2,1)S(1)}, bf16[224,512]{1,0:T(8,128)(2,1)S(1)}, u32[]{:S(2)}, u32[]{:S(2)}) collective-permute-start(bf16[224,512]{1,0:T(8,128)(2,1)S(1)} %get-tuple-element.11.one), channel_id=1, source_target_pairs={{0,6},{2,0},{4,2},{6,4},{1,7},{3,1},{5,3},{7,5},{8,14},{10,8},{12,... | collective-permute-start | bytes 688136 | tf_op jit(solution)/shard_map/ppermute | solution.py:40
  34.8 5.7 %collective-permute-done.7.two = bf16[224,512]{1,0:T(8,128)(2,1)S(1)} collective-permute-done((bf16[224,512]{1,0:T(8,128)(2,1)S(1)}, bf16[224,512]{1,0:T(8,128)(2,1)S(1)}, u32[]{:S(2)}, u32[]{:S(2)}) %collective-permute-start.7) | collective-permute-done | bytes 229408 | tf_op jit(solution)/shard_map/ppermute | solution.py:40
  40.5 0.3 collective-permute-start.11
  40.9 0.1 collective-permute-start.8
  41.0 2.7 %collective-permute-start.17 = (bf16[448,512]{1,0:T(8,128)(2,1)S(1)}, bf16[448,512]{1,0:T(8,128)(2,1)}, u32[]{:S(2)}, u32[]{:S(2)}) collective-permute-start(bf16[448,512]{1,0:T(8,128)(2,1)S(1)} %shard_map.89.refs_2_), channel_id=1, source_target_pairs={{0,192},{64,0},{128,64},{192,128},{1,193},{65,1},{129,65},{193,129... | collective-permute-start | bytes 1376264 | tf_op jit(solution)/shard_map/ppermute | solution.py:40
  43.8 0.7 copy-done.1
  44.5 1.3 %collective-permute-start.1 = (bf16[448,512]{1,0:T(8,128)(2,1)S(1)}, bf16[448,512]{1,0:T(8,128)(2,1)S(1)}, u32[]{:S(2)}, u32[]{:S(2)}) collective-permute-start(bf16[448,512]{1,0:T(8,128)(2,1)S(1)} %shard_map.87.refs_0_), channel_id=1, source_target_pairs={{0,2},{2,4},{4,6},{6,0},{1,3},{3,5},{5,7},{7,1},{8,10},{10,12},{12... | collective-permute-start | bytes 1376264 | tf_op jit(solution)/shard_map/ppermute | solution.py:40
  45.8 2.7 %collective-permute-done.11.two = bf16[224,512]{1,0:T(8,128)(2,1)S(1)} collective-permute-done((bf16[224,512]{1,0:T(8,128)(2,1)S(1)}, bf16[224,512]{1,0:T(8,128)(2,1)S(1)}, u32[]{:S(2)}, u32[]{:S(2)}) %collective-permute-start.11) | collective-permute-done | bytes 229408 | tf_op jit(solution)/shard_map/ppermute | solution.py:40
  48.5 0.1 pad_add_fusion.at
  48.7 10.1 %collective-permute-done.4.two = bf16[232,512]{1,0:T(8,128)(2,1)S(1)} collective-permute-done((bf16[232,512]{1,0:T(8,128)(2,1)S(1)}, bf16[232,512]{1,0:T(8,128)(2,1)S(1)}, u32[]{:S(2)}, u32[]{:S(2)}) %collective-permute-start.4) | collective-permute-done | bytes 237600 | tf_op jit(solution)/shard_map/ppermute | solution.py:40
  58.8 2.2 %collective-permute-start.15 = (bf16[448,512]{1,0:T(8,128)(2,1)S(1)}, bf16[448,512]{1,0:T(8,128)(2,1)S(1)}, u32[]{:S(2)}, u32[]{:S(2)}) collective-permute-start(bf16[448,512]{1,0:T(8,128)(2,1)S(1)} %shard_map.87.refs_0_), channel_id=1, source_target_pairs={{0,6},{2,0},{4,2},{6,4},{1,7},{3,1},{5,3},{7,5},{8,14},{10,8},{12,... | collective-permute-start | bytes 1376264 | tf_op jit(solution)/shard_map/ppermute | solution.py:40
  61.1 0.9 copy-done.2
  62.0 0.1 collective-permute-start.12
  62.2 1.4 %collective-permute-start.16 = (bf16[448,512]{1,0:T(8,128)(2,1)S(1)}, bf16[448,512]{1,0:T(8,128)(2,1)S(1)}, u32[]{:S(2)}, u32[]{:S(2)}) collective-permute-start(bf16[448,512]{1,0:T(8,128)(2,1)S(1)} %shard_map.90.refs_3_), channel_id=1, source_target_pairs={{0,64},{64,128},{128,192},{192,0},{1,65},{65,129},{129,193},{193,1... | collective-permute-start | bytes 1376264 | tf_op jit(solution)/shard_map/ppermute | solution.py:40
  63.6 0.7 collective-permute-start.5
  64.3 0.7 slice_bitcast_fusion.2
  65.0 0.7 slice_bitcast_fusion.1
  65.7 4.0 %collective-permute-done.15.refs_2_ = bf16[448,512]{1,0:T(8,128)(2,1)S(1)} collective-permute-done((bf16[448,512]{1,0:T(8,128)(2,1)S(1)}, bf16[448,512]{1,0:T(8,128)(2,1)S(1)}, u32[]{:S(2)}, u32[]{:S(2)}) %collective-permute-start.15) | collective-permute-done | bytes 458784 | tf_op jit(solution)/shard_map/ppermute | solution.py:40
  69.6 1.3 %collective-permute-start.14 = (bf16[448,512]{1,0:T(8,128)(2,1)S(1)}, bf16[448,512]{1,0:T(8,128)(2,1)}, u32[]{:S(2)}, u32[]{:S(2)}) collective-permute-start(bf16[448,512]{1,0:T(8,128)(2,1)S(1)} %shard_map.88.refs_1_), channel_id=1, source_target_pairs={{0,2},{2,4},{4,6},{6,0},{1,3},{3,5},{5,7},{7,1},{8,10},{10,12},{12... | collective-permute-start | bytes 1376264 | tf_op jit(solution)/shard_map/ppermute | solution.py:40
  70.9 1.6 %collective-permute-done.12.refs_7_ = bf16[448,512]{1,0:T(8,128)(2,1)} collective-permute-done((bf16[448,512]{1,0:T(8,128)(2,1)S(1)}, bf16[448,512]{1,0:T(8,128)(2,1)}, u32[]{:S(2)}, u32[]{:S(2)}) %collective-permute-start.12) | collective-permute-done | bytes 458784 | tf_op jit(solution)/shard_map/ppermute | solution.py:40
  72.5 1.0 collective-permute-done.16.refs_5_
  73.5 6.0 %collective-permute-done.5.refs_3_ = bf16[448,512]{1,0:T(8,128)(2,1)S(1)} collective-permute-done((bf16[448,512]{1,0:T(8,128)(2,1)S(1)}, bf16[448,512]{1,0:T(8,128)(2,1)S(1)}, u32[]{:S(2)}, u32[]{:S(2)}) %collective-permute-start.5) | collective-permute-done | bytes 458784 | tf_op jit(solution)/shard_map/ppermute | solution.py:40
  79.5 3.2 %collective-permute-start.6 = (bf16[448,512]{1,0:T(8,128)(2,1)S(1)}, bf16[448,512]{1,0:T(8,128)(2,1)}, u32[]{:S(2)}, u32[]{:S(2)}) collective-permute-start(bf16[448,512]{1,0:T(8,128)(2,1)S(1)} %collective-permute-done.5.refs_3_), channel_id=1, source_target_pairs={{0,6},{2,0},{4,2},{6,4},{1,7},{3,1},{5,3},{7,5},{8,14},{10,8},{12,... | collective-permute-start | bytes 1376264 | tf_op jit(solution)/shard_map/ppermute | solution.py:40
  82.8 0.1 reshape.116
  82.9 0.1 select_reduce_fusion
  83.0 0.2 reduce_window_sum.11
  83.2 5.1 %shard_map.91 = (f32[4,2,501,224]{3,2,1,0:T(8,128)S(1)}, bf16[7,2,501,512]{3,2,1,0:T(8,128)(2,1)S(1)}) custom-call(s32[4]{0:T(128)S(1)} %pad_add_fusion.at, bf16[448,512]{1,0:T(8,128)(2,1)S(1)} %shard_map.87.refs_0_, bf16[448,512]{1,0:T(8,128)(2,1)S(1)} %shard_map.88.refs_1_, bf16[448,512]{1,0:T(8,128)(2,1)S(1)} %shard_map.89.refs_2_, ...), custom_call_target="tpu_custom_call" | custom-call | tf_op jit(solution)/shard_map/pallas_call | solution.py:314
  88.3 5.9 %shard_map.92.refs_4_ = f32[4,2,501,224]{3,2,1,0:T(8,128)S(1)} custom-call(bf16[448,512]{1,0:T(8,128)(2,1)S(1)} %collective-permute-done.1.refs_0_, bf16[448,512]{1,0:T(8,128)(2,1)} %collective-permute-done.14.refs_1_, bf16[448,512]{1,0:T(8,128)(2,1)} %copy-done.3, ...), custom_call_target="tpu_custom_call", output_to_operand_aliasing={{}: (8, {})} | custom-call | tf_op jit(solution)/shard_map/pallas_call | solution.py:323
  94.3 5.6 %shard_map.93 = f32[16,8,256]{2,1,0:T(8,128)} custom-call(s32[4]{0:T(128)S(1)} %pad_add_fusion.at, bf16[448,512]{1,0:T(8,128)(2,1)} %collective-permute-done.2.refs_0_, bf16[448,512]{1,0:T(8,128)(2,1)} %collective-permute-done.6.refs_1_, bf16[448,512]{1,0:T(8,128)(2,1)} %collective-permute-done.9.refs_2_, bf16[448,512]{1,0:T(8,128)(2,1)} %collective-permute-done.13.refs_3_, ...), custom_call_target="tpu_custom_call" | custom-call | tf_op jit(solution)/shard_map/pallas_call | solution.py:336
  99.9 3.5 %all-to-all-start.1 = ((f32[16,8,256]{2,1,0:T(8,128)}), f32[16,8,256]{2,1,0:T(8,128)S(1)}, u32[]{:S(2)}, u32[]{:S(2)}) async-start(f32[16,8,256]{2,1,0:T(8,128)} %shard_map.93), calls=%async_computation.1 | async-start | bytes 262144 | tf_op jit(solution)/shard_map/all_to_all | solution.py:463
  103.4 0.1 slice_subtract_fusion
  103.5 0.1 broadcast_in_dim.85
  103.6 0.1 broadcast_in_dim.89
  103.7 0.1 broadcast_in_dim.91
  103.8 0.2 fusion.5
  104.0 6.1 %all-to-all-done.1.parts = f32[16,8,256]{2,1,0:T(8,128)S(1)} async-done(((f32[16,8,256]{2,1,0:T(8,128)}), f32[16,8,256]{2,1,0:T(8,128)S(1)}, u32[]{:S(2)}, u32[]{:S(2)}) %all-to-all-start.1) | async-done | bytes 131104 | tf_op jit(solution)/shard_map/all_to_all | solution.py:463
  110.0 0.7 shard_map.94
  110.7 7.4 %all-to-all-start.2 = ((f32[16,8,256]{2,1,0:T(8,128)}), f32[16,8,256]{2,1,0:T(8,128)S(1)}, u32[]{:S(2)}, u32[]{:S(2)}) async-start(f32[16,8,256]{2,1,0:T(8,128)} %shard_map.94), calls=%async_computation.2 | async-start | bytes 262144 | tf_op jit(solution)/shard_map/all_to_all | solution.py:471
  118.1 0.1 fusion.9.source
  118.2 9.1 %all-to-all-done.2.parts = f32[16,8,256]{2,1,0:T(8,128)S(1)} async-done(((f32[16,8,256]{2,1,0:T(8,128)}), f32[16,8,256]{2,1,0:T(8,128)S(1)}, u32[]{:S(2)}, u32[]{:S(2)}) %all-to-all-start.2) | async-done | bytes 131104 | tf_op jit(solution)/shard_map/all_to_all | solution.py:471
  127.3 1.4 %shard_map.95 = (f32[8,14]{1,0:T(8,128)}, f32[1,8]{1,0:T(1,128)}, f32[1,8]{1,0:T(1,128)}) custom-call(f32[16,8,256]{2,1,0:T(8,128)S(1)} %all-to-all-done.2.parts, s32[8,14]{1,0:T(8,128)S(1)} %fusion.9.source, s32[1,8]{1,0:T(1,128)S(1)} %bitcast.22, s32[1,8]{1,0:T(1,128)S(1)} %bitcast.21), custom_call_target="tpu_custom_call" | custom-call | tf_op jit(solution)/shard_map/pallas_call | solution.py:472
  (40 shorter events, 0.4 us)
Async XLA Ops:
  0.6 78.9 %collective-permute-start.18 = (bf16[4096,501]{0,1:T(8,128)(2,1)}, bf16[4096,501]{0,1:T(8,128)(2,1)}, u32[]{:S(2)}, u32[]{:S(2)}) collective-permute-start(bf16[4096,501]{0,1:T(8,128)(2,1)} %param.7), channel_id=1, source_target_pairs={{0,1},{1,0},{2,3},{3,2},{4,5},{5,4},{6,7},{7,6},{8,9},{9,8},{10,11... | collective-permute-start | bytes 12312584 | tf_op jit(solution)/shard_map/ppermute | solution.py:40
  29.3 11.6 %collective-permute-start = (bf16[232,512]{1,0:T(8,128)(2,1)S(1)}, bf16[232,512]{1,0:T(8,128)(2,1)S(1)}, u32[]{:S(2)}, u32[]{:S(2)}) collective-permute-start(bf16[232,512]{1,0:T(8,128)(2,1)S(1)} %get-tuple-element.10.one), channel_id=1, source_target_pairs={{0,64},{64,128},{128,192},{192,0},{1,65},{65,129},{129,193},{193,1... | collective-permute-start | bytes 712712 | tf_op jit(solution)/shard_map/ppermute | solution.py:40
  30.6 13.2 %collective-permute-start.3 = (bf16[232,512]{1,0:T(8,128)(2,1)S(1)}, bf16[232,512]{1,0:T(8,128)(2,1)S(1)}, u32[]{:S(2)}, u32[]{:S(2)}) collective-permute-start(bf16[232,512]{1,0:T(8,128)(2,1)S(1)} %get-tuple-element.10.one), channel_id=1, source_target_pairs={{0,192},{64,0},{128,64},{192,128},{1,193},{65,1},{129,65},{193,129... | collective-permute-start | bytes 712712 | tf_op jit(solution)/shard_map/ppermute | solution.py:40
  32.1 8.5 %collective-permute-start.7 = (bf16[224,512]{1,0:T(8,128)(2,1)S(1)}, bf16[224,512]{1,0:T(8,128)(2,1)S(1)}, u32[]{:S(2)}, u32[]{:S(2)}) collective-permute-start(bf16[224,512]{1,0:T(8,128)(2,1)S(1)} %get-tuple-element.11.one), channel_id=1, source_target_pairs={{0,2},{2,4},{4,6},{6,0},{1,3},{3,5},{5,7},{7,1},{8,10},{10,12},{12... | collective-permute-start | bytes 688136 | tf_op jit(solution)/shard_map/ppermute | solution.py:40
  33.4 7.7 %collective-permute-start.10 = (bf16[224,512]{1,0:T(8,128)(2,1)S(1)}, bf16[224,512]{1,0:T(8,128)(2,1)S(1)}, u32[]{:S(2)}, u32[]{:S(2)}) collective-permute-start(bf16[224,512]{1,0:T(8,128)(2,1)S(1)} %get-tuple-element.11.one), channel_id=1, source_target_pairs={{0,6},{2,0},{4,2},{6,4},{1,7},{3,1},{5,3},{7,5},{8,14},{10,8},{12,... | collective-permute-start | bytes 688136 | tf_op jit(solution)/shard_map/ppermute | solution.py:40
  40.5 8.0 %collective-permute-start.11 = (bf16[224,512]{1,0:T(8,128)(2,1)S(1)}, bf16[224,512]{1,0:T(8,128)(2,1)S(1)}, u32[]{:S(2)}, u32[]{:S(2)}) collective-permute-start(bf16[224,512]{1,0:T(8,128)(2,1)S(1)} %collective-permute-done.7.two), channel_id=1, source_target_pairs={{0,2},{2,4},{4,6},{6,0},{1,3},{3,5},{5,7},{7,1},{8,10},{10,12},{12... | collective-permute-start | bytes 688136 | tf_op jit(solution)/shard_map/ppermute | solution.py:40
  40.9 17.9 %copy-start = (bf16[232,512]{1,0:T(8,128)(2,1)}, bf16[232,512]{1,0:T(8,128)(2,1)S(1)}, u32[]{:S(2)}) copy-start(bf16[232,512]{1,0:T(8,128)(2,1)S(1)} %collective-permute-done.two) | copy-start | bytes 712708
  40.9 21.1 %collective-permute-start.8 = (bf16[448,512]{1,0:T(8,128)(2,1)S(1)}, bf16[448,512]{1,0:T(8,128)(2,1)S(1)}, u32[]{:S(2)}, u32[]{:S(2)}) collective-permute-start(bf16[448,512]{1,0:T(8,128)(2,1)S(1)} %shard_map.89.refs_2_), channel_id=1, source_target_pairs={{0,64},{64,128},{128,192},{192,0},{1,65},{65,129},{129,193},{193,1... | collective-permute-start | bytes 1376264 | tf_op jit(solution)/shard_map/ppermute | solution.py:40
  41.0 21.2 %collective-permute-start.17 = (bf16[448,512]{1,0:T(8,128)(2,1)S(1)}, bf16[448,512]{1,0:T(8,128)(2,1)}, u32[]{:S(2)}, u32[]{:S(2)}) collective-permute-start(bf16[448,512]{1,0:T(8,128)(2,1)S(1)} %shard_map.89.refs_2_), channel_id=1, source_target_pairs={{0,192},{64,0},{128,64},{192,128},{1,193},{65,1},{129,65},{193,129... | collective-permute-start | bytes 1376264 | tf_op jit(solution)/shard_map/ppermute | solution.py:40
  43.8 0.7 copy-start.1
  44.5 19.1 %collective-permute-start.1 = (bf16[448,512]{1,0:T(8,128)(2,1)S(1)}, bf16[448,512]{1,0:T(8,128)(2,1)S(1)}, u32[]{:S(2)}, u32[]{:S(2)}) collective-permute-start(bf16[448,512]{1,0:T(8,128)(2,1)S(1)} %shard_map.87.refs_0_), channel_id=1, source_target_pairs={{0,2},{2,4},{4,6},{6,0},{1,3},{3,5},{5,7},{7,1},{8,10},{10,12},{12... | collective-permute-start | bytes 1376264 | tf_op jit(solution)/shard_map/ppermute | solution.py:40
  48.5 10.3 %collective-permute-start.4 = (bf16[232,512]{1,0:T(8,128)(2,1)S(1)}, bf16[232,512]{1,0:T(8,128)(2,1)S(1)}, u32[]{:S(2)}, u32[]{:S(2)}) collective-permute-start(bf16[232,512]{1,0:T(8,128)(2,1)S(1)} %collective-permute-done.two), channel_id=1, source_target_pairs={{0,64},{64,128},{128,192},{192,0},{1,65},{65,129},{129,193},{193,1... | collective-permute-start | bytes 712712 | tf_op jit(solution)/shard_map/ppermute | solution.py:40
  58.8 10.8 %collective-permute-start.15 = (bf16[448,512]{1,0:T(8,128)(2,1)S(1)}, bf16[448,512]{1,0:T(8,128)(2,1)S(1)}, u32[]{:S(2)}, u32[]{:S(2)}) collective-permute-start(bf16[448,512]{1,0:T(8,128)(2,1)S(1)} %shard_map.87.refs_0_), channel_id=1, source_target_pairs={{0,6},{2,0},{4,2},{6,4},{1,7},{3,1},{5,3},{7,5},{8,14},{10,8},{12,... | collective-permute-start | bytes 1376264 | tf_op jit(solution)/shard_map/ppermute | solution.py:40
  61.1 0.9 copy-start.2
  62.0 10.5 %collective-permute-start.12 = (bf16[448,512]{1,0:T(8,128)(2,1)S(1)}, bf16[448,512]{1,0:T(8,128)(2,1)}, u32[]{:S(2)}, u32[]{:S(2)}) collective-permute-start(bf16[448,512]{1,0:T(8,128)(2,1)S(1)} %shard_map.90.refs_3_), channel_id=1, source_target_pairs={{0,192},{64,0},{128,64},{192,128},{1,193},{65,1},{129,65},{193,129... | collective-permute-start | bytes 1376264 | tf_op jit(solution)/shard_map/ppermute | solution.py:40
  62.2 11.3 %collective-permute-start.16 = (bf16[448,512]{1,0:T(8,128)(2,1)S(1)}, bf16[448,512]{1,0:T(8,128)(2,1)S(1)}, u32[]{:S(2)}, u32[]{:S(2)}) collective-permute-start(bf16[448,512]{1,0:T(8,128)(2,1)S(1)} %shard_map.90.refs_3_), channel_id=1, source_target_pairs={{0,64},{64,128},{128,192},{192,0},{1,65},{65,129},{129,193},{193,1... | collective-permute-start | bytes 1376264 | tf_op jit(solution)/shard_map/ppermute | solution.py:40
  63.6 15.9 %collective-permute-start.5 = (bf16[448,512]{1,0:T(8,128)(2,1)S(1)}, bf16[448,512]{1,0:T(8,128)(2,1)S(1)}, u32[]{:S(2)}, u32[]{:S(2)}) collective-permute-start(bf16[448,512]{1,0:T(8,128)(2,1)S(1)} %shard_map.88.refs_1_), channel_id=1, source_target_pairs={{0,6},{2,0},{4,2},{6,4},{1,7},{3,1},{5,3},{7,5},{8,14},{10,8},{12,... | collective-permute-start | bytes 1376264 | tf_op jit(solution)/shard_map/ppermute | solution.py:40
  69.6 13.1 %copy-start.3 = (bf16[448,512]{1,0:T(8,128)(2,1)}, bf16[448,512]{1,0:T(8,128)(2,1)S(1)}, u32[]{:S(2)}) copy-start(bf16[448,512]{1,0:T(8,128)(2,1)S(1)} %collective-permute-done.15.refs_2_) | copy-start | bytes 1376260
  69.6 18.7 %collective-permute-start.14 = (bf16[448,512]{1,0:T(8,128)(2,1)S(1)}, bf16[448,512]{1,0:T(8,128)(2,1)}, u32[]{:S(2)}, u32[]{:S(2)}) collective-permute-start(bf16[448,512]{1,0:T(8,128)(2,1)S(1)} %shard_map.88.refs_1_), channel_id=1, source_target_pairs={{0,2},{2,4},{4,6},{6,0},{1,3},{3,5},{5,7},{7,1},{8,10},{10,12},{12... | collective-permute-start | bytes 1376264 | tf_op jit(solution)/shard_map/ppermute | solution.py:40
  72.5 21.8 %collective-permute-start.9 = (bf16[448,512]{1,0:T(8,128)(2,1)S(1)}, bf16[448,512]{1,0:T(8,128)(2,1)}, u32[]{:S(2)}, u32[]{:S(2)}) collective-permute-start(bf16[448,512]{1,0:T(8,128)(2,1)S(1)} %collective-permute-done.8.refs_4_), channel_id=1, source_target_pairs={{0,64},{64,128},{128,192},{192,0},{1,65},{65,129},{129,193},{193,1... | collective-permute-start | bytes 1376264 | tf_op jit(solution)/shard_map/ppermute | solution.py:40
  73.5 9.3 %copy-start.4 = (bf16[448,512]{1,0:T(8,128)(2,1)}, bf16[448,512]{1,0:T(8,128)(2,1)S(1)}, u32[]{:S(2)}) copy-start(bf16[448,512]{1,0:T(8,128)(2,1)S(1)} %collective-permute-done.16.refs_5_) | copy-start | bytes 1376260
  73.5 20.8 %collective-permute-start.2 = (bf16[448,512]{1,0:T(8,128)(2,1)S(1)}, bf16[448,512]{1,0:T(8,128)(2,1)}, u32[]{:S(2)}, u32[]{:S(2)}) collective-permute-start(bf16[448,512]{1,0:T(8,128)(2,1)S(1)} %collective-permute-done.1.refs_0_), channel_id=1, source_target_pairs={{0,2},{2,4},{4,6},{6,0},{1,3},{3,5},{5,7},{7,1},{8,10},{10,12},{12... | collective-permute-start | bytes 1376264 | tf_op jit(solution)/shard_map/ppermute | solution.py:40
  79.5 14.8 %collective-permute-start.13 = (bf16[448,512]{1,0:T(8,128)(2,1)}, bf16[448,512]{1,0:T(8,128)(2,1)}, u32[]{:S(2)}, u32[]{:S(2)}) collective-permute-start(bf16[448,512]{1,0:T(8,128)(2,1)} %collective-permute-done.12.refs_7_), channel_id=1, source_target_pairs={{0,192},{64,0},{128,64},{192,128},{1,193},{65,1},{129,65},{193,129... | collective-permute-start | bytes 1376264 | tf_op jit(solution)/shard_map/ppermute | solution.py:40
  79.5 14.8 %collective-permute-start.6 = (bf16[448,512]{1,0:T(8,128)(2,1)S(1)}, bf16[448,512]{1,0:T(8,128)(2,1)}, u32[]{:S(2)}, u32[]{:S(2)}) collective-permute-start(bf16[448,512]{1,0:T(8,128)(2,1)S(1)} %collective-permute-done.5.refs_3_), channel_id=1, source_target_pairs={{0,6},{2,0},{4,2},{6,4},{1,7},{3,1},{5,3},{7,5},{8,14},{10,8},{12,... | collective-permute-start | bytes 1376264 | tf_op jit(solution)/shard_map/ppermute | solution.py:40
  94.3 9.5 %copy-start.5 = (s32[256]{0:T(256)S(1)}, s32[256]{0:T(256)}, u32[]{:S(2)}) copy-start(s32[256]{0:T(256)} %param.11) | copy-start | bytes 3076
  99.9 10.1 %all-to-all-start.1 = ((f32[16,8,256]{2,1,0:T(8,128)}), f32[16,8,256]{2,1,0:T(8,128)S(1)}, u32[]{:S(2)}, u32[]{:S(2)}) async-start(f32[16,8,256]{2,1,0:T(8,128)} %shard_map.93), calls=%async_computation.1 | async-start | bytes 262144 | tf_op jit(solution)/shard_map/all_to_all | solution.py:463
  110.7 16.5 %all-to-all-start.2 = ((f32[16,8,256]{2,1,0:T(8,128)}), f32[16,8,256]{2,1,0:T(8,128)S(1)}, u32[]{:S(2)}, u32[]{:S(2)}) async-start(f32[16,8,256]{2,1,0:T(8,128)} %shard_map.94), calls=%async_computation.2 | async-start | bytes 262144 | tf_op jit(solution)/shard_map/all_to_all | solution.py:471

commit v5 on v4

--- a/solution.py
+++ b/solution.py
@@ -280,20 +280,35 @@
 
 def statistics(at, ids, acc, out, held):
     x = at[1]
+    whole = SHARD // 8 * 8
     held[...] = jnp.zeros_like(held)
-    column = lax.broadcasted_iota(jnp.int32, (SHARD, ROWS), 0)
+    row = lax.broadcasted_iota(jnp.int32, (8, ROWS), 0)
+    rest_row = lax.broadcasted_iota(jnp.int32, (SHARD - whole, ROWS), 0)
     for i in range(NX):
-        own, other = acc[i, 0], acc[i, 1]
-        top = jnp.maximum(jnp.max(own, 0, keepdims=True), jnp.max(other, 0, keepdims=True))
-        total = jnp.sum(jnp.exp(own - top), 0, keepdims=True) + jnp.sum(
-            jnp.exp(other - top), 0, keepdims=True
-        )
-        wanted = ids[i : i + 1, :ROWS]
-        hit = jnp.sum(jnp.where(column == wanted - at[2], own, 0.0), 0, keepdims=True)
-        hit += jnp.sum(jnp.where(column == wanted - at[3], other, 0.0), 0, keepdims=True)
+        top = acc[i, 0, :8]
+        for w in range(2):
+            for r in range(0, whole, 8):
+                top = jnp.maximum(top, acc[i, w, r : r + 8])
+        top = jnp.max(top, 0, keepdims=True)
+        for w in range(2):
+            top = jnp.maximum(top, jnp.max(acc[i, w, whole:], 0, keepdims=True))
+        total, hit = jnp.zeros((8, ROWS), F32), jnp.zeros((8, ROWS), F32)
+        rest_total, rest_hit = jnp.zeros((1, ROWS), F32), jnp.zeros((1, ROWS), F32)
+        for w in range(2):
+            wanted = ids[i : i + 1, :ROWS] - at[2 + w]
+            column = wanted - row
+            for r in range(0, whole, 8):
+                value = acc[i, w, r : r + 8]
+                total = total + jnp.exp(value - top)
+                hit = jnp.where(column == r, value, hit)
+            value = acc[i, w, whole:]
+            rest_total += jnp.sum(jnp.exp(value - top), 0, keepdims=True)
+            here = wanted - rest_row == whole
+            rest_hit += jnp.sum(jnp.where(here, value, 0.0), 0, keepdims=True)
         x_at = (x + OFFSETS[i] + NX) % NX
+        total = jnp.sum(total, 0, keepdims=True) + rest_total
         held[pl.ds(x_at, 1), :ROWS] = top + jnp.log(total)
-        held[pl.ds(4 + x_at, 1), :ROWS] = hit
+        held[pl.ds(4 + x_at, 1), :ROWS] = jnp.sum(hit, 0, keepdims=True) + rest_hit
     for k in range(out.shape[0]):
         out[k] = held[...]
 

time: 129 us -> 129 us (level)
  no operation moved by 1% of the time
where the time goes in v5:
time: 129 us; the launch traced here: 128 us
  waiting for transfers between devices  46.2 us (36%)
  starting transfers between devices  33.1 us (26%)
  blocking collectives  23.9 us (19%)
  Pallas kernels  20.1 us (16%)
  local copies, waits for them, and re-layouts  3.41 us (3%)
    ppermute x19, waiting for transfers between devices, shift(): lax.ppermute(value, axis, [(i, (i + by) % size) for i in range(size)])  31.1 us
    all_to_all x1, blocking collectives, local(): got = lax.all_to_all(sent, ('z', 'c'), 0, 0, tiled=True)  23.9 us
    ppermute x19, starting transfers between devices, shift(): lax.ppermute(value, axis, [(i, (i + by) % size) for i in range(size)])  22.2 us
    all_to_all x1, waiting for transfers between devices, local(): stats = lax.all_to_all(stats, ('z', 'c'), 0, 0, tiled=True)  9.08 us
    all_to_all x1, starting transfers between devices, local(): stats = lax.all_to_all(stats, ('z', 'c'), 0, 0, tiled=True)  7.34 us
    all_to_all x1, waiting for transfers between devices, local(): stats = lax.all_to_all(partial, ('x', 'y'), 0, 0, tiled=True)  6.06 us
    pallas_call x1, Pallas kernels, head(): pl.pallas_call(near_kernel, out_shape=acc, in_specs=specs + [VMEM] * 2, o...  5.92 us
    pallas_call x1, Pallas kernels, head(): pl.pallas_call(far_kernel, out_shape=jax.ShapeDtypeStruct((NX * NY, 8, 25...  5.26 us
  transfers between devices with their start and end apart: 21, of which 9 were waited for; matrix products, arithmetic and copies ran while one was open for 2% of the time, Pallas kernels for 10%

profile of v5, /device:TPU:1, one launch (start us, length us, event | category | flops | bytes accessed | tf_op | source)
XLA Modules:
  0.0 128.4 jit_solution(16610635594191742133)
XLA Ops:
  0.6 3.3 %collective-permute-start.18 = (bf16[4096,501]{0,1:T(8,128)(2,1)}, bf16[4096,501]{0,1:T(8,128)(2,1)}, u32[]{:S(2)}, u32[]{:S(2)}) collective-permute-start(bf16[4096,501]{0,1:T(8,128)(2,1)} %param.7), channel_id=1, source_target_pairs={{0,1},{1,0},{2,3},{3,2},{4,5},{5,4},{6,7},{7,6},{8,9},{9,8},{10,11... | collective-permute-start | bytes 12312584 | tf_op jit(solution)/shard_map/ppermute | solution.py:40
  3.9 1.4 %shard_map.85 = bf16[16,32,512]{2,1,0:T(8,128)(2,1)S(1)} custom-call(bf16[14,8,512]{2,1,0:T(8,128)(2,1)} %bitcast.27, s32[8,14]{1,0:T(8,128)} %targets_hbm.1, s32[1,8]{1,0:T(1,128)} %lengths_hbm.1, s32[1,8]{1,0:T(1,128)} %rewards_hbm.1), custom_call_target="tpu_custom_call" | custom-call | tf_op jit(solution)/shard_map/pallas_call | solution.py:412
  5.4 23.9 %all_to_all.15.got = bf16[16,32,512]{2,1,0:T(8,128)(2,1)S(1)} all-to-all(bf16[16,32,512]{2,1,0:T(8,128)(2,1)S(1)} %shard_map.85), channel_id=1, replica_groups=mesh['x'=4,'z'=8,'y'=4,'c'=2] {'z','c'}, dimensions={0} | all-to-all | bytes 1048576 | tf_op jit(solution)/shard_map/all_to_all | solution.py:426
  29.2 0.1 shard_map.86
  29.3 1.3 %collective-permute-start = (bf16[232,512]{1,0:T(8,128)(2,1)S(1)}, bf16[232,512]{1,0:T(8,128)(2,1)S(1)}, u32[]{:S(2)}, u32[]{:S(2)}) collective-permute-start(bf16[232,512]{1,0:T(8,128)(2,1)S(1)} %get-tuple-element.10.one), channel_id=1, source_target_pairs={{0,64},{64,128},{128,192},{192,0},{1,65},{65,129},{129,193},{193,1... | collective-permute-start | bytes 712712 | tf_op jit(solution)/shard_map/ppermute | solution.py:40
  30.6 1.5 %collective-permute-start.3 = (bf16[232,512]{1,0:T(8,128)(2,1)S(1)}, bf16[232,512]{1,0:T(8,128)(2,1)S(1)}, u32[]{:S(2)}, u32[]{:S(2)}) collective-permute-start(bf16[232,512]{1,0:T(8,128)(2,1)S(1)} %get-tuple-element.10.one), channel_id=1, source_target_pairs={{0,192},{64,0},{128,64},{192,128},{1,193},{65,1},{129,65},{193,129... | collective-permute-start | bytes 712712 | tf_op jit(solution)/shard_map/ppermute | solution.py:40
  32.1 1.3 %collective-permute-start.7 = (bf16[224,512]{1,0:T(8,128)(2,1)S(1)}, bf16[224,512]{1,0:T(8,128)(2,1)S(1)}, u32[]{:S(2)}, u32[]{:S(2)}) collective-permute-start(bf16[224,512]{1,0:T(8,128)(2,1)S(1)} %get-tuple-element.11.one), channel_id=1, source_target_pairs={{0,2},{2,4},{4,6},{6,0},{1,3},{3,5},{5,7},{7,1},{8,10},{10,12},{12... | collective-permute-start | bytes 688136 | tf_op jit(solution)/shard_map/ppermute | solution.py:40
  33.4 1.4 %collective-permute-start.10 = (bf16[224,512]{1,0:T(8,128)(2,1)S(1)}, bf16[224,512]{1,0:T(8,128)(2,1)S(1)}, u32[]{:S(2)}, u32[]{:S(2)}) collective-permute-start(bf16[224,512]{1,0:T(8,128)(2,1)S(1)} %get-tuple-element.11.one), channel_id=1, source_target_pairs={{0,6},{2,0},{4,2},{6,4},{1,7},{3,1},{5,3},{7,5},{8,14},{10,8},{12,... | collective-permute-start | bytes 688136 | tf_op jit(solution)/shard_map/ppermute | solution.py:40
  34.8 5.7 %collective-permute-done.7.two = bf16[224,512]{1,0:T(8,128)(2,1)S(1)} collective-permute-done((bf16[224,512]{1,0:T(8,128)(2,1)S(1)}, bf16[224,512]{1,0:T(8,128)(2,1)S(1)}, u32[]{:S(2)}, u32[]{:S(2)}) %collective-permute-start.7) | collective-permute-done | bytes 229408 | tf_op jit(solution)/shard_map/ppermute | solution.py:40
  40.5 0.3 collective-permute-start.11
  40.9 0.1 collective-permute-start.8
  41.0 2.7 %collective-permute-start.17 = (bf16[448,512]{1,0:T(8,128)(2,1)S(1)}, bf16[448,512]{1,0:T(8,128)(2,1)}, u32[]{:S(2)}, u32[]{:S(2)}) collective-permute-start(bf16[448,512]{1,0:T(8,128)(2,1)S(1)} %shard_map.89.refs_2_), channel_id=1, source_target_pairs={{0,192},{64,0},{128,64},{192,128},{1,193},{65,1},{129,65},{193,129... | collective-permute-start | bytes 1376264 | tf_op jit(solution)/shard_map/ppermute | solution.py:40
  43.8 0.7 copy-done.1
  44.5 1.3 %collective-permute-start.1 = (bf16[448,512]{1,0:T(8,128)(2,1)S(1)}, bf16[448,512]{1,0:T(8,128)(2,1)S(1)}, u32[]{:S(2)}, u32[]{:S(2)}) collective-permute-start(bf16[448,512]{1,0:T(8,128)(2,1)S(1)} %shard_map.87.refs_0_), channel_id=1, source_target_pairs={{0,2},{2,4},{4,6},{6,0},{1,3},{3,5},{5,7},{7,1},{8,10},{10,12},{12... | collective-permute-start | bytes 1376264 | tf_op jit(solution)/shard_map/ppermute | solution.py:40
  45.8 2.7 %collective-permute-done.11.two = bf16[224,512]{1,0:T(8,128)(2,1)S(1)} collective-permute-done((bf16[224,512]{1,0:T(8,128)(2,1)S(1)}, bf16[224,512]{1,0:T(8,128)(2,1)S(1)}, u32[]{:S(2)}, u32[]{:S(2)}) %collective-permute-start.11) | collective-permute-done | bytes 229408 | tf_op jit(solution)/shard_map/ppermute | solution.py:40
  48.5 0.1 pad_add_fusion.at
  48.7 10.1 %collective-permute-done.4.two = bf16[232,512]{1,0:T(8,128)(2,1)S(1)} collective-permute-done((bf16[232,512]{1,0:T(8,128)(2,1)S(1)}, bf16[232,512]{1,0:T(8,128)(2,1)S(1)}, u32[]{:S(2)}, u32[]{:S(2)}) %collective-permute-start.4) | collective-permute-done | bytes 237600 | tf_op jit(solution)/shard_map/ppermute | solution.py:40
  58.8 2.2 %collective-permute-start.15 = (bf16[448,512]{1,0:T(8,128)(2,1)S(1)}, bf16[448,512]{1,0:T(8,128)(2,1)S(1)}, u32[]{:S(2)}, u32[]{:S(2)}) collective-permute-start(bf16[448,512]{1,0:T(8,128)(2,1)S(1)} %shard_map.87.refs_0_), channel_id=1, source_target_pairs={{0,6},{2,0},{4,2},{6,4},{1,7},{3,1},{5,3},{7,5},{8,14},{10,8},{12,... | collective-permute-start | bytes 1376264 | tf_op jit(solution)/shard_map/ppermute | solution.py:40
  61.1 0.9 copy-done.2
  62.0 0.1 collective-permute-start.12
  62.2 1.4 %collective-permute-start.16 = (bf16[448,512]{1,0:T(8,128)(2,1)S(1)}, bf16[448,512]{1,0:T(8,128)(2,1)S(1)}, u32[]{:S(2)}, u32[]{:S(2)}) collective-permute-start(bf16[448,512]{1,0:T(8,128)(2,1)S(1)} %shard_map.90.refs_3_), channel_id=1, source_target_pairs={{0,64},{64,128},{128,192},{192,0},{1,65},{65,129},{129,193},{193,1... | collective-permute-start | bytes 1376264 | tf_op jit(solution)/shard_map/ppermute | solution.py:40
  63.6 0.7 collective-permute-start.5
  64.3 0.7 slice_bitcast_fusion.2
  65.0 0.7 slice_bitcast_fusion.1
  65.7 4.0 %collective-permute-done.15.refs_2_ = bf16[448,512]{1,0:T(8,128)(2,1)S(1)} collective-permute-done((bf16[448,512]{1,0:T(8,128)(2,1)S(1)}, bf16[448,512]{1,0:T(8,128)(2,1)S(1)}, u32[]{:S(2)}, u32[]{:S(2)}) %collective-permute-start.15) | collective-permute-done | bytes 458784 | tf_op jit(solution)/shard_map/ppermute | solution.py:40
  69.6 1.3 %collective-permute-start.14 = (bf16[448,512]{1,0:T(8,128)(2,1)S(1)}, bf16[448,512]{1,0:T(8,128)(2,1)}, u32[]{:S(2)}, u32[]{:S(2)}) collective-permute-start(bf16[448,512]{1,0:T(8,128)(2,1)S(1)} %shard_map.88.refs_1_), channel_id=1, source_target_pairs={{0,2},{2,4},{4,6},{6,0},{1,3},{3,5},{5,7},{7,1},{8,10},{10,12},{12... | collective-permute-start | bytes 1376264 | tf_op jit(solution)/shard_map/ppermute | solution.py:40
  70.9 1.6 %collective-permute-done.12.refs_7_ = bf16[448,512]{1,0:T(8,128)(2,1)} collective-permute-done((bf16[448,512]{1,0:T(8,128)(2,1)S(1)}, bf16[448,512]{1,0:T(8,128)(2,1)}, u32[]{:S(2)}, u32[]{:S(2)}) %collective-permute-start.12) | collective-permute-done | bytes 458784 | tf_op jit(solution)/shard_map/ppermute | solution.py:40
  72.5 1.0 collective-permute-done.16.refs_5_
  73.5 6.0 %collective-permute-done.5.refs_3_ = bf16[448,512]{1,0:T(8,128)(2,1)S(1)} collective-permute-done((bf16[448,512]{1,0:T(8,128)(2,1)S(1)}, bf16[448,512]{1,0:T(8,128)(2,1)S(1)}, u32[]{:S(2)}, u32[]{:S(2)}) %collective-permute-start.5) | collective-permute-done | bytes 458784 | tf_op jit(solution)/shard_map/ppermute | solution.py:40
  79.5 3.2 %collective-permute-start.6 = (bf16[448,512]{1,0:T(8,128)(2,1)S(1)}, bf16[448,512]{1,0:T(8,128)(2,1)}, u32[]{:S(2)}, u32[]{:S(2)}) collective-permute-start(bf16[448,512]{1,0:T(8,128)(2,1)S(1)} %collective-permute-done.5.refs_3_), channel_id=1, source_target_pairs={{0,6},{2,0},{4,2},{6,4},{1,7},{3,1},{5,3},{7,5},{8,14},{10,8},{12,... | collective-permute-start | bytes 1376264 | tf_op jit(solution)/shard_map/ppermute | solution.py:40
  82.8 0.1 reshape.116
  82.9 0.1 select_reduce_fusion
  83.0 0.2 reduce_window_sum.11
  83.2 5.1 %shard_map.91 = (f32[4,2,501,224]{3,2,1,0:T(8,128)S(1)}, bf16[7,2,501,512]{3,2,1,0:T(8,128)(2,1)S(1)}) custom-call(s32[4]{0:T(128)S(1)} %pad_add_fusion.at, bf16[448,512]{1,0:T(8,128)(2,1)S(1)} %shard_map.87.refs_0_, bf16[448,512]{1,0:T(8,128)(2,1)S(1)} %shard_map.88.refs_1_, bf16[448,512]{1,0:T(8,128)(2,1)S(1)} %shard_map.89.refs_2_, ...), custom_call_target="tpu_custom_call" | custom-call | tf_op jit(solution)/shard_map/pallas_call | solution.py:329
  88.3 5.9 %shard_map.92.refs_4_ = f32[4,2,501,224]{3,2,1,0:T(8,128)S(1)} custom-call(bf16[448,512]{1,0:T(8,128)(2,1)S(1)} %collective-permute-done.1.refs_0_, bf16[448,512]{1,0:T(8,128)(2,1)} %collective-permute-done.14.refs_1_, bf16[448,512]{1,0:T(8,128)(2,1)} %copy-done.3, ...), custom_call_target="tpu_custom_call", output_to_operand_aliasing={{}: (8, {})} | custom-call | tf_op jit(solution)/shard_map/pallas_call | solution.py:338
  94.3 5.3 %shard_map.93 = f32[16,8,256]{2,1,0:T(8,128)} custom-call(s32[4]{0:T(128)S(1)} %pad_add_fusion.at, bf16[448,512]{1,0:T(8,128)(2,1)} %collective-permute-done.2.refs_0_, bf16[448,512]{1,0:T(8,128)(2,1)} %collective-permute-done.6.refs_1_, bf16[448,512]{1,0:T(8,128)(2,1)} %collective-permute-done.9.refs_2_, bf16[448,512]{1,0:T(8,128)(2,1)} %collective-permute-done.13.refs_3_, ...), custom_call_target="tpu_custom_call" | custom-call | tf_op jit(solution)/shard_map/pallas_call | solution.py:351
  99.6 3.5 %all-to-all-start.1 = ((f32[16,8,256]{2,1,0:T(8,128)}), f32[16,8,256]{2,1,0:T(8,128)S(1)}, u32[]{:S(2)}, u32[]{:S(2)}) async-start(f32[16,8,256]{2,1,0:T(8,128)} %shard_map.93), calls=%async_computation.1 | async-start | bytes 262144 | tf_op jit(solution)/shard_map/all_to_all | solution.py:478
  103.1 0.1 slice_subtract_fusion
  103.2 0.1 broadcast_in_dim.85
  103.2 0.1 broadcast_in_dim.89
  103.3 0.1 broadcast_in_dim.91
  103.4 0.2 fusion.5
  103.7 6.1 %all-to-all-done.1.parts = f32[16,8,256]{2,1,0:T(8,128)S(1)} async-done(((f32[16,8,256]{2,1,0:T(8,128)}), f32[16,8,256]{2,1,0:T(8,128)S(1)}, u32[]{:S(2)}, u32[]{:S(2)}) %all-to-all-start.1) | async-done | bytes 131104 | tf_op jit(solution)/shard_map/all_to_all | solution.py:478
  109.7 0.7 shard_map.94
  110.4 7.3 %all-to-all-start.2 = ((f32[16,8,256]{2,1,0:T(8,128)}), f32[16,8,256]{2,1,0:T(8,128)S(1)}, u32[]{:S(2)}, u32[]{:S(2)}) async-start(f32[16,8,256]{2,1,0:T(8,128)} %shard_map.94), calls=%async_computation.2 | async-start | bytes 262144 | tf_op jit(solution)/shard_map/all_to_all | solution.py:486
  117.8 0.1 fusion.9.source
  117.9 9.1 %all-to-all-done.2.parts = f32[16,8,256]{2,1,0:T(8,128)S(1)} async-done(((f32[16,8,256]{2,1,0:T(8,128)}), f32[16,8,256]{2,1,0:T(8,128)S(1)}, u32[]{:S(2)}, u32[]{:S(2)}) %all-to-all-start.2) | async-done | bytes 131104 | tf_op jit(solution)/shard_map/all_to_all | solution.py:486
  127.0 1.4 %shard_map.95 = (f32[8,14]{1,0:T(8,128)}, f32[1,8]{1,0:T(1,128)}, f32[1,8]{1,0:T(1,128)}) custom-call(f32[16,8,256]{2,1,0:T(8,128)S(1)} %all-to-all-done.2.parts, s32[8,14]{1,0:T(8,128)S(1)} %fusion.9.source, s32[1,8]{1,0:T(1,128)S(1)} %bitcast.22, s32[1,8]{1,0:T(1,128)S(1)} %bitcast.21), custom_call_target="tpu_custom_call" | custom-call | tf_op jit(solution)/shard_map/pallas_call | solution.py:487
  (40 shorter events, 0.4 us)
Async XLA Ops:
  0.6 78.9 %collective-permute-start.18 = (bf16[4096,501]{0,1:T(8,128)(2,1)}, bf16[4096,501]{0,1:T(8,128)(2,1)}, u32[]{:S(2)}, u32[]{:S(2)}) collective-permute-start(bf16[4096,501]{0,1:T(8,128)(2,1)} %param.7), channel_id=1, source_target_pairs={{0,1},{1,0},{2,3},{3,2},{4,5},{5,4},{6,7},{7,6},{8,9},{9,8},{10,11... | collective-permute-start | bytes 12312584 | tf_op jit(solution)/shard_map/ppermute | solution.py:40
  29.3 11.6 %collective-permute-start = (bf16[232,512]{1,0:T(8,128)(2,1)S(1)}, bf16[232,512]{1,0:T(8,128)(2,1)S(1)}, u32[]{:S(2)}, u32[]{:S(2)}) collective-permute-start(bf16[232,512]{1,0:T(8,128)(2,1)S(1)} %get-tuple-element.10.one), channel_id=1, source_target_pairs={{0,64},{64,128},{128,192},{192,0},{1,65},{65,129},{129,193},{193,1... | collective-permute-start | bytes 712712 | tf_op jit(solution)/shard_map/ppermute | solution.py:40
  30.6 13.2 %collective-permute-start.3 = (bf16[232,512]{1,0:T(8,128)(2,1)S(1)}, bf16[232,512]{1,0:T(8,128)(2,1)S(1)}, u32[]{:S(2)}, u32[]{:S(2)}) collective-permute-start(bf16[232,512]{1,0:T(8,128)(2,1)S(1)} %get-tuple-element.10.one), channel_id=1, source_target_pairs={{0,192},{64,0},{128,64},{192,128},{1,193},{65,1},{129,65},{193,129... | collective-permute-start | bytes 712712 | tf_op jit(solution)/shard_map/ppermute | solution.py:40
  32.1 8.5 %collective-permute-start.7 = (bf16[224,512]{1,0:T(8,128)(2,1)S(1)}, bf16[224,512]{1,0:T(8,128)(2,1)S(1)}, u32[]{:S(2)}, u32[]{:S(2)}) collective-permute-start(bf16[224,512]{1,0:T(8,128)(2,1)S(1)} %get-tuple-element.11.one), channel_id=1, source_target_pairs={{0,2},{2,4},{4,6},{6,0},{1,3},{3,5},{5,7},{7,1},{8,10},{10,12},{12... | collective-permute-start | bytes 688136 | tf_op jit(solution)/shard_map/ppermute | solution.py:40
  33.4 7.7 %collective-permute-start.10 = (bf16[224,512]{1,0:T(8,128)(2,1)S(1)}, bf16[224,512]{1,0:T(8,128)(2,1)S(1)}, u32[]{:S(2)}, u32[]{:S(2)}) collective-permute-start(bf16[224,512]{1,0:T(8,128)(2,1)S(1)} %get-tuple-element.11.one), channel_id=1, source_target_pairs={{0,6},{2,0},{4,2},{6,4},{1,7},{3,1},{5,3},{7,5},{8,14},{10,8},{12,... | collective-permute-start | bytes 688136 | tf_op jit(solution)/shard_map/ppermute | solution.py:40
  40.5 8.0 %collective-permute-start.11 = (bf16[224,512]{1,0:T(8,128)(2,1)S(1)}, bf16[224,512]{1,0:T(8,128)(2,1)S(1)}, u32[]{:S(2)}, u32[]{:S(2)}) collective-permute-start(bf16[224,512]{1,0:T(8,128)(2,1)S(1)} %collective-permute-done.7.two), channel_id=1, source_target_pairs={{0,2},{2,4},{4,6},{6,0},{1,3},{3,5},{5,7},{7,1},{8,10},{10,12},{12... | collective-permute-start | bytes 688136 | tf_op jit(solution)/shard_map/ppermute | solution.py:40
  40.9 17.9 %copy-start = (bf16[232,512]{1,0:T(8,128)(2,1)}, bf16[232,512]{1,0:T(8,128)(2,1)S(1)}, u32[]{:S(2)}) copy-start(bf16[232,512]{1,0:T(8,128)(2,1)S(1)} %collective-permute-done.two) | copy-start | bytes 712708
  40.9 21.1 %collective-permute-start.8 = (bf16[448,512]{1,0:T(8,128)(2,1)S(1)}, bf16[448,512]{1,0:T(8,128)(2,1)S(1)}, u32[]{:S(2)}, u32[]{:S(2)}) collective-permute-start(bf16[448,512]{1,0:T(8,128)(2,1)S(1)} %shard_map.89.refs_2_), channel_id=1, source_target_pairs={{0,64},{64,128},{128,192},{192,0},{1,65},{65,129},{129,193},{193,1... | collective-permute-start | bytes 1376264 | tf_op jit(solution)/shard_map/ppermute | solution.py:40
  41.0 21.2 %collective-permute-start.17 = (bf16[448,512]{1,0:T(8,128)(2,1)S(1)}, bf16[448,512]{1,0:T(8,128)(2,1)}, u32[]{:S(2)}, u32[]{:S(2)}) collective-permute-start(bf16[448,512]{1,0:T(8,128)(2,1)S(1)} %shard_map.89.refs_2_), channel_id=1, source_target_pairs={{0,192},{64,0},{128,64},{192,128},{1,193},{65,1},{129,65},{193,129... | collective-permute-start | bytes 1376264 | tf_op jit(solution)/shard_map/ppermute | solution.py:40
  43.8 0.7 copy-start.1
  44.5 19.1 %collective-permute-start.1 = (bf16[448,512]{1,0:T(8,128)(2,1)S(1)}, bf16[448,512]{1,0:T(8,128)(2,1)S(1)}, u32[]{:S(2)}, u32[]{:S(2)}) collective-permute-start(bf16[448,512]{1,0:T(8,128)(2,1)S(1)} %shard_map.87.refs_0_), channel_id=1, source_target_pairs={{0,2},{2,4},{4,6},{6,0},{1,3},{3,5},{5,7},{7,1},{8,10},{10,12},{12... | collective-permute-start | bytes 1376264 | tf_op jit(solution)/shard_map/ppermute | solution.py:40
  48.5 10.3 %collective-permute-start.4 = (bf16[232,512]{1,0:T(8,128)(2,1)S(1)}, bf16[232,512]{1,0:T(8,128)(2,1)S(1)}, u32[]{:S(2)}, u32[]{:S(2)}) collective-permute-start(bf16[232,512]{1,0:T(8,128)(2,1)S(1)} %collective-permute-done.two), channel_id=1, source_target_pairs={{0,64},{64,128},{128,192},{192,0},{1,65},{65,129},{129,193},{193,1... | collective-permute-start | bytes 712712 | tf_op jit(solution)/shard_map/ppermute | solution.py:40
  58.8 10.8 %collective-permute-start.15 = (bf16[448,512]{1,0:T(8,128)(2,1)S(1)}, bf16[448,512]{1,0:T(8,128)(2,1)S(1)}, u32[]{:S(2)}, u32[]{:S(2)}) collective-permute-start(bf16[448,512]{1,0:T(8,128)(2,1)S(1)} %shard_map.87.refs_0_), channel_id=1, source_target_pairs={{0,6},{2,0},{4,2},{6,4},{1,7},{3,1},{5,3},{7,5},{8,14},{10,8},{12,... | collective-permute-start | bytes 1376264 | tf_op jit(solution)/shard_map/ppermute | solution.py:40
  61.1 0.9 copy-start.2
  62.0 10.5 %collective-permute-start.12 = (bf16[448,512]{1,0:T(8,128)(2,1)S(1)}, bf16[448,512]{1,0:T(8,128)(2,1)}, u32[]{:S(2)}, u32[]{:S(2)}) collective-permute-start(bf16[448,512]{1,0:T(8,128)(2,1)S(1)} %shard_map.90.refs_3_), channel_id=1, source_target_pairs={{0,192},{64,0},{128,64},{192,128},{1,193},{65,1},{129,65},{193,129... | collective-permute-start | bytes 1376264 | tf_op jit(solution)/shard_map/ppermute | solution.py:40
  62.2 11.3 %collective-permute-start.16 = (bf16[448,512]{1,0:T(8,128)(2,1)S(1)}, bf16[448,512]{1,0:T(8,128)(2,1)S(1)}, u32[]{:S(2)}, u32[]{:S(2)}) collective-permute-start(bf16[448,512]{1,0:T(8,128)(2,1)S(1)} %shard_map.90.refs_3_), channel_id=1, source_target_pairs={{0,64},{64,128},{128,192},{192,0},{1,65},{65,129},{129,193},{193,1... | collective-permute-start | bytes 1376264 | tf_op jit(solution)/shard_map/ppermute | solution.py:40
  63.6 15.9 %collective-permute-start.5 = (bf16[448,512]{1,0:T(8,128)(2,1)S(1)}, bf16[448,512]{1,0:T(8,128)(2,1)S(1)}, u32[]{:S(2)}, u32[]{:S(2)}) collective-permute-start(bf16[448,512]{1,0:T(8,128)(2,1)S(1)} %shard_map.88.refs_1_), channel_id=1, source_target_pairs={{0,6},{2,0},{4,2},{6,4},{1,7},{3,1},{5,3},{7,5},{8,14},{10,8},{12,... | collective-permute-start | bytes 1376264 | tf_op jit(solution)/shard_map/ppermute | solution.py:40
  69.6 13.1 %copy-start.3 = (bf16[448,512]{1,0:T(8,128)(2,1)}, bf16[448,512]{1,0:T(8,128)(2,1)S(1)}, u32[]{:S(2)}) copy-start(bf16[448,512]{1,0:T(8,128)(2,1)S(1)} %collective-permute-done.15.refs_2_) | copy-start | bytes 1376260
  69.6 18.7 %collective-permute-start.14 = (bf16[448,512]{1,0:T(8,128)(2,1)S(1)}, bf16[448,512]{1,0:T(8,128)(2,1)}, u32[]{:S(2)}, u32[]{:S(2)}) collective-permute-start(bf16[448,512]{1,0:T(8,128)(2,1)S(1)} %shard_map.88.refs_1_), channel_id=1, source_target_pairs={{0,2},{2,4},{4,6},{6,0},{1,3},{3,5},{5,7},{7,1},{8,10},{10,12},{12... | collective-permute-start | bytes 1376264 | tf_op jit(solution)/shard_map/ppermute | solution.py:40
  72.5 21.8 %collective-permute-start.9 = (bf16[448,512]{1,0:T(8,128)(2,1)S(1)}, bf16[448,512]{1,0:T(8,128)(2,1)}, u32[]{:S(2)}, u32[]{:S(2)}) collective-permute-start(bf16[448,512]{1,0:T(8,128)(2,1)S(1)} %collective-permute-done.8.refs_4_), channel_id=1, source_target_pairs={{0,64},{64,128},{128,192},{192,0},{1,65},{65,129},{129,193},{193,1... | collective-permute-start | bytes 1376264 | tf_op jit(solution)/shard_map/ppermute | solution.py:40
  73.5 9.3 %copy-start.4 = (bf16[448,512]{1,0:T(8,128)(2,1)}, bf16[448,512]{1,0:T(8,128)(2,1)S(1)}, u32[]{:S(2)}) copy-start(bf16[448,512]{1,0:T(8,128)(2,1)S(1)} %collective-permute-done.16.refs_5_) | copy-start | bytes 1376260
  73.5 20.8 %collective-permute-start.2 = (bf16[448,512]{1,0:T(8,128)(2,1)S(1)}, bf16[448,512]{1,0:T(8,128)(2,1)}, u32[]{:S(2)}, u32[]{:S(2)}) collective-permute-start(bf16[448,512]{1,0:T(8,128)(2,1)S(1)} %collective-permute-done.1.refs_0_), channel_id=1, source_target_pairs={{0,2},{2,4},{4,6},{6,0},{1,3},{3,5},{5,7},{7,1},{8,10},{10,12},{12... | collective-permute-start | bytes 1376264 | tf_op jit(solution)/shard_map/ppermute | solution.py:40
  79.5 14.8 %collective-permute-start.13 = (bf16[448,512]{1,0:T(8,128)(2,1)}, bf16[448,512]{1,0:T(8,128)(2,1)}, u32[]{:S(2)}, u32[]{:S(2)}) collective-permute-start(bf16[448,512]{1,0:T(8,128)(2,1)} %collective-permute-done.12.refs_7_), channel_id=1, source_target_pairs={{0,192},{64,0},{128,64},{192,128},{1,193},{65,1},{129,65},{193,129... | collective-permute-start | bytes 1376264 | tf_op jit(solution)/shard_map/ppermute | solution.py:40
  79.5 14.8 %collective-permute-start.6 = (bf16[448,512]{1,0:T(8,128)(2,1)S(1)}, bf16[448,512]{1,0:T(8,128)(2,1)}, u32[]{:S(2)}, u32[]{:S(2)}) collective-permute-start(bf16[448,512]{1,0:T(8,128)(2,1)S(1)} %collective-permute-done.5.refs_3_), channel_id=1, source_target_pairs={{0,6},{2,0},{4,2},{6,4},{1,7},{3,1},{5,3},{7,5},{8,14},{10,8},{12,... | collective-permute-start | bytes 1376264 | tf_op jit(solution)/shard_map/ppermute | solution.py:40
  94.3 9.2 %copy-start.5 = (s32[256]{0:T(256)S(1)}, s32[256]{0:T(256)}, u32[]{:S(2)}) copy-start(s32[256]{0:T(256)} %param.11) | copy-start | bytes 3076
  99.6 10.1 %all-to-all-start.1 = ((f32[16,8,256]{2,1,0:T(8,128)}), f32[16,8,256]{2,1,0:T(8,128)S(1)}, u32[]{:S(2)}, u32[]{:S(2)}) async-start(f32[16,8,256]{2,1,0:T(8,128)} %shard_map.93), calls=%async_computation.1 | async-start | bytes 262144 | tf_op jit(solution)/shard_map/all_to_all | solution.py:478
  110.4 16.5 %all-to-all-start.2 = ((f32[16,8,256]{2,1,0:T(8,128)}), f32[16,8,256]{2,1,0:T(8,128)S(1)}, u32[]{:S(2)}, u32[]{:S(2)}) async-start(f32[16,8,256]{2,1,0:T(8,128)} %shard_map.94), calls=%async_computation.2 | async-start | bytes 262144 | tf_op jit(solution)/shard_map/all_to_all | solution.py:486
